TPU v7x, 32 devices: a whole 2x2x4 slice. The times are simulated.
32 devices in a mesh: leaf: 4 (over x, core), ctx: 8 (over z, y).
Axes of the slice: x: 2, y: 2, z: 4, core: 2. Of those that a mesh axis runs over, the one named last changes fastest.
Arguments:
- queries: bfloat16 [4096, 4096], P(('leaf', 'ctx')), parts along dimension 0, may hold values from -6 to 6
- keys: bfloat16 [4096, 512], P(('leaf', 'ctx')), parts along dimension 0, may hold values from -6 to 6
- values: bfloat16 [4096, 512], P(('leaf', 'ctx')), parts along dimension 0, may hold values from -6 to 6
- grad_out: bfloat16 [4096, 4096], P(('leaf', 'ctx')), parts along dimension 0, may hold values from -6 to 6
- block_path: int32 [32, 4], P('leaf'), parts along dimension 0, may hold values from -1 to 7, as said below
- assistant: int32 [4096], P(('leaf', 'ctx')), parts along dimension 0, may hold values from 0 to 1, as said below
Outputs:
- attention: bfloat16 [4096, 4096], P(('leaf', 'ctx')), parts along dimension 0
- grad_queries: bfloat16 [4096, 4096], P(('leaf', 'ctx')), parts along dimension 0
- grad_keys: bfloat16 [4096, 512], P(('leaf', 'ctx')), parts along dimension 0
- grad_values: bfloat16 [4096, 512], P(('leaf', 'ctx')), parts along dimension 0
There are 4 independent parts, one for each index of `leaf`. A program takes and returns all parts, laid end to end along the dimension named above; each array names one. Nothing has to cross between parts.
Inputs may be any that keep to these rules, and one draw needn't show every extreme that they name: `block_path`: blocks lie in depth-first order of the tree; every node spans one block; block 0 is the root at depth 0. Row b holds at depth e <= depth(b) the block of b's ancestor node at that depth (b itself at e = depth(b)) and -1 below. `assistant`: each block of 128 tokens holds one run of ones.
All inputs are finite; a program needn't handle non-finite values.
Results may differ from a plain program's by a relative error of at most 0.0091.
Values may be sent and summed in bfloat16 or wider, within the bound.
No kernel may reach another device: no remote copies, remote signals or barrier semaphores. Data moves between devices by JAX's collectives and lax.ppermute only.
A program may use at most 128 MiB of HBM per device.

v0:
```python
import functools
import math

import jax
import jax.numpy as jnp
from jax import lax
from jax.experimental import pallas as pl
from jax.experimental.pallas import tpu as pltpu
from jax.sharding import PartitionSpec as P


KEY_HEADS = 4
HEAD_WIDTH = 128
HEADS_PER_KEY = 8
FAR_SLOTS = 3
GROUP = KEY_HEADS
MASKED = -1e30
VMEM_LIMIT = 24 * 1024 * 1024


SMEM_SPEC = pl.BlockSpec(memory_space=pltpu.SMEM)
VMEM_SPEC = pl.BlockSpec(memory_space=pltpu.VMEM)
HBM_SPEC = pl.BlockSpec(memory_space=pltpu.HBM)


def wrap(x):
    return lax.rem(x + 2 * GROUP, GROUP)


def head_columns(head):
    return pl.ds(pl.multiple_of(head * HEAD_WIDTH, HEAD_WIDTH), HEAD_WIDTH)


def cost(flops, moved):
    return pl.CostEstimate(flops=flops, bytes_accessed=moved, transcendentals=0)


def pack_kernel(pos_ref, k_ref, v_ref, *refs):
    outs, sem = refs[:GROUP], refs[-1]
    member = lax.rem(pos_ref[0], GROUP)
    copies = []
    for t in range(GROUP):
        cols = head_columns(wrap(member + t))
        for part, source in enumerate((k_ref, v_ref)):
            copies.append(
                pltpu.make_async_copy(source.at[:, cols], outs[t].at[part], sem.at[2 * t + part])
            )
    for copy in copies:
        copy.start()
    for copy in copies:
        copy.wait()


def select_kernel(count, pos_ref, path_ref, *refs):
    pieces, outs, held = refs[:count], refs[count : count + GROUP], refs[-1]
    position = pos_ref[0]
    member, group = lax.rem(position, GROUP), lax.div(position, GROUP)
    for i in range(count):
        held[i] = pieces[i][...]
    for t in range(GROUP):
        block = group * GROUP + wrap(member + t)
        for e in range(FAR_SLOTS):
            ancestor = path_ref[block, e]
            seen = path_ref[block, e + 1] >= 0
            above = group - lax.div(ancestor, GROUP)
            index = above * GROUP + wrap(member - lax.rem(ancestor, GROUP))
            outs[t][e] = held[jnp.where(seen, index, 0)]


def stage_kernel(mask_ref, q_hbm, go_hbm, q_ref, gm_ref, sem):
    copies = [
        pltpu.make_async_copy(q_hbm, q_ref, sem.at[0]),
        pltpu.make_async_copy(go_hbm, gm_ref, sem.at[1]),
    ]
    for copy in copies:
        copy.start()
    for copy in copies:
        copy.wait()
    mask = mask_ref[...]
    for i in range(gm_ref.shape[1] // HEAD_WIDTH):
        cols = slice(i * HEAD_WIDTH, (i + 1) * HEAD_WIDTH)
        gm_ref[:, cols] = gm_ref[:, cols] * mask


def attend_kernel(turn, rows, *refs):
    (pos_ref, path_ref, q_ref, gm_ref, far_ref, own_ref) = refs[:6]
    attn_ref, gq_ref, far_grad_ref, own_grad_ref = refs[6:]
    scaling = 1.0 / math.sqrt(HEAD_WIDTH)
    position = pos_ref[0]
    head = wrap(lax.rem(position, GROUP) - turn)
    far_rows = FAR_SLOTS * rows
    last = (((1,), (1,)), ((), ()))
    first = (((0,), (0,)), ((), ()))

    def dot(left, right, dims=(((1,), (0,)), ((), ()))):
        return lax.dot_general(left, right, dims, preferred_element_type=jnp.float32)

    def rows_of(ref):
        parts = [
            ref[:, head_columns(head * HEADS_PER_KEY + i)] for i in range(HEADS_PER_KEY)
        ]
        return jnp.concatenate(parts, 0)

    kk = jnp.concatenate([far_ref[e, 0] for e in range(FAR_SLOTS)] + [own_ref[0]], 0)
    vv = jnp.concatenate([far_ref[e, 1] for e in range(FAR_SLOTS)] + [own_ref[1]], 0)
    qm, gm = rows_of(q_ref), rows_of(gm_ref)
    key = lax.broadcasted_iota(jnp.int32, (rows, rows), 0)
    token = lax.broadcasted_iota(jnp.int32, (rows, rows), 1)
    causal = jnp.where(key <= token, 0.0, MASKED)
    scores = dot(kk, qm, last)
    parts = [
        scores[e * rows : (e + 1) * rows] + jnp.where(path_ref[position, e + 1] >= 0, 0.0, MASKED)
        for e in range(FAR_SLOTS)
    ]
    parts.append(scores[far_rows:] + jnp.concatenate([causal] * HEADS_PER_KEY, 1))
    scores = jnp.concatenate(parts, 0)
    top = jnp.max(scores, axis=0, keepdims=True)
    weights = jnp.exp2((scores - top) * (scaling * math.log2(math.e)))
    weights = weights * (1.0 / jnp.sum(weights, axis=0, keepdims=True))
    rounded = weights.astype(jnp.bfloat16)
    grad_prob = dot(vv, gm, last)
    delta = jnp.sum(weights * grad_prob, axis=0, keepdims=True)
    grad_score = (weights * (grad_prob - delta)).astype(jnp.bfloat16)
    attended = dot(vv, rounded, first)
    grad_query = dot(kk, grad_score, first) * scaling
    for i in range(HEADS_PER_KEY):
        s = slice(i * rows, (i + 1) * rows)
        cols = slice(i * HEAD_WIDTH, (i + 1) * HEAD_WIDTH)
        attn_ref[:, cols] = attended[:, s].T.astype(jnp.bfloat16)
        gq_ref[:, cols] = grad_query[:, s].T.astype(jnp.bfloat16)
    grad_key = dot(grad_score, qm) * scaling
    grad_value = dot(rounded, gm)
    for e in range(FAR_SLOTS):
        s = slice(e * rows, (e + 1) * rows)
        far_grad_ref[e, 0] = grad_key[s].astype(jnp.bfloat16)
        far_grad_ref[e, 1] = grad_value[s].astype(jnp.bfloat16)
    own_grad_ref[0] = grad_key[far_rows:]
    own_grad_ref[1] = grad_value[far_rows:]


def attend(turn, pos, path, queries, grad_rows, far, own):
    rows = queries.shape[0]
    width = HEADS_PER_KEY * HEAD_WIDTH
    block = jax.ShapeDtypeStruct((rows, width), jnp.bfloat16)
    span = (FAR_SLOTS + 1) * rows
    return pl.pallas_call(
        functools.partial(attend_kernel, turn, rows),
        in_specs=[SMEM_SPEC] * 2 + [VMEM_SPEC] * 4,
        out_specs=[VMEM_SPEC] * 4,
        out_shape=[
            block,
            block,
            jax.ShapeDtypeStruct(far.shape, jnp.bfloat16),
            jax.ShapeDtypeStruct(own.shape, jnp.float32),
        ],
        cost_estimate=cost(12 * rows * HEADS_PER_KEY * span * HEAD_WIDTH, 8 * rows * width),
        compiler_params=pltpu.CompilerParams(vmem_limit_bytes=VMEM_LIMIT),
    )(pos, path, queries, grad_rows, far, own)


def store_kernel(pos_ref, *refs):
    blocks, outs, sem = refs[: 2 * GROUP], refs[2 * GROUP : -1], refs[-1]
    width = HEADS_PER_KEY * HEAD_WIDTH
    member = lax.rem(pos_ref[0], GROUP)
    copies = []
    for t in range(GROUP):
        head = wrap(member - t)
        cols = pl.ds(pl.multiple_of(head * width, width), width)
        for part in range(2):
            i = 2 * t + part
            copies.append(pltpu.make_async_copy(blocks[i], outs[part].at[:, cols], sem.at[i]))
    for copy in copies:
        copy.start()
    for copy in copies:
        copy.wait()


def reduce_kernel(count, pos_ref, path_ref, *refs):
    terms, outs, acc = refs[:GROUP], refs[GROUP : GROUP + count], refs[-1]
    position = pos_ref[0]
    member, group = lax.rem(position, GROUP), lax.div(position, GROUP)
    acc[...] = jnp.zeros_like(acc)
    for t in range(GROUP):
        block = group * GROUP + wrap(member + t)
        for e in range(FAR_SLOTS):
            ancestor = path_ref[block, e]
            above = group - lax.div(ancestor, GROUP)
            index = above * GROUP + wrap(lax.rem(ancestor, GROUP) - member)

            @pl.when(path_ref[block, e + 1] >= 0)
            def _(t=t, e=e, index=index):
                acc[index] += terms[t][e].astype(jnp.float32)

    for i in range(count):
        outs[i][...] = acc[i].astype(jnp.bfloat16)


def finish_kernel(pos_ref, *refs):
    own, pieces, gk_ref, gv_ref = refs[:GROUP], refs[GROUP:-2], refs[-2], refs[-1]
    member = lax.rem(pos_ref[0], GROUP)
    for t in range(GROUP):
        cols = head_columns(wrap(member - t))
        for part, out in enumerate((gk_ref, gv_ref)):
            total = own[t][part]
            for piece in pieces[t::GROUP]:
                total = total + piece[part].astype(jnp.float32)
            out[:, cols] = total.astype(jnp.bfloat16)


def small_call(kernel, in_specs, out_specs, out_shape, moved, scratch=()):
    return pl.pallas_call(
        kernel,
        in_specs=in_specs,
        out_specs=out_specs,
        out_shape=out_shape,
        scratch_shapes=list(scratch),
        cost_estimate=cost(2 * moved, moved),
        compiler_params=pltpu.CompilerParams(vmem_limit_bytes=VMEM_LIMIT),
    )


def on_device(size, queries, keys, values, grad_out, block_path, assistant):
    rows = queries.shape[0]
    groups = size // GROUP
    pos = lax.axis_index("ctx").astype(jnp.int32).reshape(1)
    mask = jnp.broadcast_to(assistant[:, None].astype(jnp.bfloat16), (rows, HEAD_WIDTH))
    piece = jax.ShapeDtypeStruct((2, rows, HEAD_WIDTH), jnp.bfloat16)
    chosen = jax.ShapeDtypeStruct((FAR_SLOTS, 2, rows, HEAD_WIDTH), jnp.bfloat16)
    wide = jax.ShapeDtypeStruct(queries.shape, jnp.bfloat16)
    piece_bytes = 4 * rows * HEAD_WIDTH

    def inside(shift):
        return [(i, i - i % GROUP + (i + shift) % GROUP) for i in range(size)]

    def across(up, shift):
        pairs = []
        for i in range(size):
            group = i // GROUP + up
            if 0 <= group < groups:
                pairs.append((i, group * GROUP + (i + shift) % GROUP))
        return pairs

    def send(x, pairs):
        return lax.ppermute(x, "ctx", pairs)

    def far_sends(parts, sign):
        return [
            send(parts[(d * GROUP + t) % len(parts)], across(sign * d, t))
            for d in range(1, groups)
            for t in range(GROUP)
        ]

    def near_sends(parts, sign=1):
        return [parts[0]] + [send(parts[t], inside(sign * t)) for t in range(1, GROUP)]

    packed = small_call(
        pack_kernel, [SMEM_SPEC, HBM_SPEC, HBM_SPEC], [VMEM_SPEC] * GROUP,
        [piece] * GROUP, 8 * piece_bytes, [pltpu.SemaphoreType.DMA((2 * GROUP,))],
    )(pos, keys, values)
    far_pieces = far_sends(packed, 1)
    pieces = near_sends(packed) + far_pieces

    staged, grad_rows = small_call(
        stage_kernel, [VMEM_SPEC, HBM_SPEC, HBM_SPEC], [VMEM_SPEC] * 2, [wide] * 2,
        32 * piece_bytes, [pltpu.SemaphoreType.DMA((2,))],
    )(mask, queries, grad_out)

    picked = small_call(
        functools.partial(select_kernel, size),
        [SMEM_SPEC, SMEM_SPEC] + [VMEM_SPEC] * size, [VMEM_SPEC] * GROUP, [chosen] * GROUP,
        (size + 12) * piece_bytes, [pltpu.VMEM((size,) + piece.shape, jnp.bfloat16)],
    )(pos, block_path, *pieces)
    far = near_sends(picked)

    blocks, far_grads, own_grads = [], [], []
    for t in range(GROUP):
        attended, grad_query, far_grad, own_grad = attend(
            t, pos, block_path, staged, grad_rows, far[t], packed[-t % GROUP]
        )
        blocks += [attended, grad_query]
        far_grads.append(far_grad)
        own_grads.append(own_grad)
    far_grads = near_sends(far_grads, -1)

    attention, grad_queries = small_call(
        store_kernel, [SMEM_SPEC] + [VMEM_SPEC] * (2 * GROUP), [HBM_SPEC] * 2,
        [wide] * 2, 32 * piece_bytes, [pltpu.SemaphoreType.DMA((2 * GROUP,))],
    )(pos, *blocks)

    sums = small_call(
        functools.partial(reduce_kernel, size),
        [SMEM_SPEC, SMEM_SPEC] + [VMEM_SPEC] * GROUP, [VMEM_SPEC] * size, [piece] * size,
        (size + 12) * piece_bytes, [pltpu.VMEM((size,) + piece.shape, jnp.float32)],
    )(pos, block_path, *far_grads)
    far_sums = far_sends(sums, -1)
    near_sums = near_sends(sums[:GROUP])

    grad = jax.ShapeDtypeStruct(keys.shape, jnp.bfloat16)
    grad_keys, grad_values = small_call(
        finish_kernel, [SMEM_SPEC] + [VMEM_SPEC] * (GROUP + size), [VMEM_SPEC] * 2,
        [grad, grad], (size + 12) * piece_bytes,
    )(pos, *own_grads, *near_sums, *far_sums)
    return attention, grad_queries, grad_keys, grad_values


def solution(mesh):
    tokens = P(("leaf", "ctx"))

    def body(*args):
        return on_device(mesh.shape["ctx"], *args)

    return jax.shard_map(
        body,
        mesh=mesh,
        in_specs=(tokens, tokens, tokens, tokens, P("leaf"), tokens),
        out_specs=(tokens, tokens, tokens, tokens),
        check_vma=False,
    )
```

profile of v0, /device:TPU:0, one launch (start us, length us, event | category | flops | bytes accessed | tf_op | source)
XLA Modules:
  0.0 68.5 jit_solution(7014378126099278725)
XLA Ops:
  2.6 6.0 %collective-permute-start.3 = (bf16[2,128,128]{2,1,0:T(8,128)(2,1)S(1)}, bf16[2,128,128]{2,1,0:T(8,128)(2,1)S(1)}, u32[]{:S(2)}, u32[]{:S(2)}) collective-permute-start(bf16[2,128,128]{2,1,0:T(8,128)(2,1)S(1)} %get-tuple-element.44.refs_0_.refs_5_), channel_id=1, source_target_pairs={{0,4},{1,5},{2,6},{3,7},{8,12},{9,13},{10,14},{11,15},{16,20},{17,... | collective-permute-start | bytes 196616 | tf_op jit(solution)/shard_map/ppermute | solution.py:244
  8.6 2.2 %collective-permute-start.4 = (bf16[2,128,128]{2,1,0:T(8,128)(2,1)S(1)}, bf16[2,128,128]{2,1,0:T(8,128)(2,1)S(1)}, u32[]{:S(2)}, u32[]{:S(2)}) collective-permute-start(bf16[2,128,128]{2,1,0:T(8,128)(2,1)S(1)} %get-tuple-element.45.refs_5_), channel_id=1, source_target_pairs={{0,5},{1,6},{2,7},{3,4},{8,13},{9,14},{10,15},{11,12},{16,21},{17,... | collective-permute-start | bytes 196616 | tf_op jit(solution)/shard_map/ppermute | solution.py:244
  10.8 1.6 %collective-permute-start = (bf16[2,128,128]{2,1,0:T(8,128)(2,1)S(1)}, bf16[2,128,128]{2,1,0:T(8,128)(2,1)S(1)}, u32[]{:S(2)}, u32[]{:S(2)}) collective-permute-start(bf16[2,128,128]{2,1,0:T(8,128)(2,1)S(1)} %get-tuple-element.45.refs_5_), channel_id=1, source_target_pairs={{0,1},{1,2},{2,3},{3,0},{4,5},{5,6},{6,7},{7,4},{8,9},{9,10},{10,1... | collective-permute-start | bytes 196616 | tf_op jit(solution)/shard_map/ppermute | solution.py:244
  12.4 1.3 %collective-permute-start.5 = (bf16[2,128,128]{2,1,0:T(8,128)(2,1)S(1)}, bf16[2,128,128]{2,1,0:T(8,128)(2,1)S(1)}, u32[]{:S(2)}, u32[]{:S(2)}) collective-permute-start(bf16[2,128,128]{2,1,0:T(8,128)(2,1)S(1)} %get-tuple-element.46.refs_5_), channel_id=1, source_target_pairs={{0,6},{1,7},{2,4},{3,5},{8,14},{9,15},{10,12},{11,13},{16,22},{17,... | collective-permute-start | bytes 196616 | tf_op jit(solution)/shard_map/ppermute | solution.py:244
  14.4 5.9 %collective-permute-start.6 = (bf16[2,128,128]{2,1,0:T(8,128)(2,1)S(1)}, bf16[2,128,128]{2,1,0:T(8,128)(2,1)S(1)}, u32[]{:S(2)}, u32[]{:S(2)}) collective-permute-start(bf16[2,128,128]{2,1,0:T(8,128)(2,1)S(1)} %get-tuple-element.47.refs_5_), channel_id=1, source_target_pairs={{0,7},{1,4},{2,5},{3,6},{8,15},{9,12},{10,13},{11,14},{16,23},{17,... | collective-permute-start | bytes 196616 | tf_op jit(solution)/shard_map/ppermute | solution.py:244
  22.2 2.4 %collective-permute-done.2.refs_3_ = bf16[2,128,128]{2,1,0:T(8,128)(2,1)S(1)} collective-permute-done((bf16[2,128,128]{2,1,0:T(8,128)(2,1)S(1)}, bf16[2,128,128]{2,1,0:T(8,128)(2,1)S(1)}, u32[]{:S(2)}, u32[]{:S(2)}) %collective-permute-start.2) | collective-permute-done | bytes 65568 | tf_op jit(solution)/shard_map/ppermute | solution.py:244
  25.4 1.6 %collective-permute-start.9 = (bf16[3,2,128,128]{3,2,1,0:T(8,128)(2,1)S(1)}, bf16[3,2,128,128]{3,2,1,0:T(8,128)(2,1)S(1)}, u32[]{:S(2)}, u32[]{:S(2)}) collective-permute-start(bf16[3,2,128,128]{3,2,1,0:T(8,128)(2,1)S(1)} %get-tuple-element.57), channel_id=1, source_target_pairs={{0,3},{1,0},{2,1},{3,2},{4,7},{5,4},{6,5},{7,6},{8,11},{9,8},{10,9... | collective-permute-start | bytes 589832 | tf_op jit(solution)/shard_map/ppermute | solution.py:244
  28.9 1.2 %copy-done.1 = bf16[128,4096]{1,0:T(8,128)(2,1)S(1)} copy-done((bf16[128,4096]{1,0:T(8,128)(2,1)S(1)}, bf16[128,4096]{1,0:T(8,128)(2,1)}, u32[]{:S(2)}) %copy-start.1) | copy-done | bytes 1048600
  30.6 2.1 %collective-permute-done.9.refs_4_ = bf16[3,2,128,128]{3,2,1,0:T(8,128)(2,1)S(1)} collective-permute-done((bf16[3,2,128,128]{3,2,1,0:T(8,128)(2,1)S(1)}, bf16[3,2,128,128]{3,2,1,0:T(8,128)(2,1)S(1)}, u32[]{:S(2)}, u32[]{:S(2)}) %collective-permute-start.9) | collective-permute-done | bytes 196640 | tf_op jit(solution)/shard_map/ppermute | solution.py:244
  32.6 2.8 %shard_map.99 = (bf16[128,1024]{1,0:T(8,128)(2,1)S(1)}, bf16[128,1024]{1,0:T(8,128)(2,1)S(1)}, bf16[3,2,128,128]{3,2,1,0:T(8,128)(2,1)S(1)}, f32[2,128,128]{2,1,0:T(8,128)S(1)}) custom-call(s32[1]{0:T(128)} %bitcast.pos_ref.refs_0_, s32[8,4]{1,0:T(8,128)S(1)} %copy.11.path_ref.refs_1_, bf16[128,4096]{1,0:T(8,128)(2,1)S(1)} %get-tuple-element.42.refs_2_, ...), custom_call_target="tpu_custom_call" | custom-call | flops 805306368 | bytes 1048576 | tf_op jit(solution)/shard_map/pallas_call | solution.py:146
  36.3 2.8 %shard_map.98 = (bf16[128,1024]{1,0:T(8,128)(2,1)S(1)}, bf16[128,1024]{1,0:T(8,128)(2,1)S(1)}, bf16[3,2,128,128]{3,2,1,0:T(8,128)(2,1)S(1)}, f32[2,128,128]{2,1,0:T(8,128)S(1)}) custom-call(s32[1]{0:T(128)} %bitcast.pos_ref.refs_0_, s32[8,4]{1,0:T(8,128)S(1)} %copy.11.path_ref.refs_1_, bf16[128,4096]{1,0:T(8,128)(2,1)S(1)} %get-tuple-element.42.refs_2_, ...), custom_call_target="tpu_custom_call" | custom-call | flops 805306368 | bytes 1048576 | tf_op jit(solution)/shard_map/pallas_call | solution.py:146
  39.1 1.5 %collective-permute-start.11 = (bf16[3,2,128,128]{3,2,1,0:T(8,128)(2,1)S(1)}, bf16[3,2,128,128]{3,2,1,0:T(8,128)(2,1)S(1)}, u32[]{:S(2)}, u32[]{:S(2)}) collective-permute-start(bf16[3,2,128,128]{3,2,1,0:T(8,128)(2,1)S(1)} %get-tuple-element.68), channel_id=1, source_target_pairs={{0,2},{1,3},{2,0},{3,1},{4,6},{5,7},{6,4},{7,5},{8,10},{9,11},{10,... | collective-permute-start | bytes 589832 | tf_op jit(solution)/shard_map/ppermute | solution.py:244
  40.6 2.8 %shard_map.97 = (bf16[128,1024]{1,0:T(8,128)(2,1)S(1)}, bf16[128,1024]{1,0:T(8,128)(2,1)S(1)}, bf16[3,2,128,128]{3,2,1,0:T(8,128)(2,1)S(1)}, f32[2,128,128]{2,1,0:T(8,128)S(1)}) custom-call(s32[1]{0:T(128)} %bitcast.pos_ref.refs_0_, s32[8,4]{1,0:T(8,128)S(1)} %copy.11.path_ref.refs_1_, bf16[128,4096]{1,0:T(8,128)(2,1)S(1)} %get-tuple-element.42.refs_2_, ...), custom_call_target="tpu_custom_call" | custom-call | flops 805306368 | bytes 1048576 | tf_op jit(solution)/shard_map/pallas_call | solution.py:146
  43.4 1.4 %collective-permute-start.10 = (bf16[3,2,128,128]{3,2,1,0:T(8,128)(2,1)S(1)}, bf16[3,2,128,128]{3,2,1,0:T(8,128)(2,1)S(1)}, u32[]{:S(2)}, u32[]{:S(2)}) collective-permute-start(bf16[3,2,128,128]{3,2,1,0:T(8,128)(2,1)S(1)} %get-tuple-element.67), channel_id=1, source_target_pairs={{0,3},{1,0},{2,1},{3,2},{4,7},{5,4},{6,5},{7,6},{8,11},{9,8},{10,9... | collective-permute-start | bytes 589832 | tf_op jit(solution)/shard_map/ppermute | solution.py:244
  44.8 2.8 %shard_map.96 = (bf16[128,1024]{1,0:T(8,128)(2,1)S(1)}, bf16[128,1024]{1,0:T(8,128)(2,1)S(1)}, bf16[3,2,128,128]{3,2,1,0:T(8,128)(2,1)S(1)}, f32[2,128,128]{2,1,0:T(8,128)S(1)}) custom-call(s32[1]{0:T(128)} %bitcast.pos_ref.refs_0_, s32[8,4]{1,0:T(8,128)S(1)} %copy.11.path_ref.refs_1_, bf16[128,4096]{1,0:T(8,128)(2,1)S(1)} %get-tuple-element.42.refs_2_, ...), custom_call_target="tpu_custom_call" | custom-call | flops 805306368 | bytes 1048576 | tf_op jit(solution)/shard_map/pallas_call | solution.py:146
  47.6 2.5 %collective-permute-done.10.refs_1_ = bf16[3,2,128,128]{3,2,1,0:T(8,128)(2,1)S(1)} collective-permute-done((bf16[3,2,128,128]{3,2,1,0:T(8,128)(2,1)S(1)}, bf16[3,2,128,128]{3,2,1,0:T(8,128)(2,1)S(1)}, u32[]{:S(2)}, u32[]{:S(2)}) %collective-permute-start.10) | collective-permute-done | bytes 196640 | tf_op jit(solution)/shard_map/ppermute | solution.py:244
  51.0 2.3 %collective-permute-start.13 = (bf16[2,128,128]{2,1,0:T(8,128)(2,1)S(1)}, bf16[2,128,128]{2,1,0:T(8,128)(2,1)S(1)}, u32[]{:S(2)}, u32[]{:S(2)}) collective-permute-start(bf16[2,128,128]{2,1,0:T(8,128)(2,1)S(1)} %get-tuple-element.71), channel_id=1, source_target_pairs={{0,1},{1,2},{2,3},{3,0},{4,5},{5,6},{6,7},{7,4},{8,9},{9,10},{10,1... | collective-permute-start | bytes 196616 | tf_op jit(solution)/shard_map/ppermute | solution.py:244
  54.8 1.3 %collective-permute-start.16 = (bf16[2,128,128]{2,1,0:T(8,128)(2,1)S(1)}, bf16[2,128,128]{2,1,0:T(8,128)(2,1)S(1)}, u32[]{:S(2)}, u32[]{:S(2)}) collective-permute-start(bf16[2,128,128]{2,1,0:T(8,128)(2,1)S(1)} %get-tuple-element.74), channel_id=1, source_target_pairs={{4,0},{5,1},{6,2},{7,3},{12,8},{13,9},{14,10},{15,11},{20,16},{21,... | collective-permute-start | bytes 196616 | tf_op jit(solution)/shard_map/ppermute | solution.py:244
  56.1 1.3 %collective-permute-start.17 = (bf16[2,128,128]{2,1,0:T(8,128)(2,1)S(1)}, bf16[2,128,128]{2,1,0:T(8,128)(2,1)S(1)}, u32[]{:S(2)}, u32[]{:S(2)}) collective-permute-start(bf16[2,128,128]{2,1,0:T(8,128)(2,1)S(1)} %get-tuple-element.75), channel_id=1, source_target_pairs={{4,1},{5,2},{6,3},{7,0},{12,9},{13,10},{14,11},{15,8},{20,17},{21,... | collective-permute-start | bytes 196616 | tf_op jit(solution)/shard_map/ppermute | solution.py:244
  57.4 1.3 %collective-permute-start.18 = (bf16[2,128,128]{2,1,0:T(8,128)(2,1)S(1)}, bf16[2,128,128]{2,1,0:T(8,128)(2,1)S(1)}, u32[]{:S(2)}, u32[]{:S(2)}) collective-permute-start(bf16[2,128,128]{2,1,0:T(8,128)(2,1)S(1)} %get-tuple-element.76), channel_id=1, source_target_pairs={{4,2},{5,3},{6,0},{7,1},{12,10},{13,11},{14,8},{15,9},{20,18},{21,... | collective-permute-start | bytes 196616 | tf_op jit(solution)/shard_map/ppermute | solution.py:244
  58.7 1.3 %collective-permute-start.19 = (bf16[2,128,128]{2,1,0:T(8,128)(2,1)S(1)}, bf16[2,128,128]{2,1,0:T(8,128)(2,1)S(1)}, u32[]{:S(2)}, u32[]{:S(2)}) collective-permute-start(bf16[2,128,128]{2,1,0:T(8,128)(2,1)S(1)} %get-tuple-element.77), channel_id=1, source_target_pairs={{4,3},{5,0},{6,1},{7,2},{12,11},{13,8},{14,9},{15,10},{20,19},{21,... | collective-permute-start | bytes 196616 | tf_op jit(solution)/shard_map/ppermute | solution.py:244
  60.0 1.4 %shard_map.100 = (bf16[128,4096]{1,0:T(8,128)(2,1)}, bf16[128,4096]{1,0:T(8,128)(2,1)}) custom-call(s32[1]{0:T(128)} %bitcast.pos_ref.refs_0_, bf16[128,1024]{1,0:T(8,128)(2,1)S(1)} %get-tuple-element.49.refs_0_, bf16[128,1024]{1,0:T(8,128)(2,1)S(1)} %get-tuple-element.50.refs_1_, bf16[128,1024]{1,0:T(8,128)(2,1)S(1)} %get-tuple-element.52.refs_2_, ...), custom_call_target="tpu_custom_call" | custom-call | flops 4194304 | bytes 2097152 | tf_op jit(solution)/shard_map/pallas_call | solution.py:285
  61.9 3.1 %collective-permute-done.17.refs_9_ = bf16[2,128,128]{2,1,0:T(8,128)(2,1)S(1)} collective-permute-done((bf16[2,128,128]{2,1,0:T(8,128)(2,1)S(1)}, bf16[2,128,128]{2,1,0:T(8,128)(2,1)S(1)}, u32[]{:S(2)}, u32[]{:S(2)}) %collective-permute-start.17) | collective-permute-done | bytes 65568 | tf_op jit(solution)/shard_map/ppermute | solution.py:244
  65.9 1.8 %collective-permute-done.19.refs_11_ = bf16[2,128,128]{2,1,0:T(8,128)(2,1)S(1)} collective-permute-done((bf16[2,128,128]{2,1,0:T(8,128)(2,1)S(1)}, bf16[2,128,128]{2,1,0:T(8,128)(2,1)S(1)}, u32[]{:S(2)}, u32[]{:S(2)}) %collective-permute-start.19) | collective-permute-done | bytes 65568 | tf_op jit(solution)/shard_map/ppermute | solution.py:244
  (41 shorter events, 13.0 us)
Async XLA Ops:
  0.6 0.9 %copy-start.2 = (bf16[128,512]{1,0:T(8,128)(2,1)S(1)}, bf16[128,512]{1,0:T(8,128)(2,1)}, u32[]{:S(2)}) copy-start(bf16[128,512]{1,0:T(8,128)(2,1)} %k_ref.1) | copy-start | bytes 393220
  2.6 11.8 %collective-permute-start.3 = (bf16[2,128,128]{2,1,0:T(8,128)(2,1)S(1)}, bf16[2,128,128]{2,1,0:T(8,128)(2,1)S(1)}, u32[]{:S(2)}, u32[]{:S(2)}) collective-permute-start(bf16[2,128,128]{2,1,0:T(8,128)(2,1)S(1)} %get-tuple-element.44.refs_0_.refs_5_), channel_id=1, source_target_pairs={{0,4},{1,5},{2,6},{3,7},{8,12},{9,13},{10,14},{11,15},{16,20},{17,... | collective-permute-start | bytes 196616 | tf_op jit(solution)/shard_map/ppermute | solution.py:244
  8.6 12.4 %copy-start.4 = (s32[8,4]{0,1:T(4,128)S(1)}, s32[8,4]{0,1:T(4,128)}, u32[]{:S(2)}) copy-start(s32[8,4]{0,1:T(4,128)} %param.10) | copy-start | bytes 388
  8.6 11.7 %collective-permute-start.4 = (bf16[2,128,128]{2,1,0:T(8,128)(2,1)S(1)}, bf16[2,128,128]{2,1,0:T(8,128)(2,1)S(1)}, u32[]{:S(2)}, u32[]{:S(2)}) collective-permute-start(bf16[2,128,128]{2,1,0:T(8,128)(2,1)S(1)} %get-tuple-element.45.refs_5_), channel_id=1, source_target_pairs={{0,5},{1,6},{2,7},{3,4},{8,13},{9,14},{10,15},{11,12},{16,21},{17,... | collective-permute-start | bytes 196616 | tf_op jit(solution)/shard_map/ppermute | solution.py:244
  10.8 10.2 %collective-permute-start = (bf16[2,128,128]{2,1,0:T(8,128)(2,1)S(1)}, bf16[2,128,128]{2,1,0:T(8,128)(2,1)S(1)}, u32[]{:S(2)}, u32[]{:S(2)}) collective-permute-start(bf16[2,128,128]{2,1,0:T(8,128)(2,1)S(1)} %get-tuple-element.45.refs_5_), channel_id=1, source_target_pairs={{0,1},{1,2},{2,3},{3,0},{4,5},{5,6},{6,7},{7,4},{8,9},{9,10},{10,1... | collective-permute-start | bytes 196616 | tf_op jit(solution)/shard_map/ppermute | solution.py:244
  12.4 8.6 %collective-permute-start.5 = (bf16[2,128,128]{2,1,0:T(8,128)(2,1)S(1)}, bf16[2,128,128]{2,1,0:T(8,128)(2,1)S(1)}, u32[]{:S(2)}, u32[]{:S(2)}) collective-permute-start(bf16[2,128,128]{2,1,0:T(8,128)(2,1)S(1)} %get-tuple-element.46.refs_5_), channel_id=1, source_target_pairs={{0,6},{1,7},{2,4},{3,5},{8,14},{9,15},{10,12},{11,13},{16,22},{17,... | collective-permute-start | bytes 196616 | tf_op jit(solution)/shard_map/ppermute | solution.py:244
  13.8 7.3 %collective-permute-start.1 = (bf16[2,128,128]{2,1,0:T(8,128)(2,1)S(1)}, bf16[2,128,128]{2,1,0:T(8,128)(2,1)S(1)}, u32[]{:S(2)}, u32[]{:S(2)}) collective-permute-start(bf16[2,128,128]{2,1,0:T(8,128)(2,1)S(1)} %get-tuple-element.46.refs_5_), channel_id=1, source_target_pairs={{0,2},{1,3},{2,0},{3,1},{4,6},{5,7},{6,4},{7,5},{8,10},{9,11},{10,... | collective-permute-start | bytes 196616 | tf_op jit(solution)/shard_map/ppermute | solution.py:244
  14.4 7.8 %collective-permute-start.6 = (bf16[2,128,128]{2,1,0:T(8,128)(2,1)S(1)}, bf16[2,128,128]{2,1,0:T(8,128)(2,1)S(1)}, u32[]{:S(2)}, u32[]{:S(2)}) collective-permute-start(bf16[2,128,128]{2,1,0:T(8,128)(2,1)S(1)} %get-tuple-element.47.refs_5_), channel_id=1, source_target_pairs={{0,7},{1,4},{2,5},{3,6},{8,15},{9,12},{10,13},{11,14},{16,23},{17,... | collective-permute-start | bytes 196616 | tf_op jit(solution)/shard_map/ppermute | solution.py:244
  20.3 4.3 %collective-permute-start.2 = (bf16[2,128,128]{2,1,0:T(8,128)(2,1)S(1)}, bf16[2,128,128]{2,1,0:T(8,128)(2,1)S(1)}, u32[]{:S(2)}, u32[]{:S(2)}) collective-permute-start(bf16[2,128,128]{2,1,0:T(8,128)(2,1)S(1)} %get-tuple-element.47.refs_5_), channel_id=1, source_target_pairs={{0,3},{1,0},{2,1},{3,2},{4,7},{5,4},{6,5},{7,6},{8,11},{9,8},{10,9... | collective-permute-start | bytes 196616 | tf_op jit(solution)/shard_map/ppermute | solution.py:244
  25.4 7.3 %collective-permute-start.9 = (bf16[3,2,128,128]{3,2,1,0:T(8,128)(2,1)S(1)}, bf16[3,2,128,128]{3,2,1,0:T(8,128)(2,1)S(1)}, u32[]{:S(2)}, u32[]{:S(2)}) collective-permute-start(bf16[3,2,128,128]{3,2,1,0:T(8,128)(2,1)S(1)} %get-tuple-element.57), channel_id=1, source_target_pairs={{0,3},{1,0},{2,1},{3,2},{4,7},{5,4},{6,5},{7,6},{8,11},{9,8},{10,9... | collective-permute-start | bytes 589832 | tf_op jit(solution)/shard_map/ppermute | solution.py:244
  26.9 9.3 %collective-permute-start.8 = (bf16[3,2,128,128]{3,2,1,0:T(8,128)(2,1)S(1)}, bf16[3,2,128,128]{3,2,1,0:T(8,128)(2,1)S(1)}, u32[]{:S(2)}, u32[]{:S(2)}) collective-permute-start(bf16[3,2,128,128]{3,2,1,0:T(8,128)(2,1)S(1)} %get-tuple-element.54), channel_id=1, source_target_pairs={{0,2},{1,3},{2,0},{3,1},{4,6},{5,7},{6,4},{7,5},{8,10},{9,11},{10,... | collective-permute-start | bytes 589832 | tf_op jit(solution)/shard_map/ppermute | solution.py:244
  26.9 13.6 %collective-permute-start.7 = (bf16[3,2,128,128]{3,2,1,0:T(8,128)(2,1)S(1)}, bf16[3,2,128,128]{3,2,1,0:T(8,128)(2,1)S(1)}, u32[]{:S(2)}, u32[]{:S(2)}) collective-permute-start(bf16[3,2,128,128]{3,2,1,0:T(8,128)(2,1)S(1)} %get-tuple-element.51), channel_id=1, source_target_pairs={{0,1},{1,2},{2,3},{3,0},{4,5},{5,6},{6,7},{7,4},{8,9},{9,10},{10,1... | collective-permute-start | bytes 589832 | tf_op jit(solution)/shard_map/ppermute | solution.py:244
  27.7 1.2 %copy-start = (bf16[128,4096]{1,0:T(8,128)(2,1)S(1)}, bf16[128,4096]{1,0:T(8,128)(2,1)}, u32[]{:S(2)}) copy-start(bf16[128,4096]{1,0:T(8,128)(2,1)} %q_hbm.1) | copy-start | bytes 3145732
  28.9 1.2 %copy-start.1 = (bf16[128,4096]{1,0:T(8,128)(2,1)S(1)}, bf16[128,4096]{1,0:T(8,128)(2,1)}, u32[]{:S(2)}) copy-start(bf16[128,4096]{1,0:T(8,128)(2,1)} %go_hbm.1) | copy-start | bytes 3145732
  35.4 12.1 %collective-permute-start.12 = (bf16[3,2,128,128]{3,2,1,0:T(8,128)(2,1)S(1)}, bf16[3,2,128,128]{3,2,1,0:T(8,128)(2,1)S(1)}, u32[]{:S(2)}, u32[]{:S(2)}) collective-permute-start(bf16[3,2,128,128]{3,2,1,0:T(8,128)(2,1)S(1)} %get-tuple-element.69), channel_id=1, source_target_pairs={{0,1},{1,2},{2,3},{3,0},{4,5},{5,6},{6,7},{7,4},{8,9},{9,10},{10,1... | collective-permute-start | bytes 589832 | tf_op jit(solution)/shard_map/ppermute | solution.py:244
  39.1 8.5 %collective-permute-start.11 = (bf16[3,2,128,128]{3,2,1,0:T(8,128)(2,1)S(1)}, bf16[3,2,128,128]{3,2,1,0:T(8,128)(2,1)S(1)}, u32[]{:S(2)}, u32[]{:S(2)}) collective-permute-start(bf16[3,2,128,128]{3,2,1,0:T(8,128)(2,1)S(1)} %get-tuple-element.68), channel_id=1, source_target_pairs={{0,2},{1,3},{2,0},{3,1},{4,6},{5,7},{6,4},{7,5},{8,10},{9,11},{10,... | collective-permute-start | bytes 589832 | tf_op jit(solution)/shard_map/ppermute | solution.py:244
  43.4 6.7 %collective-permute-start.10 = (bf16[3,2,128,128]{3,2,1,0:T(8,128)(2,1)S(1)}, bf16[3,2,128,128]{3,2,1,0:T(8,128)(2,1)S(1)}, u32[]{:S(2)}, u32[]{:S(2)}) collective-permute-start(bf16[3,2,128,128]{3,2,1,0:T(8,128)(2,1)S(1)} %get-tuple-element.67), channel_id=1, source_target_pairs={{0,3},{1,0},{2,1},{3,2},{4,7},{5,4},{6,5},{7,6},{8,11},{9,8},{10,9... | collective-permute-start | bytes 589832 | tf_op jit(solution)/shard_map/ppermute | solution.py:244
  51.0 6.4 %collective-permute-start.13 = (bf16[2,128,128]{2,1,0:T(8,128)(2,1)S(1)}, bf16[2,128,128]{2,1,0:T(8,128)(2,1)S(1)}, u32[]{:S(2)}, u32[]{:S(2)}) collective-permute-start(bf16[2,128,128]{2,1,0:T(8,128)(2,1)S(1)} %get-tuple-element.71), channel_id=1, source_target_pairs={{0,1},{1,2},{2,3},{3,0},{4,5},{5,6},{6,7},{7,4},{8,9},{9,10},{10,1... | collective-permute-start | bytes 196616 | tf_op jit(solution)/shard_map/ppermute | solution.py:244
  53.3 5.4 %collective-permute-start.14 = (bf16[2,128,128]{2,1,0:T(8,128)(2,1)S(1)}, bf16[2,128,128]{2,1,0:T(8,128)(2,1)S(1)}, u32[]{:S(2)}, u32[]{:S(2)}) collective-permute-start(bf16[2,128,128]{2,1,0:T(8,128)(2,1)S(1)} %get-tuple-element.72), channel_id=1, source_target_pairs={{0,2},{1,3},{2,0},{3,1},{4,6},{5,7},{6,4},{7,5},{8,10},{9,11},{10,... | collective-permute-start | bytes 196616 | tf_op jit(solution)/shard_map/ppermute | solution.py:244
  53.8 7.6 %collective-permute-start.15 = (bf16[2,128,128]{2,1,0:T(8,128)(2,1)S(1)}, bf16[2,128,128]{2,1,0:T(8,128)(2,1)S(1)}, u32[]{:S(2)}, u32[]{:S(2)}) collective-permute-start(bf16[2,128,128]{2,1,0:T(8,128)(2,1)S(1)} %get-tuple-element.73), channel_id=1, source_target_pairs={{0,3},{1,0},{2,1},{3,2},{4,7},{5,4},{6,5},{7,6},{8,11},{9,8},{10,9... | collective-permute-start | bytes 196616 | tf_op jit(solution)/shard_map/ppermute | solution.py:244
  54.8 7.1 %collective-permute-start.16 = (bf16[2,128,128]{2,1,0:T(8,128)(2,1)S(1)}, bf16[2,128,128]{2,1,0:T(8,128)(2,1)S(1)}, u32[]{:S(2)}, u32[]{:S(2)}) collective-permute-start(bf16[2,128,128]{2,1,0:T(8,128)(2,1)S(1)} %get-tuple-element.74), channel_id=1, source_target_pairs={{4,0},{5,1},{6,2},{7,3},{12,8},{13,9},{14,10},{15,11},{20,16},{21,... | collective-permute-start | bytes 196616 | tf_op jit(solution)/shard_map/ppermute | solution.py:244
  56.1 8.9 %collective-permute-start.17 = (bf16[2,128,128]{2,1,0:T(8,128)(2,1)S(1)}, bf16[2,128,128]{2,1,0:T(8,128)(2,1)S(1)}, u32[]{:S(2)}, u32[]{:S(2)}) collective-permute-start(bf16[2,128,128]{2,1,0:T(8,128)(2,1)S(1)} %get-tuple-element.75), channel_id=1, source_target_pairs={{4,1},{5,2},{6,3},{7,0},{12,9},{13,10},{14,11},{15,8},{20,17},{21,... | collective-permute-start | bytes 196616 | tf_op jit(solution)/shard_map/ppermute | solution.py:244
  57.4 8.5 %collective-permute-start.18 = (bf16[2,128,128]{2,1,0:T(8,128)(2,1)S(1)}, bf16[2,128,128]{2,1,0:T(8,128)(2,1)S(1)}, u32[]{:S(2)}, u32[]{:S(2)}) collective-permute-start(bf16[2,128,128]{2,1,0:T(8,128)(2,1)S(1)} %get-tuple-element.76), channel_id=1, source_target_pairs={{4,2},{5,3},{6,0},{7,1},{12,10},{13,11},{14,8},{15,9},{20,18},{21,... | collective-permute-start | bytes 196616 | tf_op jit(solution)/shard_map/ppermute | solution.py:244
  58.7 9.0 %collective-permute-start.19 = (bf16[2,128,128]{2,1,0:T(8,128)(2,1)S(1)}, bf16[2,128,128]{2,1,0:T(8,128)(2,1)S(1)}, u32[]{:S(2)}, u32[]{:S(2)}) collective-permute-start(bf16[2,128,128]{2,1,0:T(8,128)(2,1)S(1)} %get-tuple-element.77), channel_id=1, source_target_pairs={{4,3},{5,0},{6,1},{7,2},{12,11},{13,8},{14,9},{15,10},{20,19},{21,... | collective-permute-start | bytes 196616 | tf_op jit(solution)/shard_map/ppermute | solution.py:244
  (2 other events, 1.6 us)
where the time goes:
time: 68.9 us; the launch traced here: 68.5 us
  starting transfers between devices  33.2 us (48%)
  Pallas kernels  15.5 us (22%)
  waiting for transfers between devices  14.6 us (21%)
  local copies, waits for them, and re-layouts  4.42 us (6%)
  between operations  0.86 us (1%)
    ppermute x20, starting transfers between devices, send(): return lax.ppermute(x, 'ctx', pairs)  33.2 us
    ppermute x20, waiting for transfers between devices, send(): return lax.ppermute(x, 'ctx', pairs)  14.6 us
    pallas_call x4, Pallas kernels, attend(): pl.pallas_call(functools.partial(attend_kernel, turn, rows), in_specs=[SM...  11.2 us
    unnamed x13, local copies, waits for them, and re-layouts  4.34 us
    pallas_call x1, Pallas kernels, on_device(): small_call(store_kernel, [SMEM_SPEC] + [VMEM_SPEC] * (2 * GROUP), [HBM_SP...  1.39 us
  transfers between devices with their start and end apart: 20, of which 8 were waited for; matrix products, arithmetic and copies ran while one was open for 0% of the time, Pallas kernels for 19%

commit v1 on v0

--- a/solution.py
+++ b/solution.py
@@ -15,12 +15,26 @@
 FAR_SLOTS = 3
 GROUP = KEY_HEADS
 MASKED = -1e30
+COVER_FLOPS = 4_000_000_000
 VMEM_LIMIT = 24 * 1024 * 1024
 
 
 SMEM_SPEC = pl.BlockSpec(memory_space=pltpu.SMEM)
 VMEM_SPEC = pl.BlockSpec(memory_space=pltpu.VMEM)
 HBM_SPEC = pl.BlockSpec(memory_space=pltpu.HBM)
+
+
+LAST = (((1,), (1,)), ((), ()))
+FIRST = (((0,), (0,)), ((), ()))
+SCALING = 1.0 / math.sqrt(HEAD_WIDTH)
+
+
+def dot(left, right, dims=(((1,), (0,)), ((), ()))):
+    return lax.dot_general(left, right, dims, preferred_element_type=jnp.float32)
+
+
+def stack_slots(far_ref, own_ref, part):
+    return jnp.concatenate([far_ref[e, part] for e in range(FAR_SLOTS)] + [own_ref[part]], 0)
 
 
 def wrap(x):
@@ -67,47 +81,21 @@
             outs[t][e] = held[jnp.where(seen, index, 0)]
 
 
-def stage_kernel(mask_ref, q_hbm, go_hbm, q_ref, gm_ref, sem):
-    copies = [
-        pltpu.make_async_copy(q_hbm, q_ref, sem.at[0]),
-        pltpu.make_async_copy(go_hbm, gm_ref, sem.at[1]),
-    ]
-    for copy in copies:
-        copy.start()
-    for copy in copies:
-        copy.wait()
-    mask = mask_ref[...]
-    for i in range(gm_ref.shape[1] // HEAD_WIDTH):
-        cols = slice(i * HEAD_WIDTH, (i + 1) * HEAD_WIDTH)
-        gm_ref[:, cols] = gm_ref[:, cols] * mask
-
-
 def attend_kernel(turn, rows, *refs):
-    (pos_ref, path_ref, q_ref, gm_ref, far_ref, own_ref) = refs[:6]
-    attn_ref, gq_ref, far_grad_ref, own_grad_ref = refs[6:]
-    scaling = 1.0 / math.sqrt(HEAD_WIDTH)
+    (pos_ref, path_ref, mask_ref, q_ref, go_ref, far_ref, own_ref) = refs[:7]
+    weights_ref, grad_score_ref, far_grad_ref, own_grad_ref = refs[7:]
     position = pos_ref[0]
     head = wrap(lax.rem(position, GROUP) - turn)
     far_rows = FAR_SLOTS * rows
-    last = (((1,), (1,)), ((), ()))
-    first = (((0,), (0,)), ((), ()))
-
-    def dot(left, right, dims=(((1,), (0,)), ((), ()))):
-        return lax.dot_general(left, right, dims, preferred_element_type=jnp.float32)
-
-    def rows_of(ref):
-        parts = [
-            ref[:, head_columns(head * HEADS_PER_KEY + i)] for i in range(HEADS_PER_KEY)
-        ]
-        return jnp.concatenate(parts, 0)
-
-    kk = jnp.concatenate([far_ref[e, 0] for e in range(FAR_SLOTS)] + [own_ref[0]], 0)
-    vv = jnp.concatenate([far_ref[e, 1] for e in range(FAR_SLOTS)] + [own_ref[1]], 0)
-    qm, gm = rows_of(q_ref), rows_of(gm_ref)
+    mask = mask_ref[...]
+    blocks = [head_columns(head * HEADS_PER_KEY + i) for i in range(HEADS_PER_KEY)]
+    kk, vv = stack_slots(far_ref, own_ref, 0), stack_slots(far_ref, own_ref, 1)
+    qm = jnp.concatenate([q_ref[:, cols] for cols in blocks], 0)
+    gm = jnp.concatenate([go_ref[:, cols] * mask for cols in blocks], 0)
     key = lax.broadcasted_iota(jnp.int32, (rows, rows), 0)
     token = lax.broadcasted_iota(jnp.int32, (rows, rows), 1)
     causal = jnp.where(key <= token, 0.0, MASKED)
-    scores = dot(kk, qm, last)
+    scores = dot(kk, qm, LAST)
     parts = [
         scores[e * rows : (e + 1) * rows] + jnp.where(path_ref[position, e + 1] >= 0, 0.0, MASKED)
         for e in range(FAR_SLOTS)
@@ -115,20 +103,15 @@
     parts.append(scores[far_rows:] + jnp.concatenate([causal] * HEADS_PER_KEY, 1))
     scores = jnp.concatenate(parts, 0)
     top = jnp.max(scores, axis=0, keepdims=True)
-    weights = jnp.exp2((scores - top) * (scaling * math.log2(math.e)))
+    weights = jnp.exp2((scores - top) * (SCALING * math.log2(math.e)))
     weights = weights * (1.0 / jnp.sum(weights, axis=0, keepdims=True))
     rounded = weights.astype(jnp.bfloat16)
-    grad_prob = dot(vv, gm, last)
+    grad_prob = dot(vv, gm, LAST)
     delta = jnp.sum(weights * grad_prob, axis=0, keepdims=True)
     grad_score = (weights * (grad_prob - delta)).astype(jnp.bfloat16)
-    attended = dot(vv, rounded, first)
-    grad_query = dot(kk, grad_score, first) * scaling
-    for i in range(HEADS_PER_KEY):
-        s = slice(i * rows, (i + 1) * rows)
-        cols = slice(i * HEAD_WIDTH, (i + 1) * HEAD_WIDTH)
-        attn_ref[:, cols] = attended[:, s].T.astype(jnp.bfloat16)
-        gq_ref[:, cols] = grad_query[:, s].T.astype(jnp.bfloat16)
-    grad_key = dot(grad_score, qm) * scaling
+    weights_ref[...] = rounded
+    grad_score_ref[...] = grad_score
+    grad_key = dot(grad_score, qm) * SCALING
     grad_value = dot(rounded, gm)
     for e in range(FAR_SLOTS):
         s = slice(e * rows, (e + 1) * rows)
@@ -138,24 +121,49 @@
     own_grad_ref[1] = grad_value[far_rows:]
 
 
-def attend(turn, pos, path, queries, grad_rows, far, own):
+def output_kernel(rows, *refs):
+    weights_ref, grad_score_ref, far_ref, own_ref, attn_ref, gq_ref = refs
+    kk, vv = stack_slots(far_ref, own_ref, 0), stack_slots(far_ref, own_ref, 1)
+    attended = dot(vv, weights_ref[...], FIRST)
+    grad_query = dot(kk, grad_score_ref[...], FIRST) * SCALING
+    for i in range(HEADS_PER_KEY):
+        s = slice(i * rows, (i + 1) * rows)
+        cols = slice(i * HEAD_WIDTH, (i + 1) * HEAD_WIDTH)
+        attn_ref[:, cols] = attended[:, s].T.astype(jnp.bfloat16)
+        gq_ref[:, cols] = grad_query[:, s].T.astype(jnp.bfloat16)
+
+
+def attend(turn, pos, path, mask, queries, grad_out, far, own):
     rows = queries.shape[0]
-    width = HEADS_PER_KEY * HEAD_WIDTH
-    block = jax.ShapeDtypeStruct((rows, width), jnp.bfloat16)
     span = (FAR_SLOTS + 1) * rows
+    pairs = rows * HEADS_PER_KEY * span
+    square = jax.ShapeDtypeStruct((span, HEADS_PER_KEY * rows), jnp.bfloat16)
     return pl.pallas_call(
         functools.partial(attend_kernel, turn, rows),
-        in_specs=[SMEM_SPEC] * 2 + [VMEM_SPEC] * 4,
+        in_specs=[SMEM_SPEC] * 2 + [VMEM_SPEC] * 5,
         out_specs=[VMEM_SPEC] * 4,
         out_shape=[
-            block,
-            block,
+            square,
+            square,
             jax.ShapeDtypeStruct(far.shape, jnp.bfloat16),
             jax.ShapeDtypeStruct(own.shape, jnp.float32),
         ],
-        cost_estimate=cost(12 * rows * HEADS_PER_KEY * span * HEAD_WIDTH, 8 * rows * width),
+        cost_estimate=cost(8 * pairs * HEAD_WIDTH, 8 * pairs),
         compiler_params=pltpu.CompilerParams(vmem_limit_bytes=VMEM_LIMIT),
-    )(pos, path, queries, grad_rows, far, own)
+    )(pos, path, mask, queries, grad_out, far, own)
+
+
+def output(weights, grad_score, far, own):
+    rows = own.shape[1]
+    block = jax.ShapeDtypeStruct((rows, HEADS_PER_KEY * HEAD_WIDTH), jnp.bfloat16)
+    return pl.pallas_call(
+        functools.partial(output_kernel, rows),
+        in_specs=[VMEM_SPEC] * 4,
+        out_specs=[VMEM_SPEC] * 2,
+        out_shape=[block, block],
+        cost_estimate=cost(4 * weights.size * HEAD_WIDTH, 4 * weights.size),
+        compiler_params=pltpu.CompilerParams(vmem_limit_bytes=VMEM_LIMIT),
+    )(weights, grad_score, far, own)
 
 
 def store_kernel(pos_ref, *refs):
@@ -207,14 +215,14 @@
             out[:, cols] = total.astype(jnp.bfloat16)
 
 
-def small_call(kernel, in_specs, out_specs, out_shape, moved, scratch=()):
+def small_call(kernel, in_specs, out_specs, out_shape, moved, scratch=(), flops=0):
     return pl.pallas_call(
         kernel,
         in_specs=in_specs,
         out_specs=out_specs,
         out_shape=out_shape,
         scratch_shapes=list(scratch),
-        cost_estimate=cost(2 * moved, moved),
+        cost_estimate=cost(flops or 2 * moved, moved),
         compiler_params=pltpu.CompilerParams(vmem_limit_bytes=VMEM_LIMIT),
     )
 
@@ -256,28 +264,24 @@
     packed = small_call(
         pack_kernel, [SMEM_SPEC, HBM_SPEC, HBM_SPEC], [VMEM_SPEC] * GROUP,
         [piece] * GROUP, 8 * piece_bytes, [pltpu.SemaphoreType.DMA((2 * GROUP,))],
-    )(pos, keys, values)
+    )(pos, *(pltpu.with_memory_space_constraint(x, pltpu.HBM) for x in (keys, values)))
     far_pieces = far_sends(packed, 1)
     pieces = near_sends(packed) + far_pieces
-
-    staged, grad_rows = small_call(
-        stage_kernel, [VMEM_SPEC, HBM_SPEC, HBM_SPEC], [VMEM_SPEC] * 2, [wide] * 2,
-        32 * piece_bytes, [pltpu.SemaphoreType.DMA((2,))],
-    )(mask, queries, grad_out)
 
     picked = small_call(
         functools.partial(select_kernel, size),
         [SMEM_SPEC, SMEM_SPEC] + [VMEM_SPEC] * size, [VMEM_SPEC] * GROUP, [chosen] * GROUP,
         (size + 12) * piece_bytes, [pltpu.VMEM((size,) + piece.shape, jnp.bfloat16)],
+        COVER_FLOPS,
     )(pos, block_path, *pieces)
     far = near_sends(picked)
 
     blocks, far_grads, own_grads = [], [], []
     for t in range(GROUP):
-        attended, grad_query, far_grad, own_grad = attend(
-            t, pos, block_path, staged, grad_rows, far[t], packed[-t % GROUP]
+        weights, grad_score, far_grad, own_grad = attend(
+            t, pos, block_path, mask, queries, grad_out, far[t], packed[-t % GROUP]
         )
-        blocks += [attended, grad_query]
+        blocks += output(weights, grad_score, far[t], packed[-t % GROUP])
         far_grads.append(far_grad)
         own_grads.append(own_grad)
     far_grads = near_sends(far_grads, -1)

time: 68.9 us -> 68.1 us (0.988)
  local copies, waits for them, and re-layouts: 4.42 us -> 0.18 us
  Pallas kernels: 15.5 us -> 17.9 us
  waiting for transfers between devices: 14.6 us -> 15.5 us
    unnamed x13 -> x9, local copies, waits for them, and re-layouts: 4.34 us -> 0.1 us
    pallas_call x1 -> x4, Pallas kernels: 0.41 us -> 2.34 us  [output(): pl.pallas_call(functools.partial(output_kernel, rows), in_specs=[VMEM_SPE...]
    ppermute x20, waiting for transfers between devices: 14.6 us -> 15.5 us  [send(): return lax.ppermute(x, 'ctx', pairs)]
    pallas_call x1, Pallas kernels: 0.14 us -> 0.95 us  [on_device(): small_call(pack_kernel, [SMEM_SPEC, HBM_SPEC, HBM_SPEC], [VMEM_SPEC] * GR...]
  transfers between devices with their start and end apart: 20 -> 20, of which waited for: 8 -> 7; matrix products, arithmetic and copies ran while one was open for 0% -> 0% of each run, Pallas kernels for 19% -> 22%
where the time goes in v1:
time: 68.1 us; the launch traced here: 67.7 us
  starting transfers between devices  33.2 us (49%)
  Pallas kernels  17.9 us (26%)
  waiting for transfers between devices  15.5 us (23%)
  between operations  0.9 us (1%)
    ppermute x20, starting transfers between devices, send(): return lax.ppermute(x, 'ctx', pairs)  33.2 us
    ppermute x20, waiting for transfers between devices, send(): return lax.ppermute(x, 'ctx', pairs)  15.5 us
    pallas_call x4, Pallas kernels, attend(): pl.pallas_call(functools.partial(attend_kernel, turn, rows), in_specs=[SM...  10.8 us
    pallas_call x4, Pallas kernels, output(): pl.pallas_call(functools.partial(output_kernel, rows), in_specs=[VMEM_SPE...  2.34 us
    pallas_call x1, Pallas kernels, on_device(): small_call(store_kernel, [SMEM_SPEC] + [VMEM_SPEC] * (2 * GROUP), [HBM_SP...  1.39 us
  transfers between devices with their start and end apart: 20, of which 7 were waited for; matrix products, arithmetic and copies ran while one was open for 0% of the time, Pallas kernels for 22%

profile of v1, /device:TPU:0, one launch (start us, length us, event | category | flops | bytes accessed | tf_op | source)
XLA Modules:
  0.0 67.7 jit_solution(930020037507801671)
XLA Ops:
  1.6 6.0 %collective-permute-start.3 = (bf16[2,128,128]{2,1,0:T(8,128)(2,1)S(1)}, bf16[2,128,128]{2,1,0:T(8,128)(2,1)S(1)}, u32[]{:S(2)}, u32[]{:S(2)}) collective-permute-start(bf16[2,128,128]{2,1,0:T(8,128)(2,1)S(1)} %get-tuple-element.48.refs_0_.refs_6_.refs_3_), channel_id=1, source_target_pairs={{0,4},{1,5},{2,6},{3,7},{8,12},{9,13},{10,14},{11,15},{16,20},{17,... | collective-permute-start | bytes 196616 | tf_op jit(solution)/shard_map/ppermute | solution.py:252
  7.6 2.2 %collective-permute-start.4 = (bf16[2,128,128]{2,1,0:T(8,128)(2,1)S(1)}, bf16[2,128,128]{2,1,0:T(8,128)(2,1)S(1)}, u32[]{:S(2)}, u32[]{:S(2)}) collective-permute-start(bf16[2,128,128]{2,1,0:T(8,128)(2,1)S(1)} %get-tuple-element.49.refs_6_.refs_3_), channel_id=1, source_target_pairs={{0,5},{1,6},{2,7},{3,4},{8,13},{9,14},{10,15},{11,12},{16,21},{17,... | collective-permute-start | bytes 196616 | tf_op jit(solution)/shard_map/ppermute | solution.py:252
  9.8 1.6 %collective-permute-start = (bf16[2,128,128]{2,1,0:T(8,128)(2,1)S(1)}, bf16[2,128,128]{2,1,0:T(8,128)(2,1)S(1)}, u32[]{:S(2)}, u32[]{:S(2)}) collective-permute-start(bf16[2,128,128]{2,1,0:T(8,128)(2,1)S(1)} %get-tuple-element.49.refs_6_.refs_3_), channel_id=1, source_target_pairs={{0,1},{1,2},{2,3},{3,0},{4,5},{5,6},{6,7},{7,4},{8,9},{9,10},{10,1... | collective-permute-start | bytes 196616 | tf_op jit(solution)/shard_map/ppermute | solution.py:252
  11.4 1.3 %collective-permute-start.5 = (bf16[2,128,128]{2,1,0:T(8,128)(2,1)S(1)}, bf16[2,128,128]{2,1,0:T(8,128)(2,1)S(1)}, u32[]{:S(2)}, u32[]{:S(2)}) collective-permute-start(bf16[2,128,128]{2,1,0:T(8,128)(2,1)S(1)} %get-tuple-element.50.refs_6_.refs_3_), channel_id=1, source_target_pairs={{0,6},{1,7},{2,4},{3,5},{8,14},{9,15},{10,12},{11,13},{16,22},{17,... | collective-permute-start | bytes 196616 | tf_op jit(solution)/shard_map/ppermute | solution.py:252
  13.4 5.9 %collective-permute-start.6 = (bf16[2,128,128]{2,1,0:T(8,128)(2,1)S(1)}, bf16[2,128,128]{2,1,0:T(8,128)(2,1)S(1)}, u32[]{:S(2)}, u32[]{:S(2)}) collective-permute-start(bf16[2,128,128]{2,1,0:T(8,128)(2,1)S(1)} %get-tuple-element.51.refs_6_.refs_3_), channel_id=1, source_target_pairs={{0,7},{1,4},{2,5},{3,6},{8,15},{9,12},{10,13},{11,14},{16,23},{17,... | collective-permute-start | bytes 196616 | tf_op jit(solution)/shard_map/ppermute | solution.py:252
  20.1 1.2 %collective-permute-done.6.refs_7_ = bf16[2,128,128]{2,1,0:T(8,128)(2,1)S(1)} collective-permute-done((bf16[2,128,128]{2,1,0:T(8,128)(2,1)S(1)}, bf16[2,128,128]{2,1,0:T(8,128)(2,1)S(1)}, u32[]{:S(2)}, u32[]{:S(2)}) %collective-permute-start.6) | collective-permute-done | bytes 65568 | tf_op jit(solution)/shard_map/ppermute | solution.py:252
  21.2 2.4 %collective-permute-done.2.refs_3_ = bf16[2,128,128]{2,1,0:T(8,128)(2,1)S(1)} collective-permute-done((bf16[2,128,128]{2,1,0:T(8,128)(2,1)S(1)}, bf16[2,128,128]{2,1,0:T(8,128)(2,1)S(1)}, u32[]{:S(2)}, u32[]{:S(2)}) %collective-permute-start.2) | collective-permute-done | bytes 65568 | tf_op jit(solution)/shard_map/ppermute | solution.py:252
  24.4 1.6 %collective-permute-start.9 = (bf16[3,2,128,128]{3,2,1,0:T(8,128)(2,1)S(1)}, bf16[3,2,128,128]{3,2,1,0:T(8,128)(2,1)S(1)}, u32[]{:S(2)}, u32[]{:S(2)}) collective-permute-start(bf16[3,2,128,128]{3,2,1,0:T(8,128)(2,1)S(1)} %get-tuple-element.67), channel_id=1, source_target_pairs={{0,3},{1,0},{2,1},{3,2},{4,7},{5,4},{6,5},{7,6},{8,11},{9,8},{10,9... | collective-permute-start | bytes 589832 | tf_op jit(solution)/shard_map/ppermute | solution.py:252
  26.6 5.0 %collective-permute-done.9.refs_5_.refs_2_ = bf16[3,2,128,128]{3,2,1,0:T(8,128)(2,1)S(1)} collective-permute-done((bf16[3,2,128,128]{3,2,1,0:T(8,128)(2,1)S(1)}, bf16[3,2,128,128]{3,2,1,0:T(8,128)(2,1)S(1)}, u32[]{:S(2)}, u32[]{:S(2)}) %collective-permute-start.9) | collective-permute-done | bytes 196640 | tf_op jit(solution)/shard_map/ppermute | solution.py:252
  31.8 2.7 %shard_map.101 = (bf16[512,1024]{1,0:T(8,128)(2,1)S(1)}, bf16[512,1024]{1,0:T(8,128)(2,1)S(1)}, bf16[3,2,128,128]{3,2,1,0:T(8,128)(2,1)S(1)}, f32[2,128,128]{2,1,0:T(8,128)S(1)}) custom-call(s32[1]{0:T(128)} %bitcast.pos_ref.refs_0_, s32[8,4]{1,0:T(8,128)S(1)} %copy.11.path_ref.refs_1_, bf16[128,128]{1,0:T(8,128)(2,1)S(1)} %broadcast_in_dim.2.refs_2_, ...), custom_call_target="tpu_custom_call" | custom-call | flops 536870912 | bytes 4194304 | tf_op jit(solution)/shard_map/pallas_call | solution.py:141
  34.5 2.7 %shard_map.99 = (bf16[512,1024]{1,0:T(8,128)(2,1)S(1)}, bf16[512,1024]{1,0:T(8,128)(2,1)S(1)}, bf16[3,2,128,128]{3,2,1,0:T(8,128)(2,1)S(1)}, f32[2,128,128]{2,1,0:T(8,128)S(1)}) custom-call(s32[1]{0:T(128)} %bitcast.pos_ref.refs_0_, s32[8,4]{1,0:T(8,128)S(1)} %copy.11.path_ref.refs_1_, bf16[128,128]{1,0:T(8,128)(2,1)S(1)} %broadcast_in_dim.2.refs_2_, ...), custom_call_target="tpu_custom_call" | custom-call | flops 536870912 | bytes 4194304 | tf_op jit(solution)/shard_map/pallas_call | solution.py:141
  37.3 2.3 %collective-permute-start.11 = (bf16[3,2,128,128]{3,2,1,0:T(8,128)(2,1)S(1)}, bf16[3,2,128,128]{3,2,1,0:T(8,128)(2,1)S(1)}, u32[]{:S(2)}, u32[]{:S(2)}) collective-permute-start(bf16[3,2,128,128]{3,2,1,0:T(8,128)(2,1)S(1)} %get-tuple-element.80), channel_id=1, source_target_pairs={{0,2},{1,3},{2,0},{3,1},{4,6},{5,7},{6,4},{7,5},{8,10},{9,11},{10,... | collective-permute-start | bytes 589832 | tf_op jit(solution)/shard_map/ppermute | solution.py:252
  39.5 2.7 %shard_map.97 = (bf16[512,1024]{1,0:T(8,128)(2,1)S(1)}, bf16[512,1024]{1,0:T(8,128)(2,1)S(1)}, bf16[3,2,128,128]{3,2,1,0:T(8,128)(2,1)S(1)}, f32[2,128,128]{2,1,0:T(8,128)S(1)}) custom-call(s32[1]{0:T(128)} %bitcast.pos_ref.refs_0_, s32[8,4]{1,0:T(8,128)S(1)} %copy.11.path_ref.refs_1_, bf16[128,128]{1,0:T(8,128)(2,1)S(1)} %broadcast_in_dim.2.refs_2_, ...), custom_call_target="tpu_custom_call" | custom-call | flops 536870912 | bytes 4194304 | tf_op jit(solution)/shard_map/pallas_call | solution.py:141
  42.2 1.4 %collective-permute-start.10 = (bf16[3,2,128,128]{3,2,1,0:T(8,128)(2,1)S(1)}, bf16[3,2,128,128]{3,2,1,0:T(8,128)(2,1)S(1)}, u32[]{:S(2)}, u32[]{:S(2)}) collective-permute-start(bf16[3,2,128,128]{3,2,1,0:T(8,128)(2,1)S(1)} %get-tuple-element.79), channel_id=1, source_target_pairs={{0,3},{1,0},{2,1},{3,2},{4,7},{5,4},{6,5},{7,6},{8,11},{9,8},{10,9... | collective-permute-start | bytes 589832 | tf_op jit(solution)/shard_map/ppermute | solution.py:252
  43.6 2.7 %shard_map.95 = (bf16[512,1024]{1,0:T(8,128)(2,1)S(1)}, bf16[512,1024]{1,0:T(8,128)(2,1)S(1)}, bf16[3,2,128,128]{3,2,1,0:T(8,128)(2,1)S(1)}, f32[2,128,128]{2,1,0:T(8,128)S(1)}) custom-call(s32[1]{0:T(128)} %bitcast.pos_ref.refs_0_, s32[8,4]{1,0:T(8,128)S(1)} %copy.11.path_ref.refs_1_, bf16[128,128]{1,0:T(8,128)(2,1)S(1)} %broadcast_in_dim.2.refs_2_, ...), custom_call_target="tpu_custom_call" | custom-call | flops 536870912 | bytes 4194304 | tf_op jit(solution)/shard_map/pallas_call | solution.py:141
  46.3 2.3 %collective-permute-done.10.refs_1_ = bf16[3,2,128,128]{3,2,1,0:T(8,128)(2,1)S(1)} collective-permute-done((bf16[3,2,128,128]{3,2,1,0:T(8,128)(2,1)S(1)}, bf16[3,2,128,128]{3,2,1,0:T(8,128)(2,1)S(1)}, u32[]{:S(2)}, u32[]{:S(2)}) %collective-permute-start.10) | collective-permute-done | bytes 196640 | tf_op jit(solution)/shard_map/ppermute | solution.py:252
  49.5 2.2 %collective-permute-start.13 = (bf16[2,128,128]{2,1,0:T(8,128)(2,1)S(1)}, bf16[2,128,128]{2,1,0:T(8,128)(2,1)S(1)}, u32[]{:S(2)}, u32[]{:S(2)}) collective-permute-start(bf16[2,128,128]{2,1,0:T(8,128)(2,1)S(1)} %get-tuple-element.83), channel_id=1, source_target_pairs={{0,1},{1,2},{2,3},{3,0},{4,5},{5,6},{6,7},{7,4},{8,9},{9,10},{10,1... | collective-permute-start | bytes 196616 | tf_op jit(solution)/shard_map/ppermute | solution.py:252
  54.0 1.3 %collective-permute-start.16 = (bf16[2,128,128]{2,1,0:T(8,128)(2,1)S(1)}, bf16[2,128,128]{2,1,0:T(8,128)(2,1)S(1)}, u32[]{:S(2)}, u32[]{:S(2)}) collective-permute-start(bf16[2,128,128]{2,1,0:T(8,128)(2,1)S(1)} %get-tuple-element.86), channel_id=1, source_target_pairs={{4,0},{5,1},{6,2},{7,3},{12,8},{13,9},{14,10},{15,11},{20,16},{21,... | collective-permute-start | bytes 196616 | tf_op jit(solution)/shard_map/ppermute | solution.py:252
  55.2 1.3 %collective-permute-start.17 = (bf16[2,128,128]{2,1,0:T(8,128)(2,1)S(1)}, bf16[2,128,128]{2,1,0:T(8,128)(2,1)S(1)}, u32[]{:S(2)}, u32[]{:S(2)}) collective-permute-start(bf16[2,128,128]{2,1,0:T(8,128)(2,1)S(1)} %get-tuple-element.87), channel_id=1, source_target_pairs={{4,1},{5,2},{6,3},{7,0},{12,9},{13,10},{14,11},{15,8},{20,17},{21,... | collective-permute-start | bytes 196616 | tf_op jit(solution)/shard_map/ppermute | solution.py:252
  56.6 1.3 %collective-permute-start.18 = (bf16[2,128,128]{2,1,0:T(8,128)(2,1)S(1)}, bf16[2,128,128]{2,1,0:T(8,128)(2,1)S(1)}, u32[]{:S(2)}, u32[]{:S(2)}) collective-permute-start(bf16[2,128,128]{2,1,0:T(8,128)(2,1)S(1)} %get-tuple-element.88), channel_id=1, source_target_pairs={{4,2},{5,3},{6,0},{7,1},{12,10},{13,11},{14,8},{15,9},{20,18},{21,... | collective-permute-start | bytes 196616 | tf_op jit(solution)/shard_map/ppermute | solution.py:252
  57.9 1.3 %collective-permute-start.19 = (bf16[2,128,128]{2,1,0:T(8,128)(2,1)S(1)}, bf16[2,128,128]{2,1,0:T(8,128)(2,1)S(1)}, u32[]{:S(2)}, u32[]{:S(2)}) collective-permute-start(bf16[2,128,128]{2,1,0:T(8,128)(2,1)S(1)} %get-tuple-element.89), channel_id=1, source_target_pairs={{4,3},{5,0},{6,1},{7,2},{12,11},{13,8},{14,9},{15,10},{20,19},{21,... | collective-permute-start | bytes 196616 | tf_op jit(solution)/shard_map/ppermute | solution.py:252
  60.9 1.4 %shard_map.103 = (bf16[128,4096]{1,0:T(8,128)(2,1)}, bf16[128,4096]{1,0:T(8,128)(2,1)}) custom-call(s32[1]{0:T(128)} %bitcast.pos_ref.refs_0_, bf16[128,1024]{1,0:T(8,128)(2,1)S(1)} %get-tuple-element.55.refs_0_, bf16[128,1024]{1,0:T(8,128)(2,1)S(1)} %get-tuple-element.56.refs_1_, bf16[128,1024]{1,0:T(8,128)(2,1)S(1)} %get-tuple-element.60.refs_2_, ...), custom_call_target="tpu_custom_call" | custom-call | flops 4194304 | bytes 2097152 | tf_op jit(solution)/shard_map/pallas_call | solution.py:289
  62.4 1.8 %collective-permute-done.17.refs_9_ = bf16[2,128,128]{2,1,0:T(8,128)(2,1)S(1)} collective-permute-done((bf16[2,128,128]{2,1,0:T(8,128)(2,1)S(1)}, bf16[2,128,128]{2,1,0:T(8,128)(2,1)S(1)}, u32[]{:S(2)}, u32[]{:S(2)}) %collective-permute-start.17) | collective-permute-done | bytes 65568 | tf_op jit(solution)/shard_map/ppermute | solution.py:252
  65.1 1.8 %collective-permute-done.19.refs_11_ = bf16[2,128,128]{2,1,0:T(8,128)(2,1)S(1)} collective-permute-done((bf16[2,128,128]{2,1,0:T(8,128)(2,1)S(1)}, bf16[2,128,128]{2,1,0:T(8,128)(2,1)S(1)}, u32[]{:S(2)}, u32[]{:S(2)}) %collective-permute-start.19) | collective-permute-done | bytes 65568 | tf_op jit(solution)/shard_map/ppermute | solution.py:252
  (40 shorter events, 10.4 us)
Async XLA Ops:
  1.6 11.8 %collective-permute-start.3 = (bf16[2,128,128]{2,1,0:T(8,128)(2,1)S(1)}, bf16[2,128,128]{2,1,0:T(8,128)(2,1)S(1)}, u32[]{:S(2)}, u32[]{:S(2)}) collective-permute-start(bf16[2,128,128]{2,1,0:T(8,128)(2,1)S(1)} %get-tuple-element.48.refs_0_.refs_6_.refs_3_), channel_id=1, source_target_pairs={{0,4},{1,5},{2,6},{3,7},{8,12},{9,13},{10,14},{11,15},{16,20},{17,... | collective-permute-start | bytes 196616 | tf_op jit(solution)/shard_map/ppermute | solution.py:252
  7.6 12.4 %copy-start.2 = (s32[8,4]{0,1:T(4,128)S(1)}, s32[8,4]{0,1:T(4,128)}, u32[]{:S(2)}) copy-start(s32[8,4]{0,1:T(4,128)} %param.10) | copy-start | bytes 388
  7.6 11.7 %collective-permute-start.4 = (bf16[2,128,128]{2,1,0:T(8,128)(2,1)S(1)}, bf16[2,128,128]{2,1,0:T(8,128)(2,1)S(1)}, u32[]{:S(2)}, u32[]{:S(2)}) collective-permute-start(bf16[2,128,128]{2,1,0:T(8,128)(2,1)S(1)} %get-tuple-element.49.refs_6_.refs_3_), channel_id=1, source_target_pairs={{0,5},{1,6},{2,7},{3,4},{8,13},{9,14},{10,15},{11,12},{16,21},{17,... | collective-permute-start | bytes 196616 | tf_op jit(solution)/shard_map/ppermute | solution.py:252
  9.8 10.2 %collective-permute-start = (bf16[2,128,128]{2,1,0:T(8,128)(2,1)S(1)}, bf16[2,128,128]{2,1,0:T(8,128)(2,1)S(1)}, u32[]{:S(2)}, u32[]{:S(2)}) collective-permute-start(bf16[2,128,128]{2,1,0:T(8,128)(2,1)S(1)} %get-tuple-element.49.refs_6_.refs_3_), channel_id=1, source_target_pairs={{0,1},{1,2},{2,3},{3,0},{4,5},{5,6},{6,7},{7,4},{8,9},{9,10},{10,1... | collective-permute-start | bytes 196616 | tf_op jit(solution)/shard_map/ppermute | solution.py:252
  11.4 8.6 %collective-permute-start.5 = (bf16[2,128,128]{2,1,0:T(8,128)(2,1)S(1)}, bf16[2,128,128]{2,1,0:T(8,128)(2,1)S(1)}, u32[]{:S(2)}, u32[]{:S(2)}) collective-permute-start(bf16[2,128,128]{2,1,0:T(8,128)(2,1)S(1)} %get-tuple-element.50.refs_6_.refs_3_), channel_id=1, source_target_pairs={{0,6},{1,7},{2,4},{3,5},{8,14},{9,15},{10,12},{11,13},{16,22},{17,... | collective-permute-start | bytes 196616 | tf_op jit(solution)/shard_map/ppermute | solution.py:252
  12.8 7.3 %collective-permute-start.1 = (bf16[2,128,128]{2,1,0:T(8,128)(2,1)S(1)}, bf16[2,128,128]{2,1,0:T(8,128)(2,1)S(1)}, u32[]{:S(2)}, u32[]{:S(2)}) collective-permute-start(bf16[2,128,128]{2,1,0:T(8,128)(2,1)S(1)} %get-tuple-element.50.refs_6_.refs_3_), channel_id=1, source_target_pairs={{0,2},{1,3},{2,0},{3,1},{4,6},{5,7},{6,4},{7,5},{8,10},{9,11},{10,... | collective-permute-start | bytes 196616 | tf_op jit(solution)/shard_map/ppermute | solution.py:252
  13.4 7.8 %collective-permute-start.6 = (bf16[2,128,128]{2,1,0:T(8,128)(2,1)S(1)}, bf16[2,128,128]{2,1,0:T(8,128)(2,1)S(1)}, u32[]{:S(2)}, u32[]{:S(2)}) collective-permute-start(bf16[2,128,128]{2,1,0:T(8,128)(2,1)S(1)} %get-tuple-element.51.refs_6_.refs_3_), channel_id=1, source_target_pairs={{0,7},{1,4},{2,5},{3,6},{8,15},{9,12},{10,13},{11,14},{16,23},{17,... | collective-permute-start | bytes 196616 | tf_op jit(solution)/shard_map/ppermute | solution.py:252
  19.3 4.3 %collective-permute-start.2 = (bf16[2,128,128]{2,1,0:T(8,128)(2,1)S(1)}, bf16[2,128,128]{2,1,0:T(8,128)(2,1)S(1)}, u32[]{:S(2)}, u32[]{:S(2)}) collective-permute-start(bf16[2,128,128]{2,1,0:T(8,128)(2,1)S(1)} %get-tuple-element.51.refs_6_.refs_3_), channel_id=1, source_target_pairs={{0,3},{1,0},{2,1},{3,2},{4,7},{5,4},{6,5},{7,6},{8,11},{9,8},{10,9... | collective-permute-start | bytes 196616 | tf_op jit(solution)/shard_map/ppermute | solution.py:252
  20.0 11.7 %copy-start = (bf16[128,4096]{1,0:T(8,128)(2,1)S(1)}, bf16[128,4096]{1,0:T(8,128)(2,1)}, u32[]{:S(2)}) copy-start(bf16[128,4096]{1,0:T(8,128)(2,1)} %refs_3_.7) | copy-start | bytes 3145732
  20.0 11.7 %copy-start.1 = (bf16[128,4096]{1,0:T(8,128)(2,1)S(1)}, bf16[128,4096]{1,0:T(8,128)(2,1)}, u32[]{:S(2)}) copy-start(bf16[128,4096]{1,0:T(8,128)(2,1)} %refs_4_.7) | copy-start | bytes 3145732
  24.4 7.3 %collective-permute-start.9 = (bf16[3,2,128,128]{3,2,1,0:T(8,128)(2,1)S(1)}, bf16[3,2,128,128]{3,2,1,0:T(8,128)(2,1)S(1)}, u32[]{:S(2)}, u32[]{:S(2)}) collective-permute-start(bf16[3,2,128,128]{3,2,1,0:T(8,128)(2,1)S(1)} %get-tuple-element.67), channel_id=1, source_target_pairs={{0,3},{1,0},{2,1},{3,2},{4,7},{5,4},{6,5},{7,6},{8,11},{9,8},{10,9... | collective-permute-start | bytes 589832 | tf_op jit(solution)/shard_map/ppermute | solution.py:252
  25.9 0.7 copy-start.3
  25.9 8.6 %collective-permute-start.8 = (bf16[3,2,128,128]{3,2,1,0:T(8,128)(2,1)S(1)}, bf16[3,2,128,128]{3,2,1,0:T(8,128)(2,1)S(1)}, u32[]{:S(2)}, u32[]{:S(2)}) collective-permute-start(bf16[3,2,128,128]{3,2,1,0:T(8,128)(2,1)S(1)} %get-tuple-element.62), channel_id=1, source_target_pairs={{0,2},{1,3},{2,0},{3,1},{4,6},{5,7},{6,4},{7,5},{8,10},{9,11},{10,... | collective-permute-start | bytes 589832 | tf_op jit(solution)/shard_map/ppermute | solution.py:252
  25.9 13.6 %collective-permute-start.7 = (bf16[3,2,128,128]{3,2,1,0:T(8,128)(2,1)S(1)}, bf16[3,2,128,128]{3,2,1,0:T(8,128)(2,1)S(1)}, u32[]{:S(2)}, u32[]{:S(2)}) collective-permute-start(bf16[3,2,128,128]{3,2,1,0:T(8,128)(2,1)S(1)} %get-tuple-element.57), channel_id=1, source_target_pairs={{0,1},{1,2},{2,3},{3,0},{4,5},{5,6},{6,7},{7,4},{8,9},{9,10},{10,1... | collective-permute-start | bytes 589832 | tf_op jit(solution)/shard_map/ppermute | solution.py:252
  34.5 11.9 %collective-permute-start.12 = (bf16[3,2,128,128]{3,2,1,0:T(8,128)(2,1)S(1)}, bf16[3,2,128,128]{3,2,1,0:T(8,128)(2,1)S(1)}, u32[]{:S(2)}, u32[]{:S(2)}) collective-permute-start(bf16[3,2,128,128]{3,2,1,0:T(8,128)(2,1)S(1)} %get-tuple-element.81), channel_id=1, source_target_pairs={{0,1},{1,2},{2,3},{3,0},{4,5},{5,6},{6,7},{7,4},{8,9},{9,10},{10,1... | collective-permute-start | bytes 589832 | tf_op jit(solution)/shard_map/ppermute | solution.py:252
  37.3 9.1 %collective-permute-start.11 = (bf16[3,2,128,128]{3,2,1,0:T(8,128)(2,1)S(1)}, bf16[3,2,128,128]{3,2,1,0:T(8,128)(2,1)S(1)}, u32[]{:S(2)}, u32[]{:S(2)}) collective-permute-start(bf16[3,2,128,128]{3,2,1,0:T(8,128)(2,1)S(1)} %get-tuple-element.80), channel_id=1, source_target_pairs={{0,2},{1,3},{2,0},{3,1},{4,6},{5,7},{6,4},{7,5},{8,10},{9,11},{10,... | collective-permute-start | bytes 589832 | tf_op jit(solution)/shard_map/ppermute | solution.py:252
  42.2 6.4 %collective-permute-start.10 = (bf16[3,2,128,128]{3,2,1,0:T(8,128)(2,1)S(1)}, bf16[3,2,128,128]{3,2,1,0:T(8,128)(2,1)S(1)}, u32[]{:S(2)}, u32[]{:S(2)}) collective-permute-start(bf16[3,2,128,128]{3,2,1,0:T(8,128)(2,1)S(1)} %get-tuple-element.79), channel_id=1, source_target_pairs={{0,3},{1,0},{2,1},{3,2},{4,7},{5,4},{6,5},{7,6},{8,11},{9,8},{10,9... | collective-permute-start | bytes 589832 | tf_op jit(solution)/shard_map/ppermute | solution.py:252
  49.5 7.0 %collective-permute-start.13 = (bf16[2,128,128]{2,1,0:T(8,128)(2,1)S(1)}, bf16[2,128,128]{2,1,0:T(8,128)(2,1)S(1)}, u32[]{:S(2)}, u32[]{:S(2)}) collective-permute-start(bf16[2,128,128]{2,1,0:T(8,128)(2,1)S(1)} %get-tuple-element.83), channel_id=1, source_target_pairs={{0,1},{1,2},{2,3},{3,0},{4,5},{5,6},{6,7},{7,4},{8,9},{9,10},{10,1... | collective-permute-start | bytes 196616 | tf_op jit(solution)/shard_map/ppermute | solution.py:252
  51.8 6.1 %collective-permute-start.14 = (bf16[2,128,128]{2,1,0:T(8,128)(2,1)S(1)}, bf16[2,128,128]{2,1,0:T(8,128)(2,1)S(1)}, u32[]{:S(2)}, u32[]{:S(2)}) collective-permute-start(bf16[2,128,128]{2,1,0:T(8,128)(2,1)S(1)} %get-tuple-element.84), channel_id=1, source_target_pairs={{0,2},{1,3},{2,0},{3,1},{4,6},{5,7},{6,4},{7,5},{8,10},{9,11},{10,... | collective-permute-start | bytes 196616 | tf_op jit(solution)/shard_map/ppermute | solution.py:252
  53.0 9.4 %collective-permute-start.15 = (bf16[2,128,128]{2,1,0:T(8,128)(2,1)S(1)}, bf16[2,128,128]{2,1,0:T(8,128)(2,1)S(1)}, u32[]{:S(2)}, u32[]{:S(2)}) collective-permute-start(bf16[2,128,128]{2,1,0:T(8,128)(2,1)S(1)} %get-tuple-element.85), channel_id=1, source_target_pairs={{0,3},{1,0},{2,1},{3,2},{4,7},{5,4},{6,5},{7,6},{8,11},{9,8},{10,9... | collective-permute-start | bytes 196616 | tf_op jit(solution)/shard_map/ppermute | solution.py:252
  54.0 8.4 %collective-permute-start.16 = (bf16[2,128,128]{2,1,0:T(8,128)(2,1)S(1)}, bf16[2,128,128]{2,1,0:T(8,128)(2,1)S(1)}, u32[]{:S(2)}, u32[]{:S(2)}) collective-permute-start(bf16[2,128,128]{2,1,0:T(8,128)(2,1)S(1)} %get-tuple-element.86), channel_id=1, source_target_pairs={{4,0},{5,1},{6,2},{7,3},{12,8},{13,9},{14,10},{15,11},{20,16},{21,... | collective-permute-start | bytes 196616 | tf_op jit(solution)/shard_map/ppermute | solution.py:252
  55.2 8.9 %collective-permute-start.17 = (bf16[2,128,128]{2,1,0:T(8,128)(2,1)S(1)}, bf16[2,128,128]{2,1,0:T(8,128)(2,1)S(1)}, u32[]{:S(2)}, u32[]{:S(2)}) collective-permute-start(bf16[2,128,128]{2,1,0:T(8,128)(2,1)S(1)} %get-tuple-element.87), channel_id=1, source_target_pairs={{4,1},{5,2},{6,3},{7,0},{12,9},{13,10},{14,11},{15,8},{20,17},{21,... | collective-permute-start | bytes 196616 | tf_op jit(solution)/shard_map/ppermute | solution.py:252
  56.6 8.5 %collective-permute-start.18 = (bf16[2,128,128]{2,1,0:T(8,128)(2,1)S(1)}, bf16[2,128,128]{2,1,0:T(8,128)(2,1)S(1)}, u32[]{:S(2)}, u32[]{:S(2)}) collective-permute-start(bf16[2,128,128]{2,1,0:T(8,128)(2,1)S(1)} %get-tuple-element.88), channel_id=1, source_target_pairs={{4,2},{5,3},{6,0},{7,1},{12,10},{13,11},{14,8},{15,9},{20,18},{21,... | collective-permute-start | bytes 196616 | tf_op jit(solution)/shard_map/ppermute | solution.py:252
  57.9 9.0 %collective-permute-start.19 = (bf16[2,128,128]{2,1,0:T(8,128)(2,1)S(1)}, bf16[2,128,128]{2,1,0:T(8,128)(2,1)S(1)}, u32[]{:S(2)}, u32[]{:S(2)}) collective-permute-start(bf16[2,128,128]{2,1,0:T(8,128)(2,1)S(1)} %get-tuple-element.89), channel_id=1, source_target_pairs={{4,3},{5,0},{6,1},{7,2},{12,11},{13,8},{14,9},{15,10},{20,19},{21,... | collective-permute-start | bytes 196616 | tf_op jit(solution)/shard_map/ppermute | solution.py:252

commit v2 on v1

--- a/solution.py
+++ b/solution.py
@@ -37,10 +37,6 @@
     return jnp.concatenate([far_ref[e, part] for e in range(FAR_SLOTS)] + [own_ref[part]], 0)
 
 
-def wrap(x):
-    return lax.rem(x + 2 * GROUP, GROUP)
-
-
 def head_columns(head):
     return pl.ds(pl.multiple_of(head * HEAD_WIDTH, HEAD_WIDTH), HEAD_WIDTH)
 
@@ -54,7 +50,7 @@
     member = lax.rem(pos_ref[0], GROUP)
     copies = []
     for t in range(GROUP):
-        cols = head_columns(wrap(member + t))
+        cols = head_columns(member ^ t)
         for part, source in enumerate((k_ref, v_ref)):
             copies.append(
                 pltpu.make_async_copy(source.at[:, cols], outs[t].at[part], sem.at[2 * t + part])
@@ -72,12 +68,12 @@
     for i in range(count):
         held[i] = pieces[i][...]
     for t in range(GROUP):
-        block = group * GROUP + wrap(member + t)
+        block = group * GROUP + member ^ t
         for e in range(FAR_SLOTS):
             ancestor = path_ref[block, e]
             seen = path_ref[block, e + 1] >= 0
             above = group - lax.div(ancestor, GROUP)
-            index = above * GROUP + wrap(member - lax.rem(ancestor, GROUP))
+            index = above * GROUP + (member ^ lax.rem(ancestor, GROUP))
             outs[t][e] = held[jnp.where(seen, index, 0)]
 
 
@@ -85,7 +81,7 @@
     (pos_ref, path_ref, mask_ref, q_ref, go_ref, far_ref, own_ref) = refs[:7]
     weights_ref, grad_score_ref, far_grad_ref, own_grad_ref = refs[7:]
     position = pos_ref[0]
-    head = wrap(lax.rem(position, GROUP) - turn)
+    head = lax.rem(position, GROUP) ^ turn
     far_rows = FAR_SLOTS * rows
     mask = mask_ref[...]
     blocks = [head_columns(head * HEADS_PER_KEY + i) for i in range(HEADS_PER_KEY)]
@@ -172,7 +168,7 @@
     member = lax.rem(pos_ref[0], GROUP)
     copies = []
     for t in range(GROUP):
-        head = wrap(member - t)
+        head = member ^ t
         cols = pl.ds(pl.multiple_of(head * width, width), width)
         for part in range(2):
             i = 2 * t + part
@@ -189,11 +185,11 @@
     member, group = lax.rem(position, GROUP), lax.div(position, GROUP)
     acc[...] = jnp.zeros_like(acc)
     for t in range(GROUP):
-        block = group * GROUP + wrap(member + t)
+        block = group * GROUP + member ^ t
         for e in range(FAR_SLOTS):
             ancestor = path_ref[block, e]
             above = group - lax.div(ancestor, GROUP)
-            index = above * GROUP + wrap(lax.rem(ancestor, GROUP) - member)
+            index = above * GROUP + (member ^ lax.rem(ancestor, GROUP))
 
             @pl.when(path_ref[block, e + 1] >= 0)
             def _(t=t, e=e, index=index):
@@ -207,7 +203,7 @@
     own, pieces, gk_ref, gv_ref = refs[:GROUP], refs[GROUP:-2], refs[-2], refs[-1]
     member = lax.rem(pos_ref[0], GROUP)
     for t in range(GROUP):
-        cols = head_columns(wrap(member - t))
+        cols = head_columns(member ^ t)
         for part, out in enumerate((gk_ref, gv_ref)):
             total = own[t][part]
             for piece in pieces[t::GROUP]:
@@ -238,14 +234,14 @@
     piece_bytes = 4 * rows * HEAD_WIDTH
 
     def inside(shift):
-        return [(i, i - i % GROUP + (i + shift) % GROUP) for i in range(size)]
+        return [(i, i ^ shift) for i in range(size)]
 
     def across(up, shift):
         pairs = []
         for i in range(size):
             group = i // GROUP + up
             if 0 <= group < groups:
-                pairs.append((i, group * GROUP + (i + shift) % GROUP))
+                pairs.append((i, group * GROUP + (i % GROUP ^ shift)))
         return pairs
 
     def send(x, pairs):
@@ -258,8 +254,8 @@
             for t in range(GROUP)
         ]
 
-    def near_sends(parts, sign=1):
-        return [parts[0]] + [send(parts[t], inside(sign * t)) for t in range(1, GROUP)]
+    def near_sends(parts):
+        return [parts[0]] + [send(parts[t], inside(t)) for t in range(1, GROUP)]
 
     packed = small_call(
         pack_kernel, [SMEM_SPEC, HBM_SPEC, HBM_SPEC], [VMEM_SPEC] * GROUP,
@@ -279,12 +275,12 @@
     blocks, far_grads, own_grads = [], [], []
     for t in range(GROUP):
         weights, grad_score, far_grad, own_grad = attend(
-            t, pos, block_path, mask, queries, grad_out, far[t], packed[-t % GROUP]
+            t, pos, block_path, mask, queries, grad_out, far[t], packed[t]
         )
-        blocks += output(weights, grad_score, far[t], packed[-t % GROUP])
+        blocks += output(weights, grad_score, far[t], packed[t])
         far_grads.append(far_grad)
         own_grads.append(own_grad)
-    far_grads = near_sends(far_grads, -1)
+    far_grads = near_sends(far_grads)
 
     attention, grad_queries = small_call(
         store_kernel, [SMEM_SPEC] + [VMEM_SPEC] * (2 * GROUP), [HBM_SPEC] * 2,

time: 68.1 us -> 69 us (1.013)
  starting transfers between devices: 33.2 us -> 35 us
  waiting for transfers between devices: 15.5 us -> 14.7 us
    ppermute x20, starting transfers between devices: 33.2 us -> 35 us  [send(): return lax.ppermute(x, 'ctx', pairs)]
    ppermute x20, waiting for transfers between devices: 15.5 us -> 14.7 us  [send(): return lax.ppermute(x, 'ctx', pairs)]
  transfers between devices with their start and end apart: 20 -> 20, of which waited for: 7 -> 7; matrix products, arithmetic and copies ran while one was open for 0% -> 0% of each run, Pallas kernels for 22% -> 21%
where the time goes in v2:
time: 69 us; the launch traced here: 68.6 us
  starting transfers between devices  35 us (51%)
  Pallas kernels  17.9 us (26%)
  waiting for transfers between devices  14.7 us (21%)
  between operations  0.9 us (1%)
    ppermute x20, starting transfers between devices, send(): return lax.ppermute(x, 'ctx', pairs)  35 us
    ppermute x20, waiting for transfers between devices, send(): return lax.ppermute(x, 'ctx', pairs)  14.7 us
    pallas_call x4, Pallas kernels, attend(): pl.pallas_call(functools.partial(attend_kernel, turn, rows), in_specs=[SM...  10.8 us
    pallas_call x4, Pallas kernels, output(): pl.pallas_call(functools.partial(output_kernel, rows), in_specs=[VMEM_SPE...  2.34 us
    pallas_call x1, Pallas kernels, on_device(): small_call(store_kernel, [SMEM_SPEC] + [VMEM_SPEC] * (2 * GROUP), [HBM_SP...  1.38 us
  transfers between devices with their start and end apart: 20, of which 7 were waited for; matrix products, arithmetic and copies ran while one was open for 0% of the time, Pallas kernels for 21%

profile of v2, /device:TPU:0, one launch (start us, length us, event | category | flops | bytes accessed | tf_op | source)
XLA Modules:
  0.0 68.6 jit_solution(14877095872910944329)
XLA Ops:
  0.6 1.0 %shard_map.93 = (bf16[2,128,128]{2,1,0:T(8,128)(2,1)S(1)}, bf16[2,128,128]{2,1,0:T(8,128)(2,1)S(1)}, bf16[2,128,128]{2,1,0:T(8,128)(2,1)S(1)}, bf16[2,128,128]{2,1,0:T(8,128)(2,1)S(1)}) custom-call(s32[1]{0:T(128)} %bitcast.pos_ref.refs_0_, bf16[128,512]{1,0:T(8,128)(2,1)} %k_ref.1, bf16[128,512]{1,0:T(8,128)(2,1)} %v_ref.1), custom_call_target="tpu_custom_call" | custom-call | flops 1048576 | bytes 524288 | tf_op jit(solution)/shard_map/pallas_call | solution.py:260
  1.6 6.0 %collective-permute-start.3 = (bf16[2,128,128]{2,1,0:T(8,128)(2,1)S(1)}, bf16[2,128,128]{2,1,0:T(8,128)(2,1)S(1)}, u32[]{:S(2)}, u32[]{:S(2)}) collective-permute-start(bf16[2,128,128]{2,1,0:T(8,128)(2,1)S(1)} %get-tuple-element.48.refs_0_.refs_6_.refs_3_), channel_id=1, source_target_pairs={{0,4},{1,5},{2,6},{3,7},{8,12},{9,13},{10,14},{11,15},{16,20},{17,... | collective-permute-start | bytes 196616 | tf_op jit(solution)/shard_map/ppermute | solution.py:248
  7.6 2.2 %collective-permute-start.4 = (bf16[2,128,128]{2,1,0:T(8,128)(2,1)S(1)}, bf16[2,128,128]{2,1,0:T(8,128)(2,1)S(1)}, u32[]{:S(2)}, u32[]{:S(2)}) collective-permute-start(bf16[2,128,128]{2,1,0:T(8,128)(2,1)S(1)} %get-tuple-element.49.refs_6_.refs_3_), channel_id=1, source_target_pairs={{0,5},{1,4},{2,7},{3,6},{8,13},{9,12},{10,15},{11,14},{16,21},{17,... | collective-permute-start | bytes 196616 | tf_op jit(solution)/shard_map/ppermute | solution.py:248
  10.5 2.3 %collective-permute-start.5 = (bf16[2,128,128]{2,1,0:T(8,128)(2,1)S(1)}, bf16[2,128,128]{2,1,0:T(8,128)(2,1)S(1)}, u32[]{:S(2)}, u32[]{:S(2)}) collective-permute-start(bf16[2,128,128]{2,1,0:T(8,128)(2,1)S(1)} %get-tuple-element.50.refs_6_.refs_3_), channel_id=1, source_target_pairs={{0,6},{1,7},{2,4},{3,5},{8,14},{9,15},{10,12},{11,13},{16,22},{17,... | collective-permute-start | bytes 196616 | tf_op jit(solution)/shard_map/ppermute | solution.py:248
  13.4 6.7 %collective-permute-start.6 = (bf16[2,128,128]{2,1,0:T(8,128)(2,1)S(1)}, bf16[2,128,128]{2,1,0:T(8,128)(2,1)S(1)}, u32[]{:S(2)}, u32[]{:S(2)}) collective-permute-start(bf16[2,128,128]{2,1,0:T(8,128)(2,1)S(1)} %get-tuple-element.51.refs_6_.refs_3_), channel_id=1, source_target_pairs={{0,7},{1,6},{2,5},{3,4},{8,15},{9,14},{10,13},{11,12},{16,23},{17,... | collective-permute-start | bytes 196616 | tf_op jit(solution)/shard_map/ppermute | solution.py:248
  20.4 1.7 %collective-permute-done.6.refs_7_ = bf16[2,128,128]{2,1,0:T(8,128)(2,1)S(1)} collective-permute-done((bf16[2,128,128]{2,1,0:T(8,128)(2,1)S(1)}, bf16[2,128,128]{2,1,0:T(8,128)(2,1)S(1)}, u32[]{:S(2)}, u32[]{:S(2)}) %collective-permute-start.6) | collective-permute-done | bytes 65568 | tf_op jit(solution)/shard_map/ppermute | solution.py:248
  22.0 3.4 %collective-permute-done.2.refs_3_ = bf16[2,128,128]{2,1,0:T(8,128)(2,1)S(1)} collective-permute-done((bf16[2,128,128]{2,1,0:T(8,128)(2,1)S(1)}, bf16[2,128,128]{2,1,0:T(8,128)(2,1)S(1)}, u32[]{:S(2)}, u32[]{:S(2)}) %collective-permute-start.2) | collective-permute-done | bytes 65568 | tf_op jit(solution)/shard_map/ppermute | solution.py:248
  27.4 2.3 %collective-permute-start.7 = (bf16[3,2,128,128]{3,2,1,0:T(8,128)(2,1)S(1)}, bf16[3,2,128,128]{3,2,1,0:T(8,128)(2,1)S(1)}, u32[]{:S(2)}, u32[]{:S(2)}) collective-permute-start(bf16[3,2,128,128]{3,2,1,0:T(8,128)(2,1)S(1)} %get-tuple-element.57), channel_id=1, source_target_pairs={{0,1},{1,0},{2,3},{3,2},{4,5},{5,4},{6,7},{7,6},{8,9},{9,8},{10,11... | collective-permute-start | bytes 589832 | tf_op jit(solution)/shard_map/ppermute | solution.py:248
  29.7 3.4 %collective-permute-done.9.refs_5_.refs_2_ = bf16[3,2,128,128]{3,2,1,0:T(8,128)(2,1)S(1)} collective-permute-done((bf16[3,2,128,128]{3,2,1,0:T(8,128)(2,1)S(1)}, bf16[3,2,128,128]{3,2,1,0:T(8,128)(2,1)S(1)}, u32[]{:S(2)}, u32[]{:S(2)}) %collective-permute-start.9) | collective-permute-done | bytes 196640 | tf_op jit(solution)/shard_map/ppermute | solution.py:248
  33.2 2.7 %shard_map.101 = (bf16[512,1024]{1,0:T(8,128)(2,1)S(1)}, bf16[512,1024]{1,0:T(8,128)(2,1)S(1)}, bf16[3,2,128,128]{3,2,1,0:T(8,128)(2,1)S(1)}, f32[2,128,128]{2,1,0:T(8,128)S(1)}) custom-call(s32[1]{0:T(128)} %bitcast.pos_ref.refs_0_, s32[8,4]{1,0:T(8,128)S(1)} %copy.11.path_ref.refs_1_, bf16[128,128]{1,0:T(8,128)(2,1)S(1)} %broadcast_in_dim.2.refs_2_, ...), custom_call_target="tpu_custom_call" | custom-call | flops 536870912 | bytes 4194304 | tf_op jit(solution)/shard_map/pallas_call | solution.py:137
  36.8 2.7 %shard_map.99 = (bf16[512,1024]{1,0:T(8,128)(2,1)S(1)}, bf16[512,1024]{1,0:T(8,128)(2,1)S(1)}, bf16[3,2,128,128]{3,2,1,0:T(8,128)(2,1)S(1)}, f32[2,128,128]{2,1,0:T(8,128)S(1)}) custom-call(s32[1]{0:T(128)} %bitcast.pos_ref.refs_0_, s32[8,4]{1,0:T(8,128)S(1)} %copy.11.path_ref.refs_1_, bf16[128,128]{1,0:T(8,128)(2,1)S(1)} %broadcast_in_dim.2.refs_2_, ...), custom_call_target="tpu_custom_call" | custom-call | flops 536870912 | bytes 4194304 | tf_op jit(solution)/shard_map/pallas_call | solution.py:137
  39.9 2.7 %shard_map.97 = (bf16[512,1024]{1,0:T(8,128)(2,1)S(1)}, bf16[512,1024]{1,0:T(8,128)(2,1)S(1)}, bf16[3,2,128,128]{3,2,1,0:T(8,128)(2,1)S(1)}, f32[2,128,128]{2,1,0:T(8,128)S(1)}) custom-call(s32[1]{0:T(128)} %bitcast.pos_ref.refs_0_, s32[8,4]{1,0:T(8,128)S(1)} %copy.11.path_ref.refs_1_, bf16[128,128]{1,0:T(8,128)(2,1)S(1)} %broadcast_in_dim.2.refs_2_, ...), custom_call_target="tpu_custom_call" | custom-call | flops 536870912 | bytes 4194304 | tf_op jit(solution)/shard_map/pallas_call | solution.py:137
  42.7 2.3 %collective-permute-start.10 = (bf16[3,2,128,128]{3,2,1,0:T(8,128)(2,1)S(1)}, bf16[3,2,128,128]{3,2,1,0:T(8,128)(2,1)S(1)}, u32[]{:S(2)}, u32[]{:S(2)}) collective-permute-start(bf16[3,2,128,128]{3,2,1,0:T(8,128)(2,1)S(1)} %get-tuple-element.79), channel_id=1, source_target_pairs={{0,1},{1,0},{2,3},{3,2},{4,5},{5,4},{6,7},{7,6},{8,9},{9,8},{10,11... | collective-permute-start | bytes 589832 | tf_op jit(solution)/shard_map/ppermute | solution.py:248
  45.0 2.7 %shard_map.95 = (bf16[512,1024]{1,0:T(8,128)(2,1)S(1)}, bf16[512,1024]{1,0:T(8,128)(2,1)S(1)}, bf16[3,2,128,128]{3,2,1,0:T(8,128)(2,1)S(1)}, f32[2,128,128]{2,1,0:T(8,128)S(1)}) custom-call(s32[1]{0:T(128)} %bitcast.pos_ref.refs_0_, s32[8,4]{1,0:T(8,128)S(1)} %copy.11.path_ref.refs_1_, bf16[128,128]{1,0:T(8,128)(2,1)S(1)} %broadcast_in_dim.2.refs_2_, ...), custom_call_target="tpu_custom_call" | custom-call | flops 536870912 | bytes 4194304 | tf_op jit(solution)/shard_map/pallas_call | solution.py:137
  47.7 1.3 %collective-permute-done.10.refs_1_ = bf16[3,2,128,128]{3,2,1,0:T(8,128)(2,1)S(1)} collective-permute-done((bf16[3,2,128,128]{3,2,1,0:T(8,128)(2,1)S(1)}, bf16[3,2,128,128]{3,2,1,0:T(8,128)(2,1)S(1)}, u32[]{:S(2)}, u32[]{:S(2)}) %collective-permute-start.10) | collective-permute-done | bytes 196640 | tf_op jit(solution)/shard_map/ppermute | solution.py:248
  49.9 2.4 %collective-permute-start.13 = (bf16[2,128,128]{2,1,0:T(8,128)(2,1)S(1)}, bf16[2,128,128]{2,1,0:T(8,128)(2,1)S(1)}, u32[]{:S(2)}, u32[]{:S(2)}) collective-permute-start(bf16[2,128,128]{2,1,0:T(8,128)(2,1)S(1)} %get-tuple-element.83), channel_id=1, source_target_pairs={{0,1},{1,0},{2,3},{3,2},{4,5},{5,4},{6,7},{7,6},{8,9},{9,8},{10,11... | collective-permute-start | bytes 196616 | tf_op jit(solution)/shard_map/ppermute | solution.py:248
  52.9 1.6 %collective-permute-start.15 = (bf16[2,128,128]{2,1,0:T(8,128)(2,1)S(1)}, bf16[2,128,128]{2,1,0:T(8,128)(2,1)S(1)}, u32[]{:S(2)}, u32[]{:S(2)}) collective-permute-start(bf16[2,128,128]{2,1,0:T(8,128)(2,1)S(1)} %get-tuple-element.85), channel_id=1, source_target_pairs={{0,3},{1,2},{2,1},{3,0},{4,7},{5,6},{6,5},{7,4},{8,11},{9,10},{10,... | collective-permute-start | bytes 196616 | tf_op jit(solution)/shard_map/ppermute | solution.py:248
  54.5 1.3 %collective-permute-start.16 = (bf16[2,128,128]{2,1,0:T(8,128)(2,1)S(1)}, bf16[2,128,128]{2,1,0:T(8,128)(2,1)S(1)}, u32[]{:S(2)}, u32[]{:S(2)}) collective-permute-start(bf16[2,128,128]{2,1,0:T(8,128)(2,1)S(1)} %get-tuple-element.86), channel_id=1, source_target_pairs={{4,0},{5,1},{6,2},{7,3},{12,8},{13,9},{14,10},{15,11},{20,16},{21,... | collective-permute-start | bytes 196616 | tf_op jit(solution)/shard_map/ppermute | solution.py:248
  55.8 1.3 %collective-permute-start.17 = (bf16[2,128,128]{2,1,0:T(8,128)(2,1)S(1)}, bf16[2,128,128]{2,1,0:T(8,128)(2,1)S(1)}, u32[]{:S(2)}, u32[]{:S(2)}) collective-permute-start(bf16[2,128,128]{2,1,0:T(8,128)(2,1)S(1)} %get-tuple-element.87), channel_id=1, source_target_pairs={{4,1},{5,0},{6,3},{7,2},{12,9},{13,8},{14,11},{15,10},{20,17},{21,... | collective-permute-start | bytes 196616 | tf_op jit(solution)/shard_map/ppermute | solution.py:248
  57.1 1.3 %collective-permute-start.18 = (bf16[2,128,128]{2,1,0:T(8,128)(2,1)S(1)}, bf16[2,128,128]{2,1,0:T(8,128)(2,1)S(1)}, u32[]{:S(2)}, u32[]{:S(2)}) collective-permute-start(bf16[2,128,128]{2,1,0:T(8,128)(2,1)S(1)} %get-tuple-element.88), channel_id=1, source_target_pairs={{4,2},{5,3},{6,0},{7,1},{12,10},{13,11},{14,8},{15,9},{20,18},{21,... | collective-permute-start | bytes 196616 | tf_op jit(solution)/shard_map/ppermute | solution.py:248
  58.4 1.3 %collective-permute-start.19 = (bf16[2,128,128]{2,1,0:T(8,128)(2,1)S(1)}, bf16[2,128,128]{2,1,0:T(8,128)(2,1)S(1)}, u32[]{:S(2)}, u32[]{:S(2)}) collective-permute-start(bf16[2,128,128]{2,1,0:T(8,128)(2,1)S(1)} %get-tuple-element.89), channel_id=1, source_target_pairs={{4,3},{5,2},{6,1},{7,0},{12,11},{13,10},{14,9},{15,8},{20,19},{21,... | collective-permute-start | bytes 196616 | tf_op jit(solution)/shard_map/ppermute | solution.py:248
  61.5 1.4 %shard_map.103 = (bf16[128,4096]{1,0:T(8,128)(2,1)}, bf16[128,4096]{1,0:T(8,128)(2,1)}) custom-call(s32[1]{0:T(128)} %bitcast.pos_ref.refs_0_, bf16[128,1024]{1,0:T(8,128)(2,1)S(1)} %get-tuple-element.55.refs_0_, bf16[128,1024]{1,0:T(8,128)(2,1)S(1)} %get-tuple-element.56.refs_1_, bf16[128,1024]{1,0:T(8,128)(2,1)S(1)} %get-tuple-element.60.refs_2_, ...), custom_call_target="tpu_custom_call" | custom-call | flops 4194304 | bytes 2097152 | tf_op jit(solution)/shard_map/pallas_call | solution.py:285
  62.9 2.0 %collective-permute-done.17.refs_9_ = bf16[2,128,128]{2,1,0:T(8,128)(2,1)S(1)} collective-permute-done((bf16[2,128,128]{2,1,0:T(8,128)(2,1)S(1)}, bf16[2,128,128]{2,1,0:T(8,128)(2,1)S(1)}, u32[]{:S(2)}, u32[]{:S(2)}) %collective-permute-start.17) | collective-permute-done | bytes 65568 | tf_op jit(solution)/shard_map/ppermute | solution.py:248
  65.1 2.7 %collective-permute-done.19.refs_11_ = bf16[2,128,128]{2,1,0:T(8,128)(2,1)S(1)} collective-permute-done((bf16[2,128,128]{2,1,0:T(8,128)(2,1)S(1)}, bf16[2,128,128]{2,1,0:T(8,128)(2,1)S(1)}, u32[]{:S(2)}, u32[]{:S(2)}) %collective-permute-start.19) | collective-permute-done | bytes 65568 | tf_op jit(solution)/shard_map/ppermute | solution.py:248
  (40 shorter events, 9.1 us)
Async XLA Ops:
  1.6 11.8 %collective-permute-start.3 = (bf16[2,128,128]{2,1,0:T(8,128)(2,1)S(1)}, bf16[2,128,128]{2,1,0:T(8,128)(2,1)S(1)}, u32[]{:S(2)}, u32[]{:S(2)}) collective-permute-start(bf16[2,128,128]{2,1,0:T(8,128)(2,1)S(1)} %get-tuple-element.48.refs_0_.refs_6_.refs_3_), channel_id=1, source_target_pairs={{0,4},{1,5},{2,6},{3,7},{8,12},{9,13},{10,14},{11,15},{16,20},{17,... | collective-permute-start | bytes 196616 | tf_op jit(solution)/shard_map/ppermute | solution.py:248
  7.6 12.7 %copy-start.2 = (s32[8,4]{0,1:T(4,128)S(1)}, s32[8,4]{0,1:T(4,128)}, u32[]{:S(2)}) copy-start(s32[8,4]{0,1:T(4,128)} %param.10) | copy-start | bytes 388
  7.6 12.6 %collective-permute-start.4 = (bf16[2,128,128]{2,1,0:T(8,128)(2,1)S(1)}, bf16[2,128,128]{2,1,0:T(8,128)(2,1)S(1)}, u32[]{:S(2)}, u32[]{:S(2)}) collective-permute-start(bf16[2,128,128]{2,1,0:T(8,128)(2,1)S(1)} %get-tuple-element.49.refs_6_.refs_3_), channel_id=1, source_target_pairs={{0,5},{1,4},{2,7},{3,6},{8,13},{9,12},{10,15},{11,14},{16,21},{17,... | collective-permute-start | bytes 196616 | tf_op jit(solution)/shard_map/ppermute | solution.py:248
  9.8 10.5 %collective-permute-start = (bf16[2,128,128]{2,1,0:T(8,128)(2,1)S(1)}, bf16[2,128,128]{2,1,0:T(8,128)(2,1)S(1)}, u32[]{:S(2)}, u32[]{:S(2)}) collective-permute-start(bf16[2,128,128]{2,1,0:T(8,128)(2,1)S(1)} %get-tuple-element.49.refs_6_.refs_3_), channel_id=1, source_target_pairs={{0,1},{1,0},{2,3},{3,2},{4,5},{5,4},{6,7},{7,6},{8,9},{9,8},{10,11... | collective-permute-start | bytes 196616 | tf_op jit(solution)/shard_map/ppermute | solution.py:248
  10.5 9.9 %collective-permute-start.5 = (bf16[2,128,128]{2,1,0:T(8,128)(2,1)S(1)}, bf16[2,128,128]{2,1,0:T(8,128)(2,1)S(1)}, u32[]{:S(2)}, u32[]{:S(2)}) collective-permute-start(bf16[2,128,128]{2,1,0:T(8,128)(2,1)S(1)} %get-tuple-element.50.refs_6_.refs_3_), channel_id=1, source_target_pairs={{0,6},{1,7},{2,4},{3,5},{8,14},{9,15},{10,12},{11,13},{16,22},{17,... | collective-permute-start | bytes 196616 | tf_op jit(solution)/shard_map/ppermute | solution.py:248
  12.8 7.6 %collective-permute-start.1 = (bf16[2,128,128]{2,1,0:T(8,128)(2,1)S(1)}, bf16[2,128,128]{2,1,0:T(8,128)(2,1)S(1)}, u32[]{:S(2)}, u32[]{:S(2)}) collective-permute-start(bf16[2,128,128]{2,1,0:T(8,128)(2,1)S(1)} %get-tuple-element.50.refs_6_.refs_3_), channel_id=1, source_target_pairs={{0,2},{1,3},{2,0},{3,1},{4,6},{5,7},{6,4},{7,5},{8,10},{9,11},{10,... | collective-permute-start | bytes 196616 | tf_op jit(solution)/shard_map/ppermute | solution.py:248
  13.4 8.6 %collective-permute-start.6 = (bf16[2,128,128]{2,1,0:T(8,128)(2,1)S(1)}, bf16[2,128,128]{2,1,0:T(8,128)(2,1)S(1)}, u32[]{:S(2)}, u32[]{:S(2)}) collective-permute-start(bf16[2,128,128]{2,1,0:T(8,128)(2,1)S(1)} %get-tuple-element.51.refs_6_.refs_3_), channel_id=1, source_target_pairs={{0,7},{1,6},{2,5},{3,4},{8,15},{9,14},{10,13},{11,12},{16,23},{17,... | collective-permute-start | bytes 196616 | tf_op jit(solution)/shard_map/ppermute | solution.py:248
  20.2 5.2 %collective-permute-start.2 = (bf16[2,128,128]{2,1,0:T(8,128)(2,1)S(1)}, bf16[2,128,128]{2,1,0:T(8,128)(2,1)S(1)}, u32[]{:S(2)}, u32[]{:S(2)}) collective-permute-start(bf16[2,128,128]{2,1,0:T(8,128)(2,1)S(1)} %get-tuple-element.51.refs_6_.refs_3_), channel_id=1, source_target_pairs={{0,3},{1,2},{2,1},{3,0},{4,7},{5,6},{6,5},{7,4},{8,11},{9,10},{10,... | collective-permute-start | bytes 196616 | tf_op jit(solution)/shard_map/ppermute | solution.py:248
  20.3 12.8 %copy-start = (bf16[128,4096]{1,0:T(8,128)(2,1)S(1)}, bf16[128,4096]{1,0:T(8,128)(2,1)}, u32[]{:S(2)}) copy-start(bf16[128,4096]{1,0:T(8,128)(2,1)} %refs_3_.7) | copy-start | bytes 3145732
  20.3 12.8 %copy-start.1 = (bf16[128,4096]{1,0:T(8,128)(2,1)S(1)}, bf16[128,4096]{1,0:T(8,128)(2,1)}, u32[]{:S(2)}) copy-start(bf16[128,4096]{1,0:T(8,128)(2,1)} %refs_4_.7) | copy-start | bytes 3145732
  26.1 7.0 %collective-permute-start.9 = (bf16[3,2,128,128]{3,2,1,0:T(8,128)(2,1)S(1)}, bf16[3,2,128,128]{3,2,1,0:T(8,128)(2,1)S(1)}, u32[]{:S(2)}, u32[]{:S(2)}) collective-permute-start(bf16[3,2,128,128]{3,2,1,0:T(8,128)(2,1)S(1)} %get-tuple-element.67), channel_id=1, source_target_pairs={{0,3},{1,2},{2,1},{3,0},{4,7},{5,6},{6,5},{7,4},{8,11},{9,10},{10,... | collective-permute-start | bytes 589832 | tf_op jit(solution)/shard_map/ppermute | solution.py:248
  26.8 2.9 %copy-start.3 = (s32[128]{0:T(128)S(1)}, s32[128]{0:T(128)}, u32[]{:S(2)}) copy-start(s32[128]{0:T(128)} %param.11) | copy-start | bytes 1540
  26.8 10.0 %collective-permute-start.8 = (bf16[3,2,128,128]{3,2,1,0:T(8,128)(2,1)S(1)}, bf16[3,2,128,128]{3,2,1,0:T(8,128)(2,1)S(1)}, u32[]{:S(2)}, u32[]{:S(2)}) collective-permute-start(bf16[3,2,128,128]{3,2,1,0:T(8,128)(2,1)S(1)} %get-tuple-element.62), channel_id=1, source_target_pairs={{0,2},{1,3},{2,0},{3,1},{4,6},{5,7},{6,4},{7,5},{8,10},{9,11},{10,... | collective-permute-start | bytes 589832 | tf_op jit(solution)/shard_map/ppermute | solution.py:248
  27.4 12.6 %collective-permute-start.7 = (bf16[3,2,128,128]{3,2,1,0:T(8,128)(2,1)S(1)}, bf16[3,2,128,128]{3,2,1,0:T(8,128)(2,1)S(1)}, u32[]{:S(2)}, u32[]{:S(2)}) collective-permute-start(bf16[3,2,128,128]{3,2,1,0:T(8,128)(2,1)S(1)} %get-tuple-element.57), channel_id=1, source_target_pairs={{0,1},{1,0},{2,3},{3,2},{4,5},{5,4},{6,7},{7,6},{8,9},{9,8},{10,11... | collective-permute-start | bytes 589832 | tf_op jit(solution)/shard_map/ppermute | solution.py:248
  35.9 11.8 %collective-permute-start.12 = (bf16[3,2,128,128]{3,2,1,0:T(8,128)(2,1)S(1)}, bf16[3,2,128,128]{3,2,1,0:T(8,128)(2,1)S(1)}, u32[]{:S(2)}, u32[]{:S(2)}) collective-permute-start(bf16[3,2,128,128]{3,2,1,0:T(8,128)(2,1)S(1)} %get-tuple-element.81), channel_id=1, source_target_pairs={{0,3},{1,2},{2,1},{3,0},{4,7},{5,6},{6,5},{7,4},{8,11},{9,10},{10,... | collective-permute-start | bytes 589832 | tf_op jit(solution)/shard_map/ppermute | solution.py:248
  39.5 8.2 %collective-permute-start.11 = (bf16[3,2,128,128]{3,2,1,0:T(8,128)(2,1)S(1)}, bf16[3,2,128,128]{3,2,1,0:T(8,128)(2,1)S(1)}, u32[]{:S(2)}, u32[]{:S(2)}) collective-permute-start(bf16[3,2,128,128]{3,2,1,0:T(8,128)(2,1)S(1)} %get-tuple-element.80), channel_id=1, source_target_pairs={{0,2},{1,3},{2,0},{3,1},{4,6},{5,7},{6,4},{7,5},{8,10},{9,11},{10,... | collective-permute-start | bytes 589832 | tf_op jit(solution)/shard_map/ppermute | solution.py:248
  42.7 6.3 %collective-permute-start.10 = (bf16[3,2,128,128]{3,2,1,0:T(8,128)(2,1)S(1)}, bf16[3,2,128,128]{3,2,1,0:T(8,128)(2,1)S(1)}, u32[]{:S(2)}, u32[]{:S(2)}) collective-permute-start(bf16[3,2,128,128]{3,2,1,0:T(8,128)(2,1)S(1)} %get-tuple-element.79), channel_id=1, source_target_pairs={{0,1},{1,0},{2,3},{3,2},{4,5},{5,4},{6,7},{7,6},{8,9},{9,8},{10,11... | collective-permute-start | bytes 589832 | tf_op jit(solution)/shard_map/ppermute | solution.py:248
  49.9 7.2 %collective-permute-start.13 = (bf16[2,128,128]{2,1,0:T(8,128)(2,1)S(1)}, bf16[2,128,128]{2,1,0:T(8,128)(2,1)S(1)}, u32[]{:S(2)}, u32[]{:S(2)}) collective-permute-start(bf16[2,128,128]{2,1,0:T(8,128)(2,1)S(1)} %get-tuple-element.83), channel_id=1, source_target_pairs={{0,1},{1,0},{2,3},{3,2},{4,5},{5,4},{6,7},{7,6},{8,9},{9,8},{10,11... | collective-permute-start | bytes 196616 | tf_op jit(solution)/shard_map/ppermute | solution.py:248
  52.3 6.1 %collective-permute-start.14 = (bf16[2,128,128]{2,1,0:T(8,128)(2,1)S(1)}, bf16[2,128,128]{2,1,0:T(8,128)(2,1)S(1)}, u32[]{:S(2)}, u32[]{:S(2)}) collective-permute-start(bf16[2,128,128]{2,1,0:T(8,128)(2,1)S(1)} %get-tuple-element.84), channel_id=1, source_target_pairs={{0,2},{1,3},{2,0},{3,1},{4,6},{5,7},{6,4},{7,5},{8,10},{9,11},{10,... | collective-permute-start | bytes 196616 | tf_op jit(solution)/shard_map/ppermute | solution.py:248
  52.9 10.0 %collective-permute-start.15 = (bf16[2,128,128]{2,1,0:T(8,128)(2,1)S(1)}, bf16[2,128,128]{2,1,0:T(8,128)(2,1)S(1)}, u32[]{:S(2)}, u32[]{:S(2)}) collective-permute-start(bf16[2,128,128]{2,1,0:T(8,128)(2,1)S(1)} %get-tuple-element.85), channel_id=1, source_target_pairs={{0,3},{1,2},{2,1},{3,0},{4,7},{5,6},{6,5},{7,4},{8,11},{9,10},{10,... | collective-permute-start | bytes 196616 | tf_op jit(solution)/shard_map/ppermute | solution.py:248
  54.5 8.4 %collective-permute-start.16 = (bf16[2,128,128]{2,1,0:T(8,128)(2,1)S(1)}, bf16[2,128,128]{2,1,0:T(8,128)(2,1)S(1)}, u32[]{:S(2)}, u32[]{:S(2)}) collective-permute-start(bf16[2,128,128]{2,1,0:T(8,128)(2,1)S(1)} %get-tuple-element.86), channel_id=1, source_target_pairs={{4,0},{5,1},{6,2},{7,3},{12,8},{13,9},{14,10},{15,11},{20,16},{21,... | collective-permute-start | bytes 196616 | tf_op jit(solution)/shard_map/ppermute | solution.py:248
  55.8 9.1 %collective-permute-start.17 = (bf16[2,128,128]{2,1,0:T(8,128)(2,1)S(1)}, bf16[2,128,128]{2,1,0:T(8,128)(2,1)S(1)}, u32[]{:S(2)}, u32[]{:S(2)}) collective-permute-start(bf16[2,128,128]{2,1,0:T(8,128)(2,1)S(1)} %get-tuple-element.87), channel_id=1, source_target_pairs={{4,1},{5,0},{6,3},{7,2},{12,9},{13,8},{14,11},{15,10},{20,17},{21,... | collective-permute-start | bytes 196616 | tf_op jit(solution)/shard_map/ppermute | solution.py:248
  57.1 8.0 %collective-permute-start.18 = (bf16[2,128,128]{2,1,0:T(8,128)(2,1)S(1)}, bf16[2,128,128]{2,1,0:T(8,128)(2,1)S(1)}, u32[]{:S(2)}, u32[]{:S(2)}) collective-permute-start(bf16[2,128,128]{2,1,0:T(8,128)(2,1)S(1)} %get-tuple-element.88), channel_id=1, source_target_pairs={{4,2},{5,3},{6,0},{7,1},{12,10},{13,11},{14,8},{15,9},{20,18},{21,... | collective-permute-start | bytes 196616 | tf_op jit(solution)/shard_map/ppermute | solution.py:248
  58.4 9.4 %collective-permute-start.19 = (bf16[2,128,128]{2,1,0:T(8,128)(2,1)S(1)}, bf16[2,128,128]{2,1,0:T(8,128)(2,1)S(1)}, u32[]{:S(2)}, u32[]{:S(2)}) collective-permute-start(bf16[2,128,128]{2,1,0:T(8,128)(2,1)S(1)} %get-tuple-element.89), channel_id=1, source_target_pairs={{4,3},{5,2},{6,1},{7,0},{12,11},{13,10},{14,9},{15,8},{20,19},{21,... | collective-permute-start | bytes 196616 | tf_op jit(solution)/shard_map/ppermute | solution.py:248

commit v3 on v2

--- a/solution.py
+++ b/solution.py
@@ -27,6 +27,7 @@
 LAST = (((1,), (1,)), ((), ()))
 FIRST = (((0,), (0,)), ((), ()))
 SCALING = 1.0 / math.sqrt(HEAD_WIDTH)
+EXPONENT = SCALING * math.log2(math.e)
 
 
 def dot(left, right, dims=(((1,), (0,)), ((), ()))):
@@ -61,27 +62,38 @@
         copy.wait()
 
 
-def select_kernel(count, pos_ref, path_ref, *refs):
-    pieces, outs, held = refs[:count], refs[count : count + GROUP], refs[-1]
+def plan_kernel(pos_ref, path_ref, pick_ref, add_ref, mask_ref):
     position = pos_ref[0]
     member, group = lax.rem(position, GROUP), lax.div(position, GROUP)
-    for i in range(count):
-        held[i] = pieces[i][...]
-    for t in range(GROUP):
-        block = group * GROUP + member ^ t
+    for t in range(GROUP):
+        block = group * GROUP + (member ^ t)
         for e in range(FAR_SLOTS):
             ancestor = path_ref[block, e]
             seen = path_ref[block, e + 1] >= 0
             above = group - lax.div(ancestor, GROUP)
             index = above * GROUP + (member ^ lax.rem(ancestor, GROUP))
-            outs[t][e] = held[jnp.where(seen, index, 0)]
+            row = pl.ds(t * FAR_SLOTS + e, 1)
+            pick_ref[row, :] = jnp.full((1, HEAD_WIDTH), jnp.where(seen, index, 0), jnp.int32)
+            add_ref[row, :] = jnp.full((1, HEAD_WIDTH), jnp.where(seen, index, -1), jnp.int32)
+    for e in range(FAR_SLOTS):
+        masked = jnp.where(path_ref[position, e + 1] >= 0, 0.0, MASKED)
+        mask_ref[pl.ds(e, 1), :] = jnp.full((1, HEAD_WIDTH), masked, jnp.float32)
+
+
+def select_kernel(count, pick_ref, *refs):
+    pieces, outs, held = refs[:count], refs[count : count + GROUP], refs[-1]
+    pick = pick_ref[...]
+    for i in range(count):
+        held[i] = pieces[i][...]
+    for t in range(GROUP):
+        for e in range(FAR_SLOTS):
+            outs[t][e] = held[pick[t * FAR_SLOTS + e, 0]]
 
 
 def attend_kernel(turn, rows, *refs):
-    (pos_ref, path_ref, mask_ref, q_ref, go_ref, far_ref, own_ref) = refs[:7]
+    (pos_ref, hide_ref, mask_ref, q_ref, go_ref, far_ref, own_ref) = refs[:7]
     weights_ref, grad_score_ref, far_grad_ref, own_grad_ref = refs[7:]
-    position = pos_ref[0]
-    head = lax.rem(position, GROUP) ^ turn
+    head = lax.rem(pos_ref[0], GROUP) ^ turn
     far_rows = FAR_SLOTS * rows
     mask = mask_ref[...]
     blocks = [head_columns(head * HEADS_PER_KEY + i) for i in range(HEADS_PER_KEY)]
@@ -92,14 +104,17 @@
     token = lax.broadcasted_iota(jnp.int32, (rows, rows), 1)
     causal = jnp.where(key <= token, 0.0, MASKED)
     scores = dot(kk, qm, LAST)
-    parts = [
-        scores[e * rows : (e + 1) * rows] + jnp.where(path_ref[position, e + 1] >= 0, 0.0, MASKED)
-        for e in range(FAR_SLOTS)
-    ]
+    parts = [scores[e * rows : (e + 1) * rows] for e in range(FAR_SLOTS)]
     parts.append(scores[far_rows:] + jnp.concatenate([causal] * HEADS_PER_KEY, 1))
-    scores = jnp.concatenate(parts, 0)
-    top = jnp.max(scores, axis=0, keepdims=True)
-    weights = jnp.exp2((scores - top) * (SCALING * math.log2(math.e)))
+    hides = [jnp.concatenate([hide_ref[e : e + 1]] * HEADS_PER_KEY, 1) for e in range(FAR_SLOTS)]
+    tops = [jnp.max(part, axis=0, keepdims=True) for part in parts]
+    top = tops[-1]
+    for slot_top, hide in zip(tops, hides):
+        top = jnp.maximum(top, slot_top + hide)
+    shifts = [top - hide for hide in hides] + [top]
+    weights = jnp.concatenate(
+        [jnp.exp2((part - shift) * EXPONENT) for part, shift in zip(parts, shifts)], 0
+    )
     weights = weights * (1.0 / jnp.sum(weights, axis=0, keepdims=True))
     rounded = weights.astype(jnp.bfloat16)
     grad_prob = dot(vv, gm, LAST)
@@ -129,14 +144,14 @@
         gq_ref[:, cols] = grad_query[:, s].T.astype(jnp.bfloat16)
 
 
-def attend(turn, pos, path, mask, queries, grad_out, far, own):
+def attend(turn, pos, hide, mask, queries, grad_out, far, own):
     rows = queries.shape[0]
     span = (FAR_SLOTS + 1) * rows
     pairs = rows * HEADS_PER_KEY * span
     square = jax.ShapeDtypeStruct((span, HEADS_PER_KEY * rows), jnp.bfloat16)
     return pl.pallas_call(
         functools.partial(attend_kernel, turn, rows),
-        in_specs=[SMEM_SPEC] * 2 + [VMEM_SPEC] * 5,
+        in_specs=[SMEM_SPEC] + [VMEM_SPEC] * 6,
         out_specs=[VMEM_SPEC] * 4,
         out_shape=[
             square,
@@ -146,7 +161,7 @@
         ],
         cost_estimate=cost(8 * pairs * HEAD_WIDTH, 8 * pairs),
         compiler_params=pltpu.CompilerParams(vmem_limit_bytes=VMEM_LIMIT),
-    )(pos, path, mask, queries, grad_out, far, own)
+    )(pos, hide, mask, queries, grad_out, far, own)
 
 
 def output(weights, grad_score, far, own):
@@ -179,19 +194,15 @@
         copy.wait()
 
 
-def reduce_kernel(count, pos_ref, path_ref, *refs):
+def reduce_kernel(count, add_ref, *refs):
     terms, outs, acc = refs[:GROUP], refs[GROUP : GROUP + count], refs[-1]
-    position = pos_ref[0]
-    member, group = lax.rem(position, GROUP), lax.div(position, GROUP)
+    add = add_ref[...]
     acc[...] = jnp.zeros_like(acc)
     for t in range(GROUP):
-        block = group * GROUP + member ^ t
         for e in range(FAR_SLOTS):
-            ancestor = path_ref[block, e]
-            above = group - lax.div(ancestor, GROUP)
-            index = above * GROUP + (member ^ lax.rem(ancestor, GROUP))
-
-            @pl.when(path_ref[block, e + 1] >= 0)
+            index = add[t * FAR_SLOTS + e, 0]
+
+            @pl.when(index >= 0)
             def _(t=t, e=e, index=index):
                 acc[index] += terms[t][e].astype(jnp.float32)
 
@@ -264,18 +275,24 @@
     far_pieces = far_sends(packed, 1)
     pieces = near_sends(packed) + far_pieces
 
+    table = jax.ShapeDtypeStruct((16, HEAD_WIDTH), jnp.int32)
+    pick, add, hide = small_call(
+        plan_kernel, [SMEM_SPEC] * 2, [VMEM_SPEC] * 3,
+        [table, table, jax.ShapeDtypeStruct((8, HEAD_WIDTH), jnp.float32)], 3 * 8192,
+    )(pos, block_path)
+
     picked = small_call(
         functools.partial(select_kernel, size),
-        [SMEM_SPEC, SMEM_SPEC] + [VMEM_SPEC] * size, [VMEM_SPEC] * GROUP, [chosen] * GROUP,
+        [VMEM_SPEC] * (1 + size), [VMEM_SPEC] * GROUP, [chosen] * GROUP,
         (size + 12) * piece_bytes, [pltpu.VMEM((size,) + piece.shape, jnp.bfloat16)],
         COVER_FLOPS,
-    )(pos, block_path, *pieces)
+    )(pick, *pieces)
     far = near_sends(picked)
 
     blocks, far_grads, own_grads = [], [], []
     for t in range(GROUP):
         weights, grad_score, far_grad, own_grad = attend(
-            t, pos, block_path, mask, queries, grad_out, far[t], packed[t]
+            t, pos, hide, mask, queries, grad_out, far[t], packed[t]
         )
         blocks += output(weights, grad_score, far[t], packed[t])
         far_grads.append(far_grad)
@@ -289,9 +306,9 @@
 
     sums = small_call(
         functools.partial(reduce_kernel, size),
-        [SMEM_SPEC, SMEM_SPEC] + [VMEM_SPEC] * GROUP, [VMEM_SPEC] * size, [piece] * size,
+        [VMEM_SPEC] * (1 + GROUP), [VMEM_SPEC] * size, [piece] * size,
         (size + 12) * piece_bytes, [pltpu.VMEM((size,) + piece.shape, jnp.float32)],
-    )(pos, block_path, *far_grads)
+    )(add, *far_grads)
     far_sums = far_sends(sums, -1)
     near_sums = near_sends(sums[:GROUP])
 

time: 69 us -> 66.1 us (0.958)
  Pallas kernels: 17.9 us -> 15 us
    pallas_call x4, Pallas kernels: 10.8 us -> 8.12 us  [attend(): pl.pallas_call(functools.partial(attend_kernel, turn, rows), in_specs=[SM...]
    pallas_call x2 -> x3, Pallas kernels: 1.57 us -> 1.41 us  [the longest x1 0.67 us: on_device(): small_call(plan_kernel, [SMEM_SPEC] * 2, [VMEM_SPEC] * 3, [table, table,...]
  transfers between devices with their start and end apart: 20 -> 20, of which waited for: 7 -> 7; matrix products, arithmetic and copies ran while one was open for 0% -> 0% of each run, Pallas kernels for 21% -> 19%
where the time goes in v3:
time: 66.1 us; the launch traced here: 65.8 us
  starting transfers between devices  35.1 us (53%)
  Pallas kernels  15 us (23%)
  waiting for transfers between devices  14.6 us (22%)
  between operations  0.91 us (1%)
    ppermute x20, starting transfers between devices, send(): return lax.ppermute(x, 'ctx', pairs)  35.1 us
    ppermute x20, waiting for transfers between devices, send(): return lax.ppermute(x, 'ctx', pairs)  14.6 us
    pallas_call x4, Pallas kernels, attend(): pl.pallas_call(functools.partial(attend_kernel, turn, rows), in_specs=[SM...  8.12 us
    pallas_call x4, Pallas kernels, output(): pl.pallas_call(functools.partial(output_kernel, rows), in_specs=[VMEM_SPE...  2.34 us
    pallas_call x1, Pallas kernels, on_device(): small_call(store_kernel, [SMEM_SPEC] + [VMEM_SPEC] * (2 * GROUP), [HBM_SP...  1.38 us
  transfers between devices with their start and end apart: 20, of which 7 were waited for; matrix products, arithmetic and copies ran while one was open for 0% of the time, Pallas kernels for 19%

profile of v3, /device:TPU:0, one launch (start us, length us, event | category | flops | bytes accessed | tf_op | source)
XLA Modules:
  0.0 65.8 jit_solution(11932733673943074600)
XLA Ops:
  0.6 1.0 %shard_map.94 = (bf16[2,128,128]{2,1,0:T(8,128)(2,1)S(1)}, bf16[2,128,128]{2,1,0:T(8,128)(2,1)S(1)}, bf16[2,128,128]{2,1,0:T(8,128)(2,1)S(1)}, bf16[2,128,128]{2,1,0:T(8,128)(2,1)S(1)}) custom-call(s32[1]{0:T(128)} %bitcast.pos_ref.refs_0_, bf16[128,512]{1,0:T(8,128)(2,1)} %k_ref.1, bf16[128,512]{1,0:T(8,128)(2,1)} %v_ref.1), custom_call_target="tpu_custom_call" | custom-call | flops 1048576 | bytes 524288 | tf_op jit(solution)/shard_map/pallas_call | solution.py:271
  1.6 6.0 %collective-permute-start.3 = (bf16[2,128,128]{2,1,0:T(8,128)(2,1)S(1)}, bf16[2,128,128]{2,1,0:T(8,128)(2,1)S(1)}, u32[]{:S(2)}, u32[]{:S(2)}) collective-permute-start(bf16[2,128,128]{2,1,0:T(8,128)(2,1)S(1)} %get-tuple-element.53.refs_0_.refs_6_.refs_3_), channel_id=1, source_target_pairs={{0,4},{1,5},{2,6},{3,7},{8,12},{9,13},{10,14},{11,15},{16,20},{17,... | collective-permute-start | bytes 196616 | tf_op jit(solution)/shard_map/ppermute | solution.py:259
  7.6 2.2 %collective-permute-start.4 = (bf16[2,128,128]{2,1,0:T(8,128)(2,1)S(1)}, bf16[2,128,128]{2,1,0:T(8,128)(2,1)S(1)}, u32[]{:S(2)}, u32[]{:S(2)}) collective-permute-start(bf16[2,128,128]{2,1,0:T(8,128)(2,1)S(1)} %get-tuple-element.54.refs_6_.refs_3_), channel_id=1, source_target_pairs={{0,5},{1,4},{2,7},{3,6},{8,13},{9,12},{10,15},{11,14},{16,21},{17,... | collective-permute-start | bytes 196616 | tf_op jit(solution)/shard_map/ppermute | solution.py:259
  10.5 2.3 %collective-permute-start.5 = (bf16[2,128,128]{2,1,0:T(8,128)(2,1)S(1)}, bf16[2,128,128]{2,1,0:T(8,128)(2,1)S(1)}, u32[]{:S(2)}, u32[]{:S(2)}) collective-permute-start(bf16[2,128,128]{2,1,0:T(8,128)(2,1)S(1)} %get-tuple-element.55.refs_6_.refs_3_), channel_id=1, source_target_pairs={{0,6},{1,7},{2,4},{3,5},{8,14},{9,15},{10,12},{11,13},{16,22},{17,... | collective-permute-start | bytes 196616 | tf_op jit(solution)/shard_map/ppermute | solution.py:259
  13.4 6.7 %collective-permute-start.6 = (bf16[2,128,128]{2,1,0:T(8,128)(2,1)S(1)}, bf16[2,128,128]{2,1,0:T(8,128)(2,1)S(1)}, u32[]{:S(2)}, u32[]{:S(2)}) collective-permute-start(bf16[2,128,128]{2,1,0:T(8,128)(2,1)S(1)} %get-tuple-element.56.refs_6_.refs_3_), channel_id=1, source_target_pairs={{0,7},{1,6},{2,5},{3,4},{8,15},{9,14},{10,13},{11,12},{16,23},{17,... | collective-permute-start | bytes 196616 | tf_op jit(solution)/shard_map/ppermute | solution.py:259
  21.0 1.0 %collective-permute-done.6.refs_7_ = bf16[2,128,128]{2,1,0:T(8,128)(2,1)S(1)} collective-permute-done((bf16[2,128,128]{2,1,0:T(8,128)(2,1)S(1)}, bf16[2,128,128]{2,1,0:T(8,128)(2,1)S(1)}, u32[]{:S(2)}, u32[]{:S(2)}) %collective-permute-start.6) | collective-permute-done | bytes 65568 | tf_op jit(solution)/shard_map/ppermute | solution.py:259
  22.0 3.4 %collective-permute-done.2.refs_3_ = bf16[2,128,128]{2,1,0:T(8,128)(2,1)S(1)} collective-permute-done((bf16[2,128,128]{2,1,0:T(8,128)(2,1)S(1)}, bf16[2,128,128]{2,1,0:T(8,128)(2,1)S(1)}, u32[]{:S(2)}, u32[]{:S(2)}) %collective-permute-start.2) | collective-permute-done | bytes 65568 | tf_op jit(solution)/shard_map/ppermute | solution.py:259
  26.8 2.3 %collective-permute-start.7 = (bf16[3,2,128,128]{3,2,1,0:T(8,128)(2,1)S(1)}, bf16[3,2,128,128]{3,2,1,0:T(8,128)(2,1)S(1)}, u32[]{:S(2)}, u32[]{:S(2)}) collective-permute-start(bf16[3,2,128,128]{3,2,1,0:T(8,128)(2,1)S(1)} %get-tuple-element.62), channel_id=1, source_target_pairs={{0,1},{1,0},{2,3},{3,2},{4,5},{5,4},{6,7},{7,6},{8,9},{9,8},{10,11... | collective-permute-start | bytes 589832 | tf_op jit(solution)/shard_map/ppermute | solution.py:259
  29.1 3.4 %collective-permute-done.9.refs_5_.refs_2_ = bf16[3,2,128,128]{3,2,1,0:T(8,128)(2,1)S(1)} collective-permute-done((bf16[3,2,128,128]{3,2,1,0:T(8,128)(2,1)S(1)}, bf16[3,2,128,128]{3,2,1,0:T(8,128)(2,1)S(1)}, u32[]{:S(2)}, u32[]{:S(2)}) %collective-permute-start.9) | collective-permute-done | bytes 196640 | tf_op jit(solution)/shard_map/ppermute | solution.py:259
  32.6 2.0 %shard_map.102 = (bf16[512,1024]{1,0:T(8,128)(2,1)S(1)}, bf16[512,1024]{1,0:T(8,128)(2,1)S(1)}, bf16[3,2,128,128]{3,2,1,0:T(8,128)(2,1)S(1)}, f32[2,128,128]{2,1,0:T(8,128)S(1)}) custom-call(s32[1]{0:T(128)} %bitcast.pos_ref.refs_0_, f32[8,128]{1,0:T(8,128)S(1)} %get-tuple-element.51.refs_1_, bf16[128,128]{1,0:T(8,128)(2,1)S(1)} %broadcast_in_dim.2.refs_2_, ...), custom_call_target="tpu_custom_call" | custom-call | flops 536870912 | bytes 4194304 | tf_op jit(solution)/shard_map/pallas_call | solution.py:152
  35.5 2.0 %shard_map.100 = (bf16[512,1024]{1,0:T(8,128)(2,1)S(1)}, bf16[512,1024]{1,0:T(8,128)(2,1)S(1)}, bf16[3,2,128,128]{3,2,1,0:T(8,128)(2,1)S(1)}, f32[2,128,128]{2,1,0:T(8,128)S(1)}) custom-call(s32[1]{0:T(128)} %bitcast.pos_ref.refs_0_, f32[8,128]{1,0:T(8,128)S(1)} %get-tuple-element.51.refs_1_, bf16[128,128]{1,0:T(8,128)(2,1)S(1)} %broadcast_in_dim.2.refs_2_, ...), custom_call_target="tpu_custom_call" | custom-call | flops 536870912 | bytes 4194304 | tf_op jit(solution)/shard_map/pallas_call | solution.py:152
  38.0 2.0 %shard_map.98 = (bf16[512,1024]{1,0:T(8,128)(2,1)S(1)}, bf16[512,1024]{1,0:T(8,128)(2,1)S(1)}, bf16[3,2,128,128]{3,2,1,0:T(8,128)(2,1)S(1)}, f32[2,128,128]{2,1,0:T(8,128)S(1)}) custom-call(s32[1]{0:T(128)} %bitcast.pos_ref.refs_0_, f32[8,128]{1,0:T(8,128)S(1)} %get-tuple-element.51.refs_1_, bf16[128,128]{1,0:T(8,128)(2,1)S(1)} %broadcast_in_dim.2.refs_2_, ...), custom_call_target="tpu_custom_call" | custom-call | flops 536870912 | bytes 4194304 | tf_op jit(solution)/shard_map/pallas_call | solution.py:152
  40.0 2.3 %collective-permute-start.10 = (bf16[3,2,128,128]{3,2,1,0:T(8,128)(2,1)S(1)}, bf16[3,2,128,128]{3,2,1,0:T(8,128)(2,1)S(1)}, u32[]{:S(2)}, u32[]{:S(2)}) collective-permute-start(bf16[3,2,128,128]{3,2,1,0:T(8,128)(2,1)S(1)} %get-tuple-element.85), channel_id=1, source_target_pairs={{0,1},{1,0},{2,3},{3,2},{4,5},{5,4},{6,7},{7,6},{8,9},{9,8},{10,11... | collective-permute-start | bytes 589832 | tf_op jit(solution)/shard_map/ppermute | solution.py:259
  42.4 2.0 %shard_map.96 = (bf16[512,1024]{1,0:T(8,128)(2,1)S(1)}, bf16[512,1024]{1,0:T(8,128)(2,1)S(1)}, bf16[3,2,128,128]{3,2,1,0:T(8,128)(2,1)S(1)}, f32[2,128,128]{2,1,0:T(8,128)S(1)}) custom-call(s32[1]{0:T(128)} %bitcast.pos_ref.refs_0_, f32[8,128]{1,0:T(8,128)S(1)} %get-tuple-element.51.refs_1_, bf16[128,128]{1,0:T(8,128)(2,1)S(1)} %broadcast_in_dim.2.refs_2_, ...), custom_call_target="tpu_custom_call" | custom-call | flops 536870912 | bytes 4194304 | tf_op jit(solution)/shard_map/pallas_call | solution.py:152
  44.4 1.8 %collective-permute-done.10.refs_1_ = bf16[3,2,128,128]{3,2,1,0:T(8,128)(2,1)S(1)} collective-permute-done((bf16[3,2,128,128]{3,2,1,0:T(8,128)(2,1)S(1)}, bf16[3,2,128,128]{3,2,1,0:T(8,128)(2,1)S(1)}, u32[]{:S(2)}, u32[]{:S(2)}) %collective-permute-start.10) | collective-permute-done | bytes 196640 | tf_op jit(solution)/shard_map/ppermute | solution.py:259
  46.9 2.5 %collective-permute-start.13 = (bf16[2,128,128]{2,1,0:T(8,128)(2,1)S(1)}, bf16[2,128,128]{2,1,0:T(8,128)(2,1)S(1)}, u32[]{:S(2)}, u32[]{:S(2)}) collective-permute-start(bf16[2,128,128]{2,1,0:T(8,128)(2,1)S(1)} %get-tuple-element.89), channel_id=1, source_target_pairs={{0,1},{1,0},{2,3},{3,2},{4,5},{5,4},{6,7},{7,6},{8,9},{9,8},{10,11... | collective-permute-start | bytes 196616 | tf_op jit(solution)/shard_map/ppermute | solution.py:259
  50.0 1.6 %collective-permute-start.15 = (bf16[2,128,128]{2,1,0:T(8,128)(2,1)S(1)}, bf16[2,128,128]{2,1,0:T(8,128)(2,1)S(1)}, u32[]{:S(2)}, u32[]{:S(2)}) collective-permute-start(bf16[2,128,128]{2,1,0:T(8,128)(2,1)S(1)} %get-tuple-element.91), channel_id=1, source_target_pairs={{0,3},{1,2},{2,1},{3,0},{4,7},{5,6},{6,5},{7,4},{8,11},{9,10},{10,... | collective-permute-start | bytes 196616 | tf_op jit(solution)/shard_map/ppermute | solution.py:259
  51.6 1.3 %collective-permute-start.16 = (bf16[2,128,128]{2,1,0:T(8,128)(2,1)S(1)}, bf16[2,128,128]{2,1,0:T(8,128)(2,1)S(1)}, u32[]{:S(2)}, u32[]{:S(2)}) collective-permute-start(bf16[2,128,128]{2,1,0:T(8,128)(2,1)S(1)} %get-tuple-element.92), channel_id=1, source_target_pairs={{4,0},{5,1},{6,2},{7,3},{12,8},{13,9},{14,10},{15,11},{20,16},{21,... | collective-permute-start | bytes 196616 | tf_op jit(solution)/shard_map/ppermute | solution.py:259
  52.9 1.3 %collective-permute-start.17 = (bf16[2,128,128]{2,1,0:T(8,128)(2,1)S(1)}, bf16[2,128,128]{2,1,0:T(8,128)(2,1)S(1)}, u32[]{:S(2)}, u32[]{:S(2)}) collective-permute-start(bf16[2,128,128]{2,1,0:T(8,128)(2,1)S(1)} %get-tuple-element.93), channel_id=1, source_target_pairs={{4,1},{5,0},{6,3},{7,2},{12,9},{13,8},{14,11},{15,10},{20,17},{21,... | collective-permute-start | bytes 196616 | tf_op jit(solution)/shard_map/ppermute | solution.py:259
  54.2 1.3 %collective-permute-start.18 = (bf16[2,128,128]{2,1,0:T(8,128)(2,1)S(1)}, bf16[2,128,128]{2,1,0:T(8,128)(2,1)S(1)}, u32[]{:S(2)}, u32[]{:S(2)}) collective-permute-start(bf16[2,128,128]{2,1,0:T(8,128)(2,1)S(1)} %get-tuple-element.94), channel_id=1, source_target_pairs={{4,2},{5,3},{6,0},{7,1},{12,10},{13,11},{14,8},{15,9},{20,18},{21,... | collective-permute-start | bytes 196616 | tf_op jit(solution)/shard_map/ppermute | solution.py:259
  55.6 1.3 %collective-permute-start.19 = (bf16[2,128,128]{2,1,0:T(8,128)(2,1)S(1)}, bf16[2,128,128]{2,1,0:T(8,128)(2,1)S(1)}, u32[]{:S(2)}, u32[]{:S(2)}) collective-permute-start(bf16[2,128,128]{2,1,0:T(8,128)(2,1)S(1)} %get-tuple-element.95), channel_id=1, source_target_pairs={{4,3},{5,2},{6,1},{7,0},{12,11},{13,10},{14,9},{15,8},{20,19},{21,... | collective-permute-start | bytes 196616 | tf_op jit(solution)/shard_map/ppermute | solution.py:259
  58.6 1.4 %shard_map.104 = (bf16[128,4096]{1,0:T(8,128)(2,1)}, bf16[128,4096]{1,0:T(8,128)(2,1)}) custom-call(s32[1]{0:T(128)} %bitcast.pos_ref.refs_0_, bf16[128,1024]{1,0:T(8,128)(2,1)S(1)} %get-tuple-element.60.refs_0_, bf16[128,1024]{1,0:T(8,128)(2,1)S(1)} %get-tuple-element.61.refs_1_, bf16[128,1024]{1,0:T(8,128)(2,1)S(1)} %get-tuple-element.65.refs_2_, ...), custom_call_target="tpu_custom_call" | custom-call | flops 4194304 | bytes 2097152 | tf_op jit(solution)/shard_map/pallas_call | solution.py:302
  60.0 2.0 %collective-permute-done.17.refs_9_ = bf16[2,128,128]{2,1,0:T(8,128)(2,1)S(1)} collective-permute-done((bf16[2,128,128]{2,1,0:T(8,128)(2,1)S(1)}, bf16[2,128,128]{2,1,0:T(8,128)(2,1)S(1)}, u32[]{:S(2)}, u32[]{:S(2)}) %collective-permute-start.17) | collective-permute-done | bytes 65568 | tf_op jit(solution)/shard_map/ppermute | solution.py:259
  62.2 2.7 %collective-permute-done.19.refs_11_ = bf16[2,128,128]{2,1,0:T(8,128)(2,1)S(1)} collective-permute-done((bf16[2,128,128]{2,1,0:T(8,128)(2,1)S(1)}, bf16[2,128,128]{2,1,0:T(8,128)(2,1)S(1)}, u32[]{:S(2)}, u32[]{:S(2)}) %collective-permute-start.19) | collective-permute-done | bytes 65568 | tf_op jit(solution)/shard_map/ppermute | solution.py:259
  (41 shorter events, 8.9 us)
Async XLA Ops:
  1.6 11.8 %collective-permute-start.3 = (bf16[2,128,128]{2,1,0:T(8,128)(2,1)S(1)}, bf16[2,128,128]{2,1,0:T(8,128)(2,1)S(1)}, u32[]{:S(2)}, u32[]{:S(2)}) collective-permute-start(bf16[2,128,128]{2,1,0:T(8,128)(2,1)S(1)} %get-tuple-element.53.refs_0_.refs_6_.refs_3_), channel_id=1, source_target_pairs={{0,4},{1,5},{2,6},{3,7},{8,12},{9,13},{10,14},{11,15},{16,20},{17,... | collective-permute-start | bytes 196616 | tf_op jit(solution)/shard_map/ppermute | solution.py:259
  7.6 12.7 %copy-start.2 = (s32[8,4]{0,1:T(4,128)S(1)}, s32[8,4]{0,1:T(4,128)}, u32[]{:S(2)}) copy-start(s32[8,4]{0,1:T(4,128)} %param.10) | copy-start | bytes 388
  7.6 12.6 %collective-permute-start.4 = (bf16[2,128,128]{2,1,0:T(8,128)(2,1)S(1)}, bf16[2,128,128]{2,1,0:T(8,128)(2,1)S(1)}, u32[]{:S(2)}, u32[]{:S(2)}) collective-permute-start(bf16[2,128,128]{2,1,0:T(8,128)(2,1)S(1)} %get-tuple-element.54.refs_6_.refs_3_), channel_id=1, source_target_pairs={{0,5},{1,4},{2,7},{3,6},{8,13},{9,12},{10,15},{11,14},{16,21},{17,... | collective-permute-start | bytes 196616 | tf_op jit(solution)/shard_map/ppermute | solution.py:259
  9.8 11.2 %collective-permute-start = (bf16[2,128,128]{2,1,0:T(8,128)(2,1)S(1)}, bf16[2,128,128]{2,1,0:T(8,128)(2,1)S(1)}, u32[]{:S(2)}, u32[]{:S(2)}) collective-permute-start(bf16[2,128,128]{2,1,0:T(8,128)(2,1)S(1)} %get-tuple-element.54.refs_6_.refs_3_), channel_id=1, source_target_pairs={{0,1},{1,0},{2,3},{3,2},{4,5},{5,4},{6,7},{7,6},{8,9},{9,8},{10,11... | collective-permute-start | bytes 196616 | tf_op jit(solution)/shard_map/ppermute | solution.py:259
  10.5 10.5 %collective-permute-start.5 = (bf16[2,128,128]{2,1,0:T(8,128)(2,1)S(1)}, bf16[2,128,128]{2,1,0:T(8,128)(2,1)S(1)}, u32[]{:S(2)}, u32[]{:S(2)}) collective-permute-start(bf16[2,128,128]{2,1,0:T(8,128)(2,1)S(1)} %get-tuple-element.55.refs_6_.refs_3_), channel_id=1, source_target_pairs={{0,6},{1,7},{2,4},{3,5},{8,14},{9,15},{10,12},{11,13},{16,22},{17,... | collective-permute-start | bytes 196616 | tf_op jit(solution)/shard_map/ppermute | solution.py:259
  12.8 8.3 %collective-permute-start.1 = (bf16[2,128,128]{2,1,0:T(8,128)(2,1)S(1)}, bf16[2,128,128]{2,1,0:T(8,128)(2,1)S(1)}, u32[]{:S(2)}, u32[]{:S(2)}) collective-permute-start(bf16[2,128,128]{2,1,0:T(8,128)(2,1)S(1)} %get-tuple-element.55.refs_6_.refs_3_), channel_id=1, source_target_pairs={{0,2},{1,3},{2,0},{3,1},{4,6},{5,7},{6,4},{7,5},{8,10},{9,11},{10,... | collective-permute-start | bytes 196616 | tf_op jit(solution)/shard_map/ppermute | solution.py:259
  13.4 8.6 %collective-permute-start.6 = (bf16[2,128,128]{2,1,0:T(8,128)(2,1)S(1)}, bf16[2,128,128]{2,1,0:T(8,128)(2,1)S(1)}, u32[]{:S(2)}, u32[]{:S(2)}) collective-permute-start(bf16[2,128,128]{2,1,0:T(8,128)(2,1)S(1)} %get-tuple-element.56.refs_6_.refs_3_), channel_id=1, source_target_pairs={{0,7},{1,6},{2,5},{3,4},{8,15},{9,14},{10,13},{11,12},{16,23},{17,... | collective-permute-start | bytes 196616 | tf_op jit(solution)/shard_map/ppermute | solution.py:259
  20.2 5.2 %collective-permute-start.2 = (bf16[2,128,128]{2,1,0:T(8,128)(2,1)S(1)}, bf16[2,128,128]{2,1,0:T(8,128)(2,1)S(1)}, u32[]{:S(2)}, u32[]{:S(2)}) collective-permute-start(bf16[2,128,128]{2,1,0:T(8,128)(2,1)S(1)} %get-tuple-element.56.refs_6_.refs_3_), channel_id=1, source_target_pairs={{0,3},{1,2},{2,1},{3,0},{4,7},{5,6},{6,5},{7,4},{8,11},{9,10},{10,... | collective-permute-start | bytes 196616 | tf_op jit(solution)/shard_map/ppermute | solution.py:259
  25.4 7.2 %copy-start = (bf16[128,4096]{1,0:T(8,128)(2,1)S(1)}, bf16[128,4096]{1,0:T(8,128)(2,1)}, u32[]{:S(2)}) copy-start(bf16[128,4096]{1,0:T(8,128)(2,1)} %refs_3_.7) | copy-start | bytes 3145732
  25.4 7.2 %copy-start.1 = (bf16[128,4096]{1,0:T(8,128)(2,1)S(1)}, bf16[128,4096]{1,0:T(8,128)(2,1)}, u32[]{:S(2)}) copy-start(bf16[128,4096]{1,0:T(8,128)(2,1)} %refs_4_.7) | copy-start | bytes 3145732
  25.5 7.0 %collective-permute-start.9 = (bf16[3,2,128,128]{3,2,1,0:T(8,128)(2,1)S(1)}, bf16[3,2,128,128]{3,2,1,0:T(8,128)(2,1)S(1)}, u32[]{:S(2)}, u32[]{:S(2)}) collective-permute-start(bf16[3,2,128,128]{3,2,1,0:T(8,128)(2,1)S(1)} %get-tuple-element.72), channel_id=1, source_target_pairs={{0,3},{1,2},{2,1},{3,0},{4,7},{5,6},{6,5},{7,4},{8,11},{9,10},{10,... | collective-permute-start | bytes 589832 | tf_op jit(solution)/shard_map/ppermute | solution.py:259
  26.2 2.9 %copy-start.3 = (s32[128]{0:T(128)S(1)}, s32[128]{0:T(128)}, u32[]{:S(2)}) copy-start(s32[128]{0:T(128)} %param.11) | copy-start | bytes 1540
  26.2 9.4 %collective-permute-start.8 = (bf16[3,2,128,128]{3,2,1,0:T(8,128)(2,1)S(1)}, bf16[3,2,128,128]{3,2,1,0:T(8,128)(2,1)S(1)}, u32[]{:S(2)}, u32[]{:S(2)}) collective-permute-start(bf16[3,2,128,128]{3,2,1,0:T(8,128)(2,1)S(1)} %get-tuple-element.67), channel_id=1, source_target_pairs={{0,2},{1,3},{2,0},{3,1},{4,6},{5,7},{6,4},{7,5},{8,10},{9,11},{10,... | collective-permute-start | bytes 589832 | tf_op jit(solution)/shard_map/ppermute | solution.py:259
  26.8 11.2 %collective-permute-start.7 = (bf16[3,2,128,128]{3,2,1,0:T(8,128)(2,1)S(1)}, bf16[3,2,128,128]{3,2,1,0:T(8,128)(2,1)S(1)}, u32[]{:S(2)}, u32[]{:S(2)}) collective-permute-start(bf16[3,2,128,128]{3,2,1,0:T(8,128)(2,1)S(1)} %get-tuple-element.62), channel_id=1, source_target_pairs={{0,1},{1,0},{2,3},{3,2},{4,5},{5,4},{6,7},{7,6},{8,9},{9,8},{10,11... | collective-permute-start | bytes 589832 | tf_op jit(solution)/shard_map/ppermute | solution.py:259
  34.6 9.8 %collective-permute-start.12 = (bf16[3,2,128,128]{3,2,1,0:T(8,128)(2,1)S(1)}, bf16[3,2,128,128]{3,2,1,0:T(8,128)(2,1)S(1)}, u32[]{:S(2)}, u32[]{:S(2)}) collective-permute-start(bf16[3,2,128,128]{3,2,1,0:T(8,128)(2,1)S(1)} %get-tuple-element.87), channel_id=1, source_target_pairs={{0,3},{1,2},{2,1},{3,0},{4,7},{5,6},{6,5},{7,4},{8,11},{9,10},{10,... | collective-permute-start | bytes 589832 | tf_op jit(solution)/shard_map/ppermute | solution.py:259
  37.6 6.8 %collective-permute-start.11 = (bf16[3,2,128,128]{3,2,1,0:T(8,128)(2,1)S(1)}, bf16[3,2,128,128]{3,2,1,0:T(8,128)(2,1)S(1)}, u32[]{:S(2)}, u32[]{:S(2)}) collective-permute-start(bf16[3,2,128,128]{3,2,1,0:T(8,128)(2,1)S(1)} %get-tuple-element.86), channel_id=1, source_target_pairs={{0,2},{1,3},{2,0},{3,1},{4,6},{5,7},{6,4},{7,5},{8,10},{9,11},{10,... | collective-permute-start | bytes 589832 | tf_op jit(solution)/shard_map/ppermute | solution.py:259
  40.0 6.2 %collective-permute-start.10 = (bf16[3,2,128,128]{3,2,1,0:T(8,128)(2,1)S(1)}, bf16[3,2,128,128]{3,2,1,0:T(8,128)(2,1)S(1)}, u32[]{:S(2)}, u32[]{:S(2)}) collective-permute-start(bf16[3,2,128,128]{3,2,1,0:T(8,128)(2,1)S(1)} %get-tuple-element.85), channel_id=1, source_target_pairs={{0,1},{1,0},{2,3},{3,2},{4,5},{5,4},{6,7},{7,6},{8,9},{9,8},{10,11... | collective-permute-start | bytes 589832 | tf_op jit(solution)/shard_map/ppermute | solution.py:259
  46.9 7.3 %collective-permute-start.13 = (bf16[2,128,128]{2,1,0:T(8,128)(2,1)S(1)}, bf16[2,128,128]{2,1,0:T(8,128)(2,1)S(1)}, u32[]{:S(2)}, u32[]{:S(2)}) collective-permute-start(bf16[2,128,128]{2,1,0:T(8,128)(2,1)S(1)} %get-tuple-element.89), channel_id=1, source_target_pairs={{0,1},{1,0},{2,3},{3,2},{4,5},{5,4},{6,7},{7,6},{8,9},{9,8},{10,11... | collective-permute-start | bytes 196616 | tf_op jit(solution)/shard_map/ppermute | solution.py:259
  49.4 6.1 %collective-permute-start.14 = (bf16[2,128,128]{2,1,0:T(8,128)(2,1)S(1)}, bf16[2,128,128]{2,1,0:T(8,128)(2,1)S(1)}, u32[]{:S(2)}, u32[]{:S(2)}) collective-permute-start(bf16[2,128,128]{2,1,0:T(8,128)(2,1)S(1)} %get-tuple-element.90), channel_id=1, source_target_pairs={{0,2},{1,3},{2,0},{3,1},{4,6},{5,7},{6,4},{7,5},{8,10},{9,11},{10,... | collective-permute-start | bytes 196616 | tf_op jit(solution)/shard_map/ppermute | solution.py:259
  50.0 10.0 %collective-permute-start.15 = (bf16[2,128,128]{2,1,0:T(8,128)(2,1)S(1)}, bf16[2,128,128]{2,1,0:T(8,128)(2,1)S(1)}, u32[]{:S(2)}, u32[]{:S(2)}) collective-permute-start(bf16[2,128,128]{2,1,0:T(8,128)(2,1)S(1)} %get-tuple-element.91), channel_id=1, source_target_pairs={{0,3},{1,2},{2,1},{3,0},{4,7},{5,6},{6,5},{7,4},{8,11},{9,10},{10,... | collective-permute-start | bytes 196616 | tf_op jit(solution)/shard_map/ppermute | solution.py:259
  51.6 8.4 %collective-permute-start.16 = (bf16[2,128,128]{2,1,0:T(8,128)(2,1)S(1)}, bf16[2,128,128]{2,1,0:T(8,128)(2,1)S(1)}, u32[]{:S(2)}, u32[]{:S(2)}) collective-permute-start(bf16[2,128,128]{2,1,0:T(8,128)(2,1)S(1)} %get-tuple-element.92), channel_id=1, source_target_pairs={{4,0},{5,1},{6,2},{7,3},{12,8},{13,9},{14,10},{15,11},{20,16},{21,... | collective-permute-start | bytes 196616 | tf_op jit(solution)/shard_map/ppermute | solution.py:259
  52.9 9.1 %collective-permute-start.17 = (bf16[2,128,128]{2,1,0:T(8,128)(2,1)S(1)}, bf16[2,128,128]{2,1,0:T(8,128)(2,1)S(1)}, u32[]{:S(2)}, u32[]{:S(2)}) collective-permute-start(bf16[2,128,128]{2,1,0:T(8,128)(2,1)S(1)} %get-tuple-element.93), channel_id=1, source_target_pairs={{4,1},{5,0},{6,3},{7,2},{12,9},{13,8},{14,11},{15,10},{20,17},{21,... | collective-permute-start | bytes 196616 | tf_op jit(solution)/shard_map/ppermute | solution.py:259
  54.2 8.0 %collective-permute-start.18 = (bf16[2,128,128]{2,1,0:T(8,128)(2,1)S(1)}, bf16[2,128,128]{2,1,0:T(8,128)(2,1)S(1)}, u32[]{:S(2)}, u32[]{:S(2)}) collective-permute-start(bf16[2,128,128]{2,1,0:T(8,128)(2,1)S(1)} %get-tuple-element.94), channel_id=1, source_target_pairs={{4,2},{5,3},{6,0},{7,1},{12,10},{13,11},{14,8},{15,9},{20,18},{21,... | collective-permute-start | bytes 196616 | tf_op jit(solution)/shard_map/ppermute | solution.py:259
  55.6 9.4 %collective-permute-start.19 = (bf16[2,128,128]{2,1,0:T(8,128)(2,1)S(1)}, bf16[2,128,128]{2,1,0:T(8,128)(2,1)S(1)}, u32[]{:S(2)}, u32[]{:S(2)}) collective-permute-start(bf16[2,128,128]{2,1,0:T(8,128)(2,1)S(1)} %get-tuple-element.95), channel_id=1, source_target_pairs={{4,3},{5,2},{6,1},{7,0},{12,11},{13,10},{14,9},{15,8},{20,19},{21,... | collective-permute-start | bytes 196616 | tf_op jit(solution)/shard_map/ppermute | solution.py:259

commit v4 on v3

--- a/solution.py
+++ b/solution.py
@@ -36,6 +36,11 @@
 
 def stack_slots(far_ref, own_ref, part):
     return jnp.concatenate([far_ref[e, part] for e in range(FAR_SLOTS)] + [own_ref[part]], 0)
+
+
+def stack_heads(ref, head, mask=None):
+    parts = [ref[:, head_columns(head * HEADS_PER_KEY + i)] for i in range(HEADS_PER_KEY)]
+    return jnp.concatenate(parts if mask is None else [part * mask for part in parts], 0)
 
 
 def head_columns(head):
@@ -92,14 +97,12 @@
 
 def attend_kernel(turn, rows, *refs):
     (pos_ref, hide_ref, mask_ref, q_ref, go_ref, far_ref, own_ref) = refs[:7]
-    weights_ref, grad_score_ref, far_grad_ref, own_grad_ref = refs[7:]
+    weights_ref, grad_score_ref, far_grad_ref = refs[7:]
     head = lax.rem(pos_ref[0], GROUP) ^ turn
     far_rows = FAR_SLOTS * rows
     mask = mask_ref[...]
-    blocks = [head_columns(head * HEADS_PER_KEY + i) for i in range(HEADS_PER_KEY)]
     kk, vv = stack_slots(far_ref, own_ref, 0), stack_slots(far_ref, own_ref, 1)
-    qm = jnp.concatenate([q_ref[:, cols] for cols in blocks], 0)
-    gm = jnp.concatenate([go_ref[:, cols] * mask for cols in blocks], 0)
+    qm, gm = stack_heads(q_ref, head), stack_heads(go_ref, head, mask)
     key = lax.broadcasted_iota(jnp.int32, (rows, rows), 0)
     token = lax.broadcasted_iota(jnp.int32, (rows, rows), 1)
     causal = jnp.where(key <= token, 0.0, MASKED)
@@ -122,18 +125,22 @@
     grad_score = (weights * (grad_prob - delta)).astype(jnp.bfloat16)
     weights_ref[...] = rounded
     grad_score_ref[...] = grad_score
-    grad_key = dot(grad_score, qm) * SCALING
-    grad_value = dot(rounded, gm)
+    grad_key = dot(grad_score[:far_rows], qm) * SCALING
+    grad_value = dot(rounded[:far_rows], gm)
     for e in range(FAR_SLOTS):
         s = slice(e * rows, (e + 1) * rows)
         far_grad_ref[e, 0] = grad_key[s].astype(jnp.bfloat16)
         far_grad_ref[e, 1] = grad_value[s].astype(jnp.bfloat16)
-    own_grad_ref[0] = grad_key[far_rows:]
-    own_grad_ref[1] = grad_value[far_rows:]
-
-
-def output_kernel(rows, *refs):
-    weights_ref, grad_score_ref, far_ref, own_ref, attn_ref, gq_ref = refs
+
+
+def output_kernel(turn, rows, *refs):
+    pos_ref, mask_ref, q_ref, go_ref, weights_ref, grad_score_ref, far_ref, own_ref = refs[:8]
+    attn_ref, gq_ref, own_grad_ref = refs[8:]
+    head = lax.rem(pos_ref[0], GROUP) ^ turn
+    own_rows = pl.ds(FAR_SLOTS * rows, rows)
+    own_grad_ref[0] = dot(grad_score_ref[own_rows, :], stack_heads(q_ref, head)) * SCALING
+    gm = stack_heads(go_ref, head, mask_ref[...])
+    own_grad_ref[1] = dot(weights_ref[own_rows, :], gm)
     kk, vv = stack_slots(far_ref, own_ref, 0), stack_slots(far_ref, own_ref, 1)
     attended = dot(vv, weights_ref[...], FIRST)
     grad_query = dot(kk, grad_score_ref[...], FIRST) * SCALING
@@ -152,29 +159,24 @@
     return pl.pallas_call(
         functools.partial(attend_kernel, turn, rows),
         in_specs=[SMEM_SPEC] + [VMEM_SPEC] * 6,
-        out_specs=[VMEM_SPEC] * 4,
-        out_shape=[
-            square,
-            square,
-            jax.ShapeDtypeStruct(far.shape, jnp.bfloat16),
-            jax.ShapeDtypeStruct(own.shape, jnp.float32),
-        ],
+        out_specs=[VMEM_SPEC] * 3,
+        out_shape=[square, square, jax.ShapeDtypeStruct(far.shape, jnp.bfloat16)],
         cost_estimate=cost(8 * pairs * HEAD_WIDTH, 8 * pairs),
         compiler_params=pltpu.CompilerParams(vmem_limit_bytes=VMEM_LIMIT),
     )(pos, hide, mask, queries, grad_out, far, own)
 
 
-def output(weights, grad_score, far, own):
+def output(turn, pos, mask, queries, grad_out, weights, grad_score, far, own):
     rows = own.shape[1]
     block = jax.ShapeDtypeStruct((rows, HEADS_PER_KEY * HEAD_WIDTH), jnp.bfloat16)
     return pl.pallas_call(
-        functools.partial(output_kernel, rows),
-        in_specs=[VMEM_SPEC] * 4,
-        out_specs=[VMEM_SPEC] * 2,
-        out_shape=[block, block],
-        cost_estimate=cost(4 * weights.size * HEAD_WIDTH, 4 * weights.size),
+        functools.partial(output_kernel, turn, rows),
+        in_specs=[SMEM_SPEC] + [VMEM_SPEC] * 7,
+        out_specs=[VMEM_SPEC] * 3,
+        out_shape=[block, block, jax.ShapeDtypeStruct(own.shape, jnp.float32)],
+        cost_estimate=cost(5 * weights.size * HEAD_WIDTH, 4 * weights.size),
         compiler_params=pltpu.CompilerParams(vmem_limit_bytes=VMEM_LIMIT),
-    )(weights, grad_score, far, own)
+    )(pos, mask, queries, grad_out, weights, grad_score, far, own)
 
 
 def store_kernel(pos_ref, *refs):
@@ -194,20 +196,28 @@
         copy.wait()
 
 
-def reduce_kernel(count, add_ref, *refs):
-    terms, outs, acc = refs[:GROUP], refs[GROUP : GROUP + count], refs[-1]
+def partial_kernel(add_ref, *refs):
+    terms, acc = refs[:-1], refs[-1]
     add = add_ref[...]
     acc[...] = jnp.zeros_like(acc)
-    for t in range(GROUP):
+    for t, term in enumerate(terms):
         for e in range(FAR_SLOTS):
             index = add[t * FAR_SLOTS + e, 0]
 
             @pl.when(index >= 0)
-            def _(t=t, e=e, index=index):
-                acc[index] += terms[t][e].astype(jnp.float32)
-
-    for i in range(count):
-        outs[i][...] = acc[i].astype(jnp.bfloat16)
+            def _(term=term, e=e, index=index):
+                acc[index] += term[e].astype(jnp.float32)
+
+
+def total_kernel(begin, add_ref, acc_ref, last_ref, *outs):
+    add = add_ref[...]
+    row = (GROUP - 1) * FAR_SLOTS
+    for i, out in enumerate(outs):
+        total = acc_ref[begin + i]
+        for e in range(FAR_SLOTS):
+            hit = add[row + e, 0] == begin + i
+            total = total + jnp.where(hit, last_ref[e].astype(jnp.float32), 0.0)
+        out[...] = total.astype(jnp.bfloat16)
 
 
 def finish_kernel(pos_ref, *refs):
@@ -291,10 +301,13 @@
 
     blocks, far_grads, own_grads = [], [], []
     for t in range(GROUP):
-        weights, grad_score, far_grad, own_grad = attend(
+        weights, grad_score, far_grad = attend(
             t, pos, hide, mask, queries, grad_out, far[t], packed[t]
         )
-        blocks += output(weights, grad_score, far[t], packed[t])
+        attended, grad_query, own_grad = output(
+            t, pos, mask, queries, grad_out, weights, grad_score, far[t], packed[t]
+        )
+        blocks += [attended, grad_query]
         far_grads.append(far_grad)
         own_grads.append(own_grad)
     far_grads = near_sends(far_grads)
@@ -304,13 +317,20 @@
         [wide] * 2, 32 * piece_bytes, [pltpu.SemaphoreType.DMA((2 * GROUP,))],
     )(pos, *blocks)
 
-    sums = small_call(
-        functools.partial(reduce_kernel, size),
-        [VMEM_SPEC] * (1 + GROUP), [VMEM_SPEC] * size, [piece] * size,
-        (size + 12) * piece_bytes, [pltpu.VMEM((size,) + piece.shape, jnp.float32)],
-    )(add, *far_grads)
-    far_sums = far_sends(sums, -1)
-    near_sums = near_sends(sums[:GROUP])
+    (acc,) = small_call(
+        partial_kernel, [VMEM_SPEC] * GROUP, [VMEM_SPEC],
+        [jax.ShapeDtypeStruct((size,) + piece.shape, jnp.float32)], (2 * size + 9) * piece_bytes,
+    )(add, *far_grads[:-1])
+
+    def total(begin, count):
+        return small_call(
+            functools.partial(total_kernel, begin), [VMEM_SPEC] * 3,
+            [VMEM_SPEC] * count, [piece] * count, (3 * count + 3) * piece_bytes,
+        )(add, acc, far_grads[-1])
+
+    far_sums = total(GROUP, size - GROUP)
+    far_sums = far_sends([None] * GROUP + list(far_sums), -1)
+    near_sums = near_sends(total(0, GROUP))
 
     grad = jax.ShapeDtypeStruct(keys.shape, jnp.bfloat16)
     grad_keys, grad_values = small_call(

time: 66.1 us -> 63.1 us (0.955)
  waiting for transfers between devices: 14.6 us -> 12.2 us
  starting transfers between devices: 35.1 us -> 34.1 us
    ppermute x20, waiting for transfers between devices: 14.6 us -> 12.2 us  [send(): return lax.ppermute(x, 'ctx', pairs)]
    ppermute x20, starting transfers between devices: 35.1 us -> 34.1 us  [send(): return lax.ppermute(x, 'ctx', pairs)]
    pallas_call x5 -> x7, Pallas kernels: 2.97 us -> 3.9 us  [the longest x4 3.05 us: output(): pl.pallas_call(functools.partial(output_kernel, turn, rows), in_specs=[SM...]
  transfers between devices with their start and end apart: 20 -> 20, of which waited for: 7 -> 7; matrix products, arithmetic and copies ran while one was open for 0% -> 0% of each run, Pallas kernels for 19% -> 21%
where the time goes in v4:
time: 63.1 us; the launch traced here: 62.7 us
  starting transfers between devices  34.1 us (54%)
  Pallas kernels  15.3 us (24%)
  waiting for transfers between devices  12.2 us (19%)
  between operations  0.95 us (2%)
    ppermute x20, starting transfers between devices, send(): return lax.ppermute(x, 'ctx', pairs)  34.1 us
    ppermute x20, waiting for transfers between devices, send(): return lax.ppermute(x, 'ctx', pairs)  12.2 us
    pallas_call x4, Pallas kernels, attend(): pl.pallas_call(functools.partial(attend_kernel, turn, rows), in_specs=[SM...  7.48 us
    pallas_call x4, Pallas kernels, output(): pl.pallas_call(functools.partial(output_kernel, turn, rows), in_specs=[SM...  3.05 us
    pallas_call x1, Pallas kernels, on_device(): small_call(store_kernel, [SMEM_SPEC] + [VMEM_SPEC] * (2 * GROUP), [HBM_SP...  1.38 us
  transfers between devices with their start and end apart: 20, of which 7 were waited for; matrix products, arithmetic and copies ran while one was open for 0% of the time, Pallas kernels for 21%

profile of v4, /device:TPU:0, one launch (start us, length us, event | category | flops | bytes accessed | tf_op | source)
XLA Modules:
  0.0 62.7 jit_solution(11706503453239062641)
XLA Ops:
  0.6 1.0 %shard_map.94 = (bf16[2,128,128]{2,1,0:T(8,128)(2,1)S(1)}, bf16[2,128,128]{2,1,0:T(8,128)(2,1)S(1)}, bf16[2,128,128]{2,1,0:T(8,128)(2,1)S(1)}, bf16[2,128,128]{2,1,0:T(8,128)(2,1)S(1)}) custom-call(s32[1]{0:T(128)} %bitcast.pos_ref.refs_0_, bf16[128,512]{1,0:T(8,128)(2,1)} %k_ref.1, bf16[128,512]{1,0:T(8,128)(2,1)} %v_ref.1), custom_call_target="tpu_custom_call" | custom-call | flops 1048576 | bytes 524288 | tf_op jit(solution)/shard_map/pallas_call | solution.py:281
  1.6 6.0 %collective-permute-start.3 = (bf16[2,128,128]{2,1,0:T(8,128)(2,1)S(1)}, bf16[2,128,128]{2,1,0:T(8,128)(2,1)S(1)}, u32[]{:S(2)}, u32[]{:S(2)}) collective-permute-start(bf16[2,128,128]{2,1,0:T(8,128)(2,1)S(1)} %get-tuple-element.53.refs_0_.refs_6_.refs_7_), channel_id=1, source_target_pairs={{0,4},{1,5},{2,6},{3,7},{8,12},{9,13},{10,14},{11,15},{16,20},{17,... | collective-permute-start | bytes 196616 | tf_op jit(solution)/shard_map/ppermute | solution.py:269
  7.6 2.2 %collective-permute-start.4 = (bf16[2,128,128]{2,1,0:T(8,128)(2,1)S(1)}, bf16[2,128,128]{2,1,0:T(8,128)(2,1)S(1)}, u32[]{:S(2)}, u32[]{:S(2)}) collective-permute-start(bf16[2,128,128]{2,1,0:T(8,128)(2,1)S(1)} %get-tuple-element.54.refs_6_.refs_7_), channel_id=1, source_target_pairs={{0,5},{1,4},{2,7},{3,6},{8,13},{9,12},{10,15},{11,14},{16,21},{17,... | collective-permute-start | bytes 196616 | tf_op jit(solution)/shard_map/ppermute | solution.py:269
  10.5 2.3 %collective-permute-start.5 = (bf16[2,128,128]{2,1,0:T(8,128)(2,1)S(1)}, bf16[2,128,128]{2,1,0:T(8,128)(2,1)S(1)}, u32[]{:S(2)}, u32[]{:S(2)}) collective-permute-start(bf16[2,128,128]{2,1,0:T(8,128)(2,1)S(1)} %get-tuple-element.55.refs_6_.refs_7_), channel_id=1, source_target_pairs={{0,6},{1,7},{2,4},{3,5},{8,14},{9,15},{10,12},{11,13},{16,22},{17,... | collective-permute-start | bytes 196616 | tf_op jit(solution)/shard_map/ppermute | solution.py:269
  13.4 6.7 %collective-permute-start.6 = (bf16[2,128,128]{2,1,0:T(8,128)(2,1)S(1)}, bf16[2,128,128]{2,1,0:T(8,128)(2,1)S(1)}, u32[]{:S(2)}, u32[]{:S(2)}) collective-permute-start(bf16[2,128,128]{2,1,0:T(8,128)(2,1)S(1)} %get-tuple-element.56.refs_6_.refs_7_), channel_id=1, source_target_pairs={{0,7},{1,6},{2,5},{3,4},{8,15},{9,14},{10,13},{11,12},{16,23},{17,... | collective-permute-start | bytes 196616 | tf_op jit(solution)/shard_map/ppermute | solution.py:269
  21.0 1.0 %collective-permute-done.6.refs_7_ = bf16[2,128,128]{2,1,0:T(8,128)(2,1)S(1)} collective-permute-done((bf16[2,128,128]{2,1,0:T(8,128)(2,1)S(1)}, bf16[2,128,128]{2,1,0:T(8,128)(2,1)S(1)}, u32[]{:S(2)}, u32[]{:S(2)}) %collective-permute-start.6) | collective-permute-done | bytes 65568 | tf_op jit(solution)/shard_map/ppermute | solution.py:269
  22.0 4.1 %collective-permute-done.2.refs_3_ = bf16[2,128,128]{2,1,0:T(8,128)(2,1)S(1)} collective-permute-done((bf16[2,128,128]{2,1,0:T(8,128)(2,1)S(1)}, bf16[2,128,128]{2,1,0:T(8,128)(2,1)S(1)}, u32[]{:S(2)}, u32[]{:S(2)}) %collective-permute-start.2) | collective-permute-done | bytes 65568 | tf_op jit(solution)/shard_map/ppermute | solution.py:269
  26.7 3.0 %collective-permute-start.9 = (bf16[3,2,128,128]{3,2,1,0:T(8,128)(2,1)S(1)}, bf16[3,2,128,128]{3,2,1,0:T(8,128)(2,1)S(1)}, u32[]{:S(2)}, u32[]{:S(2)}) collective-permute-start(bf16[3,2,128,128]{3,2,1,0:T(8,128)(2,1)S(1)} %get-tuple-element.72), channel_id=1, source_target_pairs={{0,3},{1,2},{2,1},{3,0},{4,7},{5,6},{6,5},{7,4},{8,11},{9,10},{10,... | collective-permute-start | bytes 589832 | tf_op jit(solution)/shard_map/ppermute | solution.py:269
  29.8 2.4 %collective-permute-done.8.refs_5_.refs_6_ = bf16[3,2,128,128]{3,2,1,0:T(8,128)(2,1)S(1)} collective-permute-done((bf16[3,2,128,128]{3,2,1,0:T(8,128)(2,1)S(1)}, bf16[3,2,128,128]{3,2,1,0:T(8,128)(2,1)S(1)}, u32[]{:S(2)}, u32[]{:S(2)}) %collective-permute-start.8) | collective-permute-done | bytes 196640 | tf_op jit(solution)/shard_map/ppermute | solution.py:269
  32.3 1.9 %shard_map.100 = (bf16[512,1024]{1,0:T(8,128)(2,1)S(1)}, bf16[512,1024]{1,0:T(8,128)(2,1)S(1)}, bf16[3,2,128,128]{3,2,1,0:T(8,128)(2,1)S(1)}) custom-call(s32[1]{0:T(128)} %bitcast.pos_ref.refs_0_, f32[8,128]{1,0:T(8,128)S(1)} %get-tuple-element.51.refs_1_, bf16[128,128]{1,0:T(8,128)(2,1)S(1)} %broadcast_in_dim.2.refs_2_.refs_1_, ...), custom_call_target="tpu_custom_call" | custom-call | flops 536870912 | bytes 4194304 | tf_op jit(solution)/shard_map/pallas_call | solution.py:159
  34.6 1.9 %shard_map.98 = (bf16[512,1024]{1,0:T(8,128)(2,1)S(1)}, bf16[512,1024]{1,0:T(8,128)(2,1)S(1)}, bf16[3,2,128,128]{3,2,1,0:T(8,128)(2,1)S(1)}) custom-call(s32[1]{0:T(128)} %bitcast.pos_ref.refs_0_, f32[8,128]{1,0:T(8,128)S(1)} %get-tuple-element.51.refs_1_, bf16[128,128]{1,0:T(8,128)(2,1)S(1)} %broadcast_in_dim.2.refs_2_.refs_1_, ...), custom_call_target="tpu_custom_call" | custom-call | flops 536870912 | bytes 4194304 | tf_op jit(solution)/shard_map/pallas_call | solution.py:159
  36.9 1.9 %shard_map.102 = (bf16[512,1024]{1,0:T(8,128)(2,1)S(1)}, bf16[512,1024]{1,0:T(8,128)(2,1)S(1)}, bf16[3,2,128,128]{3,2,1,0:T(8,128)(2,1)S(1)}) custom-call(s32[1]{0:T(128)} %bitcast.pos_ref.refs_0_, f32[8,128]{1,0:T(8,128)S(1)} %get-tuple-element.51.refs_1_, bf16[128,128]{1,0:T(8,128)(2,1)S(1)} %broadcast_in_dim.2.refs_2_.refs_1_, ...), custom_call_target="tpu_custom_call" | custom-call | flops 536870912 | bytes 4194304 | tf_op jit(solution)/shard_map/pallas_call | solution.py:159
  38.8 2.8 %collective-permute-start.12 = (bf16[3,2,128,128]{3,2,1,0:T(8,128)(2,1)S(1)}, bf16[3,2,128,128]{3,2,1,0:T(8,128)(2,1)S(1)}, u32[]{:S(2)}, u32[]{:S(2)}) collective-permute-start(bf16[3,2,128,128]{3,2,1,0:T(8,128)(2,1)S(1)} %get-tuple-element.87), channel_id=1, source_target_pairs={{0,3},{1,2},{2,1},{3,0},{4,7},{5,6},{6,5},{7,4},{8,11},{9,10},{10,... | collective-permute-start | bytes 589832 | tf_op jit(solution)/shard_map/ppermute | solution.py:269
  41.6 1.9 %shard_map.96 = (bf16[512,1024]{1,0:T(8,128)(2,1)S(1)}, bf16[512,1024]{1,0:T(8,128)(2,1)S(1)}, bf16[3,2,128,128]{3,2,1,0:T(8,128)(2,1)S(1)}) custom-call(s32[1]{0:T(128)} %bitcast.pos_ref.refs_0_, f32[8,128]{1,0:T(8,128)S(1)} %get-tuple-element.51.refs_1_, bf16[128,128]{1,0:T(8,128)(2,1)S(1)} %broadcast_in_dim.2.refs_2_.refs_1_, ...), custom_call_target="tpu_custom_call" | custom-call | flops 536870912 | bytes 4194304 | tf_op jit(solution)/shard_map/pallas_call | solution.py:159
  43.9 1.5 %collective-permute-done.12.last_ref = bf16[3,2,128,128]{3,2,1,0:T(8,128)(2,1)S(1)} collective-permute-done((bf16[3,2,128,128]{3,2,1,0:T(8,128)(2,1)S(1)}, bf16[3,2,128,128]{3,2,1,0:T(8,128)(2,1)S(1)}, u32[]{:S(2)}, u32[]{:S(2)}) %collective-permute-start.12) | collective-permute-done | bytes 196640 | tf_op jit(solution)/shard_map/ppermute | solution.py:269
  45.6 1.3 %collective-permute-start.16 = (bf16[2,128,128]{2,1,0:T(8,128)(2,1)S(1)}, bf16[2,128,128]{2,1,0:T(8,128)(2,1)S(1)}, u32[]{:S(2)}, u32[]{:S(2)}) collective-permute-start(bf16[2,128,128]{2,1,0:T(8,128)(2,1)S(1)} %get-tuple-element.92), channel_id=1, source_target_pairs={{4,0},{5,1},{6,2},{7,3},{12,8},{13,9},{14,10},{15,11},{20,16},{21,... | collective-permute-start | bytes 196616 | tf_op jit(solution)/shard_map/ppermute | solution.py:269
  46.9 1.3 %collective-permute-start.17 = (bf16[2,128,128]{2,1,0:T(8,128)(2,1)S(1)}, bf16[2,128,128]{2,1,0:T(8,128)(2,1)S(1)}, u32[]{:S(2)}, u32[]{:S(2)}) collective-permute-start(bf16[2,128,128]{2,1,0:T(8,128)(2,1)S(1)} %get-tuple-element.93), channel_id=1, source_target_pairs={{4,1},{5,0},{6,3},{7,2},{12,9},{13,8},{14,11},{15,10},{20,17},{21,... | collective-permute-start | bytes 196616 | tf_op jit(solution)/shard_map/ppermute | solution.py:269
  49.0 1.3 %collective-permute-start.18 = (bf16[2,128,128]{2,1,0:T(8,128)(2,1)S(1)}, bf16[2,128,128]{2,1,0:T(8,128)(2,1)S(1)}, u32[]{:S(2)}, u32[]{:S(2)}) collective-permute-start(bf16[2,128,128]{2,1,0:T(8,128)(2,1)S(1)} %get-tuple-element.94), channel_id=1, source_target_pairs={{4,2},{5,3},{6,0},{7,1},{12,10},{13,11},{14,8},{15,9},{20,18},{21,... | collective-permute-start | bytes 196616 | tf_op jit(solution)/shard_map/ppermute | solution.py:269
  50.3 1.5 %collective-permute-start.19 = (bf16[2,128,128]{2,1,0:T(8,128)(2,1)S(1)}, bf16[2,128,128]{2,1,0:T(8,128)(2,1)S(1)}, u32[]{:S(2)}, u32[]{:S(2)}) collective-permute-start(bf16[2,128,128]{2,1,0:T(8,128)(2,1)S(1)} %get-tuple-element.95), channel_id=1, source_target_pairs={{4,3},{5,2},{6,1},{7,0},{12,11},{13,10},{14,9},{15,8},{20,19},{21,... | collective-permute-start | bytes 196616 | tf_op jit(solution)/shard_map/ppermute | solution.py:269
  52.0 1.7 %collective-permute-start.13 = (bf16[2,128,128]{2,1,0:T(8,128)(2,1)S(1)}, bf16[2,128,128]{2,1,0:T(8,128)(2,1)S(1)}, u32[]{:S(2)}, u32[]{:S(2)}) collective-permute-start(bf16[2,128,128]{2,1,0:T(8,128)(2,1)S(1)} %get-tuple-element.89), channel_id=1, source_target_pairs={{0,1},{1,0},{2,3},{3,2},{4,5},{5,4},{6,7},{7,6},{8,9},{9,8},{10,11... | collective-permute-start | bytes 196616 | tf_op jit(solution)/shard_map/ppermute | solution.py:269
  53.7 1.4 %collective-permute-done.16.refs_8_ = bf16[2,128,128]{2,1,0:T(8,128)(2,1)S(1)} collective-permute-done((bf16[2,128,128]{2,1,0:T(8,128)(2,1)S(1)}, bf16[2,128,128]{2,1,0:T(8,128)(2,1)S(1)}, u32[]{:S(2)}, u32[]{:S(2)}) %collective-permute-start.16) | collective-permute-done | bytes 65568 | tf_op jit(solution)/shard_map/ppermute | solution.py:269
  55.4 1.4 %collective-permute-done.17.refs_9_ = bf16[2,128,128]{2,1,0:T(8,128)(2,1)S(1)} collective-permute-done((bf16[2,128,128]{2,1,0:T(8,128)(2,1)S(1)}, bf16[2,128,128]{2,1,0:T(8,128)(2,1)S(1)}, u32[]{:S(2)}, u32[]{:S(2)}) %collective-permute-start.17) | collective-permute-done | bytes 65568 | tf_op jit(solution)/shard_map/ppermute | solution.py:269
  56.7 1.0 %collective-permute-start.15 = (bf16[2,128,128]{2,1,0:T(8,128)(2,1)S(1)}, bf16[2,128,128]{2,1,0:T(8,128)(2,1)S(1)}, u32[]{:S(2)}, u32[]{:S(2)}) collective-permute-start(bf16[2,128,128]{2,1,0:T(8,128)(2,1)S(1)} %get-tuple-element.91), channel_id=1, source_target_pairs={{0,3},{1,2},{2,1},{3,0},{4,7},{5,6},{6,5},{7,4},{8,11},{9,10},{10,... | collective-permute-start | bytes 196616 | tf_op jit(solution)/shard_map/ppermute | solution.py:269
  60.0 1.4 %shard_map.104 = (bf16[128,4096]{1,0:T(8,128)(2,1)}, bf16[128,4096]{1,0:T(8,128)(2,1)}) custom-call(s32[1]{0:T(128)} %bitcast.pos_ref.refs_0_, bf16[128,1024]{1,0:T(8,128)(2,1)S(1)} %get-tuple-element.60.refs_0_, bf16[128,1024]{1,0:T(8,128)(2,1)S(1)} %get-tuple-element.61.refs_1_, bf16[128,1024]{1,0:T(8,128)(2,1)S(1)} %get-tuple-element.65.refs_2_, ...), custom_call_target="tpu_custom_call" | custom-call | flops 4194304 | bytes 2097152 | tf_op jit(solution)/shard_map/pallas_call | solution.py:315
  (43 shorter events, 9.1 us)
Async XLA Ops:
  1.6 11.8 %collective-permute-start.3 = (bf16[2,128,128]{2,1,0:T(8,128)(2,1)S(1)}, bf16[2,128,128]{2,1,0:T(8,128)(2,1)S(1)}, u32[]{:S(2)}, u32[]{:S(2)}) collective-permute-start(bf16[2,128,128]{2,1,0:T(8,128)(2,1)S(1)} %get-tuple-element.53.refs_0_.refs_6_.refs_7_), channel_id=1, source_target_pairs={{0,4},{1,5},{2,6},{3,7},{8,12},{9,13},{10,14},{11,15},{16,20},{17,... | collective-permute-start | bytes 196616 | tf_op jit(solution)/shard_map/ppermute | solution.py:269
  7.6 12.7 %copy-start.2 = (s32[8,4]{0,1:T(4,128)S(1)}, s32[8,4]{0,1:T(4,128)}, u32[]{:S(2)}) copy-start(s32[8,4]{0,1:T(4,128)} %param.10) | copy-start | bytes 388
  7.6 12.6 %collective-permute-start.4 = (bf16[2,128,128]{2,1,0:T(8,128)(2,1)S(1)}, bf16[2,128,128]{2,1,0:T(8,128)(2,1)S(1)}, u32[]{:S(2)}, u32[]{:S(2)}) collective-permute-start(bf16[2,128,128]{2,1,0:T(8,128)(2,1)S(1)} %get-tuple-element.54.refs_6_.refs_7_), channel_id=1, source_target_pairs={{0,5},{1,4},{2,7},{3,6},{8,13},{9,12},{10,15},{11,14},{16,21},{17,... | collective-permute-start | bytes 196616 | tf_op jit(solution)/shard_map/ppermute | solution.py:269
  9.8 11.2 %collective-permute-start = (bf16[2,128,128]{2,1,0:T(8,128)(2,1)S(1)}, bf16[2,128,128]{2,1,0:T(8,128)(2,1)S(1)}, u32[]{:S(2)}, u32[]{:S(2)}) collective-permute-start(bf16[2,128,128]{2,1,0:T(8,128)(2,1)S(1)} %get-tuple-element.54.refs_6_.refs_7_), channel_id=1, source_target_pairs={{0,1},{1,0},{2,3},{3,2},{4,5},{5,4},{6,7},{7,6},{8,9},{9,8},{10,11... | collective-permute-start | bytes 196616 | tf_op jit(solution)/shard_map/ppermute | solution.py:269
  10.5 10.5 %collective-permute-start.5 = (bf16[2,128,128]{2,1,0:T(8,128)(2,1)S(1)}, bf16[2,128,128]{2,1,0:T(8,128)(2,1)S(1)}, u32[]{:S(2)}, u32[]{:S(2)}) collective-permute-start(bf16[2,128,128]{2,1,0:T(8,128)(2,1)S(1)} %get-tuple-element.55.refs_6_.refs_7_), channel_id=1, source_target_pairs={{0,6},{1,7},{2,4},{3,5},{8,14},{9,15},{10,12},{11,13},{16,22},{17,... | collective-permute-start | bytes 196616 | tf_op jit(solution)/shard_map/ppermute | solution.py:269
  12.8 8.3 %collective-permute-start.1 = (bf16[2,128,128]{2,1,0:T(8,128)(2,1)S(1)}, bf16[2,128,128]{2,1,0:T(8,128)(2,1)S(1)}, u32[]{:S(2)}, u32[]{:S(2)}) collective-permute-start(bf16[2,128,128]{2,1,0:T(8,128)(2,1)S(1)} %get-tuple-element.55.refs_6_.refs_7_), channel_id=1, source_target_pairs={{0,2},{1,3},{2,0},{3,1},{4,6},{5,7},{6,4},{7,5},{8,10},{9,11},{10,... | collective-permute-start | bytes 196616 | tf_op jit(solution)/shard_map/ppermute | solution.py:269
  13.4 8.6 %collective-permute-start.6 = (bf16[2,128,128]{2,1,0:T(8,128)(2,1)S(1)}, bf16[2,128,128]{2,1,0:T(8,128)(2,1)S(1)}, u32[]{:S(2)}, u32[]{:S(2)}) collective-permute-start(bf16[2,128,128]{2,1,0:T(8,128)(2,1)S(1)} %get-tuple-element.56.refs_6_.refs_7_), channel_id=1, source_target_pairs={{0,7},{1,6},{2,5},{3,4},{8,15},{9,14},{10,13},{11,12},{16,23},{17,... | collective-permute-start | bytes 196616 | tf_op jit(solution)/shard_map/ppermute | solution.py:269
  20.2 5.9 %collective-permute-start.2 = (bf16[2,128,128]{2,1,0:T(8,128)(2,1)S(1)}, bf16[2,128,128]{2,1,0:T(8,128)(2,1)S(1)}, u32[]{:S(2)}, u32[]{:S(2)}) collective-permute-start(bf16[2,128,128]{2,1,0:T(8,128)(2,1)S(1)} %get-tuple-element.56.refs_6_.refs_7_), channel_id=1, source_target_pairs={{0,3},{1,2},{2,1},{3,0},{4,7},{5,6},{6,5},{7,4},{8,11},{9,10},{10,... | collective-permute-start | bytes 196616 | tf_op jit(solution)/shard_map/ppermute | solution.py:269
  26.1 6.2 %copy-start = (bf16[128,4096]{1,0:T(8,128)(2,1)S(1)}, bf16[128,4096]{1,0:T(8,128)(2,1)}, u32[]{:S(2)}) copy-start(bf16[128,4096]{1,0:T(8,128)(2,1)} %refs_2_.7) | copy-start | bytes 3145732
  26.1 6.2 %copy-start.1 = (bf16[128,4096]{1,0:T(8,128)(2,1)S(1)}, bf16[128,4096]{1,0:T(8,128)(2,1)}, u32[]{:S(2)}) copy-start(bf16[128,4096]{1,0:T(8,128)(2,1)} %refs_3_.15) | copy-start | bytes 3145732
  26.2 6.0 %collective-permute-start.8 = (bf16[3,2,128,128]{3,2,1,0:T(8,128)(2,1)S(1)}, bf16[3,2,128,128]{3,2,1,0:T(8,128)(2,1)S(1)}, u32[]{:S(2)}, u32[]{:S(2)}) collective-permute-start(bf16[3,2,128,128]{3,2,1,0:T(8,128)(2,1)S(1)} %get-tuple-element.67), channel_id=1, source_target_pairs={{0,2},{1,3},{2,0},{3,1},{4,6},{5,7},{6,4},{7,5},{8,10},{9,11},{10,... | collective-permute-start | bytes 589832 | tf_op jit(solution)/shard_map/ppermute | solution.py:269
  26.3 3.5 %copy-start.3 = (s32[128]{0:T(128)S(1)}, s32[128]{0:T(128)}, u32[]{:S(2)}) copy-start(s32[128]{0:T(128)} %param.11) | copy-start | bytes 1540
  26.3 8.3 %collective-permute-start.7 = (bf16[3,2,128,128]{3,2,1,0:T(8,128)(2,1)S(1)}, bf16[3,2,128,128]{3,2,1,0:T(8,128)(2,1)S(1)}, u32[]{:S(2)}, u32[]{:S(2)}) collective-permute-start(bf16[3,2,128,128]{3,2,1,0:T(8,128)(2,1)S(1)} %get-tuple-element.62), channel_id=1, source_target_pairs={{0,1},{1,0},{2,3},{3,2},{4,5},{5,4},{6,7},{7,6},{8,9},{9,8},{10,11... | collective-permute-start | bytes 589832 | tf_op jit(solution)/shard_map/ppermute | solution.py:269
  26.7 10.2 %collective-permute-start.9 = (bf16[3,2,128,128]{3,2,1,0:T(8,128)(2,1)S(1)}, bf16[3,2,128,128]{3,2,1,0:T(8,128)(2,1)S(1)}, u32[]{:S(2)}, u32[]{:S(2)}) collective-permute-start(bf16[3,2,128,128]{3,2,1,0:T(8,128)(2,1)S(1)} %get-tuple-element.72), channel_id=1, source_target_pairs={{0,3},{1,2},{2,1},{3,0},{4,7},{5,6},{6,5},{7,4},{8,11},{9,10},{10,... | collective-permute-start | bytes 589832 | tf_op jit(solution)/shard_map/ppermute | solution.py:269
  34.2 9.3 %collective-permute-start.11 = (bf16[3,2,128,128]{3,2,1,0:T(8,128)(2,1)S(1)}, bf16[3,2,128,128]{3,2,1,0:T(8,128)(2,1)S(1)}, u32[]{:S(2)}, u32[]{:S(2)}) collective-permute-start(bf16[3,2,128,128]{3,2,1,0:T(8,128)(2,1)S(1)} %get-tuple-element.86), channel_id=1, source_target_pairs={{0,2},{1,3},{2,0},{3,1},{4,6},{5,7},{6,4},{7,5},{8,10},{9,11},{10,... | collective-permute-start | bytes 589832 | tf_op jit(solution)/shard_map/ppermute | solution.py:269
  36.5 7.0 %collective-permute-start.10 = (bf16[3,2,128,128]{3,2,1,0:T(8,128)(2,1)S(1)}, bf16[3,2,128,128]{3,2,1,0:T(8,128)(2,1)S(1)}, u32[]{:S(2)}, u32[]{:S(2)}) collective-permute-start(bf16[3,2,128,128]{3,2,1,0:T(8,128)(2,1)S(1)} %get-tuple-element.85), channel_id=1, source_target_pairs={{0,1},{1,0},{2,3},{3,2},{4,5},{5,4},{6,7},{7,6},{8,9},{9,8},{10,11... | collective-permute-start | bytes 589832 | tf_op jit(solution)/shard_map/ppermute | solution.py:269
  38.8 6.6 %collective-permute-start.12 = (bf16[3,2,128,128]{3,2,1,0:T(8,128)(2,1)S(1)}, bf16[3,2,128,128]{3,2,1,0:T(8,128)(2,1)S(1)}, u32[]{:S(2)}, u32[]{:S(2)}) collective-permute-start(bf16[3,2,128,128]{3,2,1,0:T(8,128)(2,1)S(1)} %get-tuple-element.87), channel_id=1, source_target_pairs={{0,3},{1,2},{2,1},{3,0},{4,7},{5,6},{6,5},{7,4},{8,11},{9,10},{10,... | collective-permute-start | bytes 589832 | tf_op jit(solution)/shard_map/ppermute | solution.py:269
  45.6 9.5 %collective-permute-start.16 = (bf16[2,128,128]{2,1,0:T(8,128)(2,1)S(1)}, bf16[2,128,128]{2,1,0:T(8,128)(2,1)S(1)}, u32[]{:S(2)}, u32[]{:S(2)}) collective-permute-start(bf16[2,128,128]{2,1,0:T(8,128)(2,1)S(1)} %get-tuple-element.92), channel_id=1, source_target_pairs={{4,0},{5,1},{6,2},{7,3},{12,8},{13,9},{14,10},{15,11},{20,16},{21,... | collective-permute-start | bytes 196616 | tf_op jit(solution)/shard_map/ppermute | solution.py:269
  46.9 9.8 %collective-permute-start.17 = (bf16[2,128,128]{2,1,0:T(8,128)(2,1)S(1)}, bf16[2,128,128]{2,1,0:T(8,128)(2,1)S(1)}, u32[]{:S(2)}, u32[]{:S(2)}) collective-permute-start(bf16[2,128,128]{2,1,0:T(8,128)(2,1)S(1)} %get-tuple-element.93), channel_id=1, source_target_pairs={{4,1},{5,0},{6,3},{7,2},{12,9},{13,8},{14,11},{15,10},{20,17},{21,... | collective-permute-start | bytes 196616 | tf_op jit(solution)/shard_map/ppermute | solution.py:269
  49.0 12.4 %collective-permute-start.18 = (bf16[2,128,128]{2,1,0:T(8,128)(2,1)S(1)}, bf16[2,128,128]{2,1,0:T(8,128)(2,1)S(1)}, u32[]{:S(2)}, u32[]{:S(2)}) collective-permute-start(bf16[2,128,128]{2,1,0:T(8,128)(2,1)S(1)} %get-tuple-element.94), channel_id=1, source_target_pairs={{4,2},{5,3},{6,0},{7,1},{12,10},{13,11},{14,8},{15,9},{20,18},{21,... | collective-permute-start | bytes 196616 | tf_op jit(solution)/shard_map/ppermute | solution.py:269
  50.3 11.1 %collective-permute-start.19 = (bf16[2,128,128]{2,1,0:T(8,128)(2,1)S(1)}, bf16[2,128,128]{2,1,0:T(8,128)(2,1)S(1)}, u32[]{:S(2)}, u32[]{:S(2)}) collective-permute-start(bf16[2,128,128]{2,1,0:T(8,128)(2,1)S(1)} %get-tuple-element.95), channel_id=1, source_target_pairs={{4,3},{5,2},{6,1},{7,0},{12,11},{13,10},{14,9},{15,8},{20,19},{21,... | collective-permute-start | bytes 196616 | tf_op jit(solution)/shard_map/ppermute | solution.py:269
  52.0 9.5 %collective-permute-start.13 = (bf16[2,128,128]{2,1,0:T(8,128)(2,1)S(1)}, bf16[2,128,128]{2,1,0:T(8,128)(2,1)S(1)}, u32[]{:S(2)}, u32[]{:S(2)}) collective-permute-start(bf16[2,128,128]{2,1,0:T(8,128)(2,1)S(1)} %get-tuple-element.89), channel_id=1, source_target_pairs={{0,1},{1,0},{2,3},{3,2},{4,5},{5,4},{6,7},{7,6},{8,9},{9,8},{10,11... | collective-permute-start | bytes 196616 | tf_op jit(solution)/shard_map/ppermute | solution.py:269
  55.1 6.4 %collective-permute-start.14 = (bf16[2,128,128]{2,1,0:T(8,128)(2,1)S(1)}, bf16[2,128,128]{2,1,0:T(8,128)(2,1)S(1)}, u32[]{:S(2)}, u32[]{:S(2)}) collective-permute-start(bf16[2,128,128]{2,1,0:T(8,128)(2,1)S(1)} %get-tuple-element.90), channel_id=1, source_target_pairs={{0,2},{1,3},{2,0},{3,1},{4,6},{5,7},{6,4},{7,5},{8,10},{9,11},{10,... | collective-permute-start | bytes 196616 | tf_op jit(solution)/shard_map/ppermute | solution.py:269
  56.7 5.2 %collective-permute-start.15 = (bf16[2,128,128]{2,1,0:T(8,128)(2,1)S(1)}, bf16[2,128,128]{2,1,0:T(8,128)(2,1)S(1)}, u32[]{:S(2)}, u32[]{:S(2)}) collective-permute-start(bf16[2,128,128]{2,1,0:T(8,128)(2,1)S(1)} %get-tuple-element.91), channel_id=1, source_target_pairs={{0,3},{1,2},{2,1},{3,0},{4,7},{5,6},{6,5},{7,4},{8,11},{9,10},{10,... | collective-permute-start | bytes 196616 | tf_op jit(solution)/shard_map/ppermute | solution.py:269

commit v5 on v4

--- a/solution.py
+++ b/solution.py
@@ -97,7 +97,7 @@
 
 def attend_kernel(turn, rows, *refs):
     (pos_ref, hide_ref, mask_ref, q_ref, go_ref, far_ref, own_ref) = refs[:7]
-    weights_ref, grad_score_ref, far_grad_ref = refs[7:]
+    weights_ref, grad_score_ref, attended_ref, far_grad_ref = refs[7:]
     head = lax.rem(pos_ref[0], GROUP) ^ turn
     far_rows = FAR_SLOTS * rows
     mask = mask_ref[...]
@@ -121,8 +121,12 @@
     weights = weights * (1.0 / jnp.sum(weights, axis=0, keepdims=True))
     rounded = weights.astype(jnp.bfloat16)
     grad_prob = dot(vv, gm, LAST)
-    delta = jnp.sum(weights * grad_prob, axis=0, keepdims=True)
+    attended = dot(vv, rounded, FIRST).astype(jnp.bfloat16)
+    gm_heads = [gm[i * rows : (i + 1) * rows].T for i in range(HEADS_PER_KEY)]
+    gm_columns = jnp.concatenate(gm_heads, 1).astype(jnp.float32)
+    delta = jnp.sum(gm_columns * attended.astype(jnp.float32), axis=0, keepdims=True)
     grad_score = (weights * (grad_prob - delta)).astype(jnp.bfloat16)
+    attended_ref[...] = attended
     weights_ref[...] = rounded
     grad_score_ref[...] = grad_score
     grad_key = dot(grad_score[:far_rows], qm) * SCALING
@@ -134,20 +138,19 @@
 
 
 def output_kernel(turn, rows, *refs):
-    pos_ref, mask_ref, q_ref, go_ref, weights_ref, grad_score_ref, far_ref, own_ref = refs[:8]
-    attn_ref, gq_ref, own_grad_ref = refs[8:]
+    pos_ref, mask_ref, q_ref, go_ref, weights_ref, grad_score_ref = refs[:6]
+    attended_ref, far_ref, own_ref, attn_ref, gq_ref, own_grad_ref = refs[6:]
     head = lax.rem(pos_ref[0], GROUP) ^ turn
     own_rows = pl.ds(FAR_SLOTS * rows, rows)
     own_grad_ref[0] = dot(grad_score_ref[own_rows, :], stack_heads(q_ref, head)) * SCALING
     gm = stack_heads(go_ref, head, mask_ref[...])
     own_grad_ref[1] = dot(weights_ref[own_rows, :], gm)
-    kk, vv = stack_slots(far_ref, own_ref, 0), stack_slots(far_ref, own_ref, 1)
-    attended = dot(vv, weights_ref[...], FIRST)
+    kk = stack_slots(far_ref, own_ref, 0)
     grad_query = dot(kk, grad_score_ref[...], FIRST) * SCALING
     for i in range(HEADS_PER_KEY):
         s = slice(i * rows, (i + 1) * rows)
         cols = slice(i * HEAD_WIDTH, (i + 1) * HEAD_WIDTH)
-        attn_ref[:, cols] = attended[:, s].T.astype(jnp.bfloat16)
+        attn_ref[:, cols] = attended_ref[:, s].T
         gq_ref[:, cols] = grad_query[:, s].T.astype(jnp.bfloat16)
 
 
@@ -159,24 +162,29 @@
     return pl.pallas_call(
         functools.partial(attend_kernel, turn, rows),
         in_specs=[SMEM_SPEC] + [VMEM_SPEC] * 6,
-        out_specs=[VMEM_SPEC] * 3,
-        out_shape=[square, square, jax.ShapeDtypeStruct(far.shape, jnp.bfloat16)],
+        out_specs=[VMEM_SPEC] * 4,
+        out_shape=[
+            square,
+            square,
+            jax.ShapeDtypeStruct((HEAD_WIDTH, HEADS_PER_KEY * rows), jnp.bfloat16),
+            jax.ShapeDtypeStruct(far.shape, jnp.bfloat16),
+        ],
         cost_estimate=cost(8 * pairs * HEAD_WIDTH, 8 * pairs),
         compiler_params=pltpu.CompilerParams(vmem_limit_bytes=VMEM_LIMIT),
     )(pos, hide, mask, queries, grad_out, far, own)
 
 
-def output(turn, pos, mask, queries, grad_out, weights, grad_score, far, own):
+def output(turn, pos, mask, queries, grad_out, weights, grad_score, attended, far, own):
     rows = own.shape[1]
     block = jax.ShapeDtypeStruct((rows, HEADS_PER_KEY * HEAD_WIDTH), jnp.bfloat16)
     return pl.pallas_call(
         functools.partial(output_kernel, turn, rows),
-        in_specs=[SMEM_SPEC] + [VMEM_SPEC] * 7,
+        in_specs=[SMEM_SPEC] + [VMEM_SPEC] * 8,
         out_specs=[VMEM_SPEC] * 3,
         out_shape=[block, block, jax.ShapeDtypeStruct(own.shape, jnp.float32)],
         cost_estimate=cost(5 * weights.size * HEAD_WIDTH, 4 * weights.size),
         compiler_params=pltpu.CompilerParams(vmem_limit_bytes=VMEM_LIMIT),
-    )(pos, mask, queries, grad_out, weights, grad_score, far, own)
+    )(pos, mask, queries, grad_out, weights, grad_score, attended, far, own)
 
 
 def store_kernel(pos_ref, *refs):
@@ -301,11 +309,11 @@
 
     blocks, far_grads, own_grads = [], [], []
     for t in range(GROUP):
-        weights, grad_score, far_grad = attend(
+        weights, grad_score, transposed, far_grad = attend(
             t, pos, hide, mask, queries, grad_out, far[t], packed[t]
         )
         attended, grad_query, own_grad = output(
-            t, pos, mask, queries, grad_out, weights, grad_score, far[t], packed[t]
+            t, pos, mask, queries, grad_out, weights, grad_score, transposed, far[t], packed[t]
         )
         blocks += [attended, grad_query]
         far_grads.append(far_grad)

time: 63.1 us -> 63.1 us (level)
  waiting for transfers between devices: 12.2 us -> 11.1 us
  starting transfers between devices: 34.1 us -> 35 us
    ppermute x20, waiting for transfers between devices: 12.2 us -> 11.1 us  [send(): return lax.ppermute(x, 'ctx', pairs)]
    ppermute x20, starting transfers between devices: 34.1 us -> 35 us  [send(): return lax.ppermute(x, 'ctx', pairs)]
    pallas_call x4, Pallas kernels: 7.48 us -> 8.32 us  [attend(): pl.pallas_call(functools.partial(attend_kernel, turn, rows), in_specs=[SM...]
  transfers between devices with their start and end apart: 20 -> 20, of which waited for: 7 -> 6; matrix products, arithmetic and copies ran while one was open for 0% -> 0% of each run, Pallas kernels for 21% -> 22%
where the time goes in v5:
time: 63.1 us; the launch traced here: 62.8 us
  starting transfers between devices  35 us (55%)
  Pallas kernels  15.6 us (25%)
  waiting for transfers between devices  11.1 us (18%)
  between operations  0.96 us (2%)
    ppermute x20, starting transfers between devices, send(): return lax.ppermute(x, 'ctx', pairs)  35 us
    ppermute x20, waiting for transfers between devices, send(): return lax.ppermute(x, 'ctx', pairs)  11.1 us
    pallas_call x4, Pallas kernels, attend(): pl.pallas_call(functools.partial(attend_kernel, turn, rows), in_specs=[SM...  8.32 us
    pallas_call x4, Pallas kernels, output(): pl.pallas_call(functools.partial(output_kernel, turn, rows), in_specs=[SM...  2.49 us
    pallas_call x1, Pallas kernels, on_device(): small_call(store_kernel, [SMEM_SPEC] + [VMEM_SPEC] * (2 * GROUP), [HBM_SP...  1.38 us
  transfers between devices with their start and end apart: 20, of which 6 were waited for; matrix products, arithmetic and copies ran while one was open for 0% of the time, Pallas kernels for 22%

profile of v5, /device:TPU:0, one launch (start us, length us, event | category | flops | bytes accessed | tf_op | source)
XLA Modules:
  0.0 62.8 jit_solution(2008328847689024554)
XLA Ops:
  0.6 1.0 %shard_map.94 = (bf16[2,128,128]{2,1,0:T(8,128)(2,1)S(1)}, bf16[2,128,128]{2,1,0:T(8,128)(2,1)S(1)}, bf16[2,128,128]{2,1,0:T(8,128)(2,1)S(1)}, bf16[2,128,128]{2,1,0:T(8,128)(2,1)S(1)}) custom-call(s32[1]{0:T(128)} %bitcast.pos_ref.refs_0_, bf16[128,512]{1,0:T(8,128)(2,1)} %k_ref.1, bf16[128,512]{1,0:T(8,128)(2,1)} %v_ref.1), custom_call_target="tpu_custom_call" | custom-call | flops 1048576 | bytes 524288 | tf_op jit(solution)/shard_map/pallas_call | solution.py:289
  1.6 6.0 %collective-permute-start.3 = (bf16[2,128,128]{2,1,0:T(8,128)(2,1)S(1)}, bf16[2,128,128]{2,1,0:T(8,128)(2,1)S(1)}, u32[]{:S(2)}, u32[]{:S(2)}) collective-permute-start(bf16[2,128,128]{2,1,0:T(8,128)(2,1)S(1)} %get-tuple-element.57.refs_0_.refs_6_.refs_8_), channel_id=1, source_target_pairs={{0,4},{1,5},{2,6},{3,7},{8,12},{9,13},{10,14},{11,15},{16,20},{17,... | collective-permute-start | bytes 196616 | tf_op jit(solution)/shard_map/ppermute | solution.py:277
  7.6 2.2 %collective-permute-start.4 = (bf16[2,128,128]{2,1,0:T(8,128)(2,1)S(1)}, bf16[2,128,128]{2,1,0:T(8,128)(2,1)S(1)}, u32[]{:S(2)}, u32[]{:S(2)}) collective-permute-start(bf16[2,128,128]{2,1,0:T(8,128)(2,1)S(1)} %get-tuple-element.58.refs_6_.refs_8_), channel_id=1, source_target_pairs={{0,5},{1,4},{2,7},{3,6},{8,13},{9,12},{10,15},{11,14},{16,21},{17,... | collective-permute-start | bytes 196616 | tf_op jit(solution)/shard_map/ppermute | solution.py:277
  10.5 2.3 %collective-permute-start.5 = (bf16[2,128,128]{2,1,0:T(8,128)(2,1)S(1)}, bf16[2,128,128]{2,1,0:T(8,128)(2,1)S(1)}, u32[]{:S(2)}, u32[]{:S(2)}) collective-permute-start(bf16[2,128,128]{2,1,0:T(8,128)(2,1)S(1)} %get-tuple-element.59.refs_6_.refs_8_), channel_id=1, source_target_pairs={{0,6},{1,7},{2,4},{3,5},{8,14},{9,15},{10,12},{11,13},{16,22},{17,... | collective-permute-start | bytes 196616 | tf_op jit(solution)/shard_map/ppermute | solution.py:277
  13.4 6.7 %collective-permute-start.6 = (bf16[2,128,128]{2,1,0:T(8,128)(2,1)S(1)}, bf16[2,128,128]{2,1,0:T(8,128)(2,1)S(1)}, u32[]{:S(2)}, u32[]{:S(2)}) collective-permute-start(bf16[2,128,128]{2,1,0:T(8,128)(2,1)S(1)} %get-tuple-element.60.refs_6_.refs_8_), channel_id=1, source_target_pairs={{0,7},{1,6},{2,5},{3,4},{8,15},{9,14},{10,13},{11,12},{16,23},{17,... | collective-permute-start | bytes 196616 | tf_op jit(solution)/shard_map/ppermute | solution.py:277
  21.0 1.0 %collective-permute-done.6.refs_7_ = bf16[2,128,128]{2,1,0:T(8,128)(2,1)S(1)} collective-permute-done((bf16[2,128,128]{2,1,0:T(8,128)(2,1)S(1)}, bf16[2,128,128]{2,1,0:T(8,128)(2,1)S(1)}, u32[]{:S(2)}, u32[]{:S(2)}) %collective-permute-start.6) | collective-permute-done | bytes 65568 | tf_op jit(solution)/shard_map/ppermute | solution.py:277
  22.0 4.1 %collective-permute-done.2.refs_3_ = bf16[2,128,128]{2,1,0:T(8,128)(2,1)S(1)} collective-permute-done((bf16[2,128,128]{2,1,0:T(8,128)(2,1)S(1)}, bf16[2,128,128]{2,1,0:T(8,128)(2,1)S(1)}, u32[]{:S(2)}, u32[]{:S(2)}) %collective-permute-start.2) | collective-permute-done | bytes 65568 | tf_op jit(solution)/shard_map/ppermute | solution.py:277
  26.7 3.0 %collective-permute-start.9 = (bf16[3,2,128,128]{3,2,1,0:T(8,128)(2,1)S(1)}, bf16[3,2,128,128]{3,2,1,0:T(8,128)(2,1)S(1)}, u32[]{:S(2)}, u32[]{:S(2)}) collective-permute-start(bf16[3,2,128,128]{3,2,1,0:T(8,128)(2,1)S(1)} %get-tuple-element.79), channel_id=1, source_target_pairs={{0,3},{1,2},{2,1},{3,0},{4,7},{5,6},{6,5},{7,4},{8,11},{9,10},{10,... | collective-permute-start | bytes 589832 | tf_op jit(solution)/shard_map/ppermute | solution.py:277
  29.8 2.2 %collective-permute-done.8.refs_5_.refs_7_ = bf16[3,2,128,128]{3,2,1,0:T(8,128)(2,1)S(1)} collective-permute-done((bf16[3,2,128,128]{3,2,1,0:T(8,128)(2,1)S(1)}, bf16[3,2,128,128]{3,2,1,0:T(8,128)(2,1)S(1)}, u32[]{:S(2)}, u32[]{:S(2)}) %collective-permute-start.8) | collective-permute-done | bytes 196640 | tf_op jit(solution)/shard_map/ppermute | solution.py:277
  32.1 2.1 %shard_map.100 = (bf16[512,1024]{1,0:T(8,128)(2,1)S(1)}, bf16[512,1024]{1,0:T(8,128)(2,1)S(1)}, bf16[128,1024]{1,0:T(8,128)(2,1)S(1)}, bf16[3,2,128,128]{3,2,1,0:T(8,128)(2,1)S(1)}) custom-call(s32[1]{0:T(128)} %bitcast.pos_ref.refs_0_, f32[8,128]{1,0:T(8,128)S(1)} %get-tuple-element.55.refs_1_, bf16[128,128]{1,0:T(8,128)(2,1)S(1)} %broadcast_in_dim.2.refs_2_.refs_1_, ...), custom_call_target="tpu_custom_call" | custom-call | flops 536870912 | bytes 4194304 | tf_op jit(solution)/shard_map/pallas_call | solution.py:162
  34.6 2.1 %shard_map.98 = (bf16[512,1024]{1,0:T(8,128)(2,1)S(1)}, bf16[512,1024]{1,0:T(8,128)(2,1)S(1)}, bf16[128,1024]{1,0:T(8,128)(2,1)S(1)}, bf16[3,2,128,128]{3,2,1,0:T(8,128)(2,1)S(1)}) custom-call(s32[1]{0:T(128)} %bitcast.pos_ref.refs_0_, f32[8,128]{1,0:T(8,128)S(1)} %get-tuple-element.55.refs_1_, bf16[128,128]{1,0:T(8,128)(2,1)S(1)} %broadcast_in_dim.2.refs_2_.refs_1_, ...), custom_call_target="tpu_custom_call" | custom-call | flops 536870912 | bytes 4194304 | tf_op jit(solution)/shard_map/pallas_call | solution.py:162
  37.4 2.1 %shard_map.102 = (bf16[512,1024]{1,0:T(8,128)(2,1)S(1)}, bf16[512,1024]{1,0:T(8,128)(2,1)S(1)}, bf16[128,1024]{1,0:T(8,128)(2,1)S(1)}, bf16[3,2,128,128]{3,2,1,0:T(8,128)(2,1)S(1)}) custom-call(s32[1]{0:T(128)} %bitcast.pos_ref.refs_0_, f32[8,128]{1,0:T(8,128)S(1)} %get-tuple-element.55.refs_1_, bf16[128,128]{1,0:T(8,128)(2,1)S(1)} %broadcast_in_dim.2.refs_2_.refs_1_, ...), custom_call_target="tpu_custom_call" | custom-call | flops 536870912 | bytes 4194304 | tf_op jit(solution)/shard_map/pallas_call | solution.py:162
  39.4 2.6 %collective-permute-start.12 = (bf16[3,2,128,128]{3,2,1,0:T(8,128)(2,1)S(1)}, bf16[3,2,128,128]{3,2,1,0:T(8,128)(2,1)S(1)}, u32[]{:S(2)}, u32[]{:S(2)}) collective-permute-start(bf16[3,2,128,128]{3,2,1,0:T(8,128)(2,1)S(1)} %get-tuple-element.95), channel_id=1, source_target_pairs={{0,3},{1,2},{2,1},{3,0},{4,7},{5,6},{6,5},{7,4},{8,11},{9,10},{10,... | collective-permute-start | bytes 589832 | tf_op jit(solution)/shard_map/ppermute | solution.py:277
  42.0 2.1 %shard_map.96 = (bf16[512,1024]{1,0:T(8,128)(2,1)S(1)}, bf16[512,1024]{1,0:T(8,128)(2,1)S(1)}, bf16[128,1024]{1,0:T(8,128)(2,1)S(1)}, bf16[3,2,128,128]{3,2,1,0:T(8,128)(2,1)S(1)}) custom-call(s32[1]{0:T(128)} %bitcast.pos_ref.refs_0_, f32[8,128]{1,0:T(8,128)S(1)} %get-tuple-element.55.refs_1_, bf16[128,128]{1,0:T(8,128)(2,1)S(1)} %broadcast_in_dim.2.refs_2_.refs_1_, ...), custom_call_target="tpu_custom_call" | custom-call | flops 536870912 | bytes 4194304 | tf_op jit(solution)/shard_map/pallas_call | solution.py:162
  44.6 1.5 %collective-permute-done.12.last_ref = bf16[3,2,128,128]{3,2,1,0:T(8,128)(2,1)S(1)} collective-permute-done((bf16[3,2,128,128]{3,2,1,0:T(8,128)(2,1)S(1)}, bf16[3,2,128,128]{3,2,1,0:T(8,128)(2,1)S(1)}, u32[]{:S(2)}, u32[]{:S(2)}) %collective-permute-start.12) | collective-permute-done | bytes 196640 | tf_op jit(solution)/shard_map/ppermute | solution.py:277
  46.3 1.3 %collective-permute-start.16 = (bf16[2,128,128]{2,1,0:T(8,128)(2,1)S(1)}, bf16[2,128,128]{2,1,0:T(8,128)(2,1)S(1)}, u32[]{:S(2)}, u32[]{:S(2)}) collective-permute-start(bf16[2,128,128]{2,1,0:T(8,128)(2,1)S(1)} %get-tuple-element.100), channel_id=1, source_target_pairs={{4,0},{5,1},{6,2},{7,3},{12,8},{13,9},{14,10},{15,11},{20,16},{21,... | collective-permute-start | bytes 196616 | tf_op jit(solution)/shard_map/ppermute | solution.py:277
  47.6 1.3 %collective-permute-start.17 = (bf16[2,128,128]{2,1,0:T(8,128)(2,1)S(1)}, bf16[2,128,128]{2,1,0:T(8,128)(2,1)S(1)}, u32[]{:S(2)}, u32[]{:S(2)}) collective-permute-start(bf16[2,128,128]{2,1,0:T(8,128)(2,1)S(1)} %get-tuple-element.101), channel_id=1, source_target_pairs={{4,1},{5,0},{6,3},{7,2},{12,9},{13,8},{14,11},{15,10},{20,17},{21,... | collective-permute-start | bytes 196616 | tf_op jit(solution)/shard_map/ppermute | solution.py:277
  49.5 1.3 %collective-permute-start.18 = (bf16[2,128,128]{2,1,0:T(8,128)(2,1)S(1)}, bf16[2,128,128]{2,1,0:T(8,128)(2,1)S(1)}, u32[]{:S(2)}, u32[]{:S(2)}) collective-permute-start(bf16[2,128,128]{2,1,0:T(8,128)(2,1)S(1)} %get-tuple-element.102), channel_id=1, source_target_pairs={{4,2},{5,3},{6,0},{7,1},{12,10},{13,11},{14,8},{15,9},{20,18},{21,... | collective-permute-start | bytes 196616 | tf_op jit(solution)/shard_map/ppermute | solution.py:277
  50.8 1.3 %collective-permute-start.19 = (bf16[2,128,128]{2,1,0:T(8,128)(2,1)S(1)}, bf16[2,128,128]{2,1,0:T(8,128)(2,1)S(1)}, u32[]{:S(2)}, u32[]{:S(2)}) collective-permute-start(bf16[2,128,128]{2,1,0:T(8,128)(2,1)S(1)} %get-tuple-element.103), channel_id=1, source_target_pairs={{4,3},{5,2},{6,1},{7,0},{12,11},{13,10},{14,9},{15,8},{20,19},{21,... | collective-permute-start | bytes 196616 | tf_op jit(solution)/shard_map/ppermute | solution.py:277
  52.3 1.5 %collective-permute-start.13 = (bf16[2,128,128]{2,1,0:T(8,128)(2,1)S(1)}, bf16[2,128,128]{2,1,0:T(8,128)(2,1)S(1)}, u32[]{:S(2)}, u32[]{:S(2)}) collective-permute-start(bf16[2,128,128]{2,1,0:T(8,128)(2,1)S(1)} %get-tuple-element.97), channel_id=1, source_target_pairs={{0,1},{1,0},{2,3},{3,2},{4,5},{5,4},{6,7},{7,6},{8,9},{9,8},{10,11... | collective-permute-start | bytes 196616 | tf_op jit(solution)/shard_map/ppermute | solution.py:277
  53.8 1.3 %collective-permute-done.16.refs_8_ = bf16[2,128,128]{2,1,0:T(8,128)(2,1)S(1)} collective-permute-done((bf16[2,128,128]{2,1,0:T(8,128)(2,1)S(1)}, bf16[2,128,128]{2,1,0:T(8,128)(2,1)S(1)}, u32[]{:S(2)}, u32[]{:S(2)}) %collective-permute-start.16) | collective-permute-done | bytes 65568 | tf_op jit(solution)/shard_map/ppermute | solution.py:277
  55.5 1.1 %collective-permute-done.17.refs_9_ = bf16[2,128,128]{2,1,0:T(8,128)(2,1)S(1)} collective-permute-done((bf16[2,128,128]{2,1,0:T(8,128)(2,1)S(1)}, bf16[2,128,128]{2,1,0:T(8,128)(2,1)S(1)}, u32[]{:S(2)}, u32[]{:S(2)}) %collective-permute-start.17) | collective-permute-done | bytes 65568 | tf_op jit(solution)/shard_map/ppermute | solution.py:277
  56.5 2.1 %collective-permute-start.15 = (bf16[2,128,128]{2,1,0:T(8,128)(2,1)S(1)}, bf16[2,128,128]{2,1,0:T(8,128)(2,1)S(1)}, u32[]{:S(2)}, u32[]{:S(2)}) collective-permute-start(bf16[2,128,128]{2,1,0:T(8,128)(2,1)S(1)} %get-tuple-element.99), channel_id=1, source_target_pairs={{0,3},{1,2},{2,1},{3,0},{4,7},{5,6},{6,5},{7,4},{8,11},{9,10},{10,... | collective-permute-start | bytes 196616 | tf_op jit(solution)/shard_map/ppermute | solution.py:277
  60.5 1.4 %shard_map.104 = (bf16[128,4096]{1,0:T(8,128)(2,1)}, bf16[128,4096]{1,0:T(8,128)(2,1)}) custom-call(s32[1]{0:T(128)} %bitcast.pos_ref.refs_0_, bf16[128,1024]{1,0:T(8,128)(2,1)S(1)} %get-tuple-element.65.refs_0_, bf16[128,1024]{1,0:T(8,128)(2,1)S(1)} %get-tuple-element.66.refs_1_, bf16[128,1024]{1,0:T(8,128)(2,1)S(1)} %get-tuple-element.71.refs_2_, ...), custom_call_target="tpu_custom_call" | custom-call | flops 4194304 | bytes 2097152 | tf_op jit(solution)/shard_map/pallas_call | solution.py:323
  (43 shorter events, 8.5 us)
Async XLA Ops:
  1.6 11.8 %collective-permute-start.3 = (bf16[2,128,128]{2,1,0:T(8,128)(2,1)S(1)}, bf16[2,128,128]{2,1,0:T(8,128)(2,1)S(1)}, u32[]{:S(2)}, u32[]{:S(2)}) collective-permute-start(bf16[2,128,128]{2,1,0:T(8,128)(2,1)S(1)} %get-tuple-element.57.refs_0_.refs_6_.refs_8_), channel_id=1, source_target_pairs={{0,4},{1,5},{2,6},{3,7},{8,12},{9,13},{10,14},{11,15},{16,20},{17,... | collective-permute-start | bytes 196616 | tf_op jit(solution)/shard_map/ppermute | solution.py:277
  7.6 12.7 %copy-start.2 = (s32[8,4]{0,1:T(4,128)S(1)}, s32[8,4]{0,1:T(4,128)}, u32[]{:S(2)}) copy-start(s32[8,4]{0,1:T(4,128)} %param.10) | copy-start | bytes 388
  7.6 12.6 %collective-permute-start.4 = (bf16[2,128,128]{2,1,0:T(8,128)(2,1)S(1)}, bf16[2,128,128]{2,1,0:T(8,128)(2,1)S(1)}, u32[]{:S(2)}, u32[]{:S(2)}) collective-permute-start(bf16[2,128,128]{2,1,0:T(8,128)(2,1)S(1)} %get-tuple-element.58.refs_6_.refs_8_), channel_id=1, source_target_pairs={{0,5},{1,4},{2,7},{3,6},{8,13},{9,12},{10,15},{11,14},{16,21},{17,... | collective-permute-start | bytes 196616 | tf_op jit(solution)/shard_map/ppermute | solution.py:277
  9.8 11.2 %collective-permute-start = (bf16[2,128,128]{2,1,0:T(8,128)(2,1)S(1)}, bf16[2,128,128]{2,1,0:T(8,128)(2,1)S(1)}, u32[]{:S(2)}, u32[]{:S(2)}) collective-permute-start(bf16[2,128,128]{2,1,0:T(8,128)(2,1)S(1)} %get-tuple-element.58.refs_6_.refs_8_), channel_id=1, source_target_pairs={{0,1},{1,0},{2,3},{3,2},{4,5},{5,4},{6,7},{7,6},{8,9},{9,8},{10,11... | collective-permute-start | bytes 196616 | tf_op jit(solution)/shard_map/ppermute | solution.py:277
  10.5 10.5 %collective-permute-start.5 = (bf16[2,128,128]{2,1,0:T(8,128)(2,1)S(1)}, bf16[2,128,128]{2,1,0:T(8,128)(2,1)S(1)}, u32[]{:S(2)}, u32[]{:S(2)}) collective-permute-start(bf16[2,128,128]{2,1,0:T(8,128)(2,1)S(1)} %get-tuple-element.59.refs_6_.refs_8_), channel_id=1, source_target_pairs={{0,6},{1,7},{2,4},{3,5},{8,14},{9,15},{10,12},{11,13},{16,22},{17,... | collective-permute-start | bytes 196616 | tf_op jit(solution)/shard_map/ppermute | solution.py:277
  12.8 8.3 %collective-permute-start.1 = (bf16[2,128,128]{2,1,0:T(8,128)(2,1)S(1)}, bf16[2,128,128]{2,1,0:T(8,128)(2,1)S(1)}, u32[]{:S(2)}, u32[]{:S(2)}) collective-permute-start(bf16[2,128,128]{2,1,0:T(8,128)(2,1)S(1)} %get-tuple-element.59.refs_6_.refs_8_), channel_id=1, source_target_pairs={{0,2},{1,3},{2,0},{3,1},{4,6},{5,7},{6,4},{7,5},{8,10},{9,11},{10,... | collective-permute-start | bytes 196616 | tf_op jit(solution)/shard_map/ppermute | solution.py:277
  13.4 8.6 %collective-permute-start.6 = (bf16[2,128,128]{2,1,0:T(8,128)(2,1)S(1)}, bf16[2,128,128]{2,1,0:T(8,128)(2,1)S(1)}, u32[]{:S(2)}, u32[]{:S(2)}) collective-permute-start(bf16[2,128,128]{2,1,0:T(8,128)(2,1)S(1)} %get-tuple-element.60.refs_6_.refs_8_), channel_id=1, source_target_pairs={{0,7},{1,6},{2,5},{3,4},{8,15},{9,14},{10,13},{11,12},{16,23},{17,... | collective-permute-start | bytes 196616 | tf_op jit(solution)/shard_map/ppermute | solution.py:277
  20.2 5.9 %collective-permute-start.2 = (bf16[2,128,128]{2,1,0:T(8,128)(2,1)S(1)}, bf16[2,128,128]{2,1,0:T(8,128)(2,1)S(1)}, u32[]{:S(2)}, u32[]{:S(2)}) collective-permute-start(bf16[2,128,128]{2,1,0:T(8,128)(2,1)S(1)} %get-tuple-element.60.refs_6_.refs_8_), channel_id=1, source_target_pairs={{0,3},{1,2},{2,1},{3,0},{4,7},{5,6},{6,5},{7,4},{8,11},{9,10},{10,... | collective-permute-start | bytes 196616 | tf_op jit(solution)/shard_map/ppermute | solution.py:277
  26.1 6.0 %copy-start = (bf16[128,4096]{1,0:T(8,128)(2,1)S(1)}, bf16[128,4096]{1,0:T(8,128)(2,1)}, u32[]{:S(2)}) copy-start(bf16[128,4096]{1,0:T(8,128)(2,1)} %refs_2_.7) | copy-start | bytes 3145732
  26.1 6.0 %copy-start.1 = (bf16[128,4096]{1,0:T(8,128)(2,1)S(1)}, bf16[128,4096]{1,0:T(8,128)(2,1)}, u32[]{:S(2)}) copy-start(bf16[128,4096]{1,0:T(8,128)(2,1)} %refs_3_.15) | copy-start | bytes 3145732
  26.2 5.8 %collective-permute-start.8 = (bf16[3,2,128,128]{3,2,1,0:T(8,128)(2,1)S(1)}, bf16[3,2,128,128]{3,2,1,0:T(8,128)(2,1)S(1)}, u32[]{:S(2)}, u32[]{:S(2)}) collective-permute-start(bf16[3,2,128,128]{3,2,1,0:T(8,128)(2,1)S(1)} %get-tuple-element.73), channel_id=1, source_target_pairs={{0,2},{1,3},{2,0},{3,1},{4,6},{5,7},{6,4},{7,5},{8,10},{9,11},{10,... | collective-permute-start | bytes 589832 | tf_op jit(solution)/shard_map/ppermute | solution.py:277
  26.3 3.5 %copy-start.3 = (s32[128]{0:T(128)S(1)}, s32[128]{0:T(128)}, u32[]{:S(2)}) copy-start(s32[128]{0:T(128)} %param.11) | copy-start | bytes 1540
  26.3 8.3 %collective-permute-start.7 = (bf16[3,2,128,128]{3,2,1,0:T(8,128)(2,1)S(1)}, bf16[3,2,128,128]{3,2,1,0:T(8,128)(2,1)S(1)}, u32[]{:S(2)}, u32[]{:S(2)}) collective-permute-start(bf16[3,2,128,128]{3,2,1,0:T(8,128)(2,1)S(1)} %get-tuple-element.67), channel_id=1, source_target_pairs={{0,1},{1,0},{2,3},{3,2},{4,5},{5,4},{6,7},{7,6},{8,9},{9,8},{10,11... | collective-permute-start | bytes 589832 | tf_op jit(solution)/shard_map/ppermute | solution.py:277
  26.7 10.6 %collective-permute-start.9 = (bf16[3,2,128,128]{3,2,1,0:T(8,128)(2,1)S(1)}, bf16[3,2,128,128]{3,2,1,0:T(8,128)(2,1)S(1)}, u32[]{:S(2)}, u32[]{:S(2)}) collective-permute-start(bf16[3,2,128,128]{3,2,1,0:T(8,128)(2,1)S(1)} %get-tuple-element.79), channel_id=1, source_target_pairs={{0,3},{1,2},{2,1},{3,0},{4,7},{5,6},{6,5},{7,4},{8,11},{9,10},{10,... | collective-permute-start | bytes 589832 | tf_op jit(solution)/shard_map/ppermute | solution.py:277
  34.1 10.0 %collective-permute-start.11 = (bf16[3,2,128,128]{3,2,1,0:T(8,128)(2,1)S(1)}, bf16[3,2,128,128]{3,2,1,0:T(8,128)(2,1)S(1)}, u32[]{:S(2)}, u32[]{:S(2)}) collective-permute-start(bf16[3,2,128,128]{3,2,1,0:T(8,128)(2,1)S(1)} %get-tuple-element.94), channel_id=1, source_target_pairs={{0,2},{1,3},{2,0},{3,1},{4,6},{5,7},{6,4},{7,5},{8,10},{9,11},{10,... | collective-permute-start | bytes 589832 | tf_op jit(solution)/shard_map/ppermute | solution.py:277
  36.7 7.4 %collective-permute-start.10 = (bf16[3,2,128,128]{3,2,1,0:T(8,128)(2,1)S(1)}, bf16[3,2,128,128]{3,2,1,0:T(8,128)(2,1)S(1)}, u32[]{:S(2)}, u32[]{:S(2)}) collective-permute-start(bf16[3,2,128,128]{3,2,1,0:T(8,128)(2,1)S(1)} %get-tuple-element.93), channel_id=1, source_target_pairs={{0,1},{1,0},{2,3},{3,2},{4,5},{5,4},{6,7},{7,6},{8,9},{9,8},{10,11... | collective-permute-start | bytes 589832 | tf_op jit(solution)/shard_map/ppermute | solution.py:277
  39.4 6.6 %collective-permute-start.12 = (bf16[3,2,128,128]{3,2,1,0:T(8,128)(2,1)S(1)}, bf16[3,2,128,128]{3,2,1,0:T(8,128)(2,1)S(1)}, u32[]{:S(2)}, u32[]{:S(2)}) collective-permute-start(bf16[3,2,128,128]{3,2,1,0:T(8,128)(2,1)S(1)} %get-tuple-element.95), channel_id=1, source_target_pairs={{0,3},{1,2},{2,1},{3,0},{4,7},{5,6},{6,5},{7,4},{8,11},{9,10},{10,... | collective-permute-start | bytes 589832 | tf_op jit(solution)/shard_map/ppermute | solution.py:277
  46.3 8.8 %collective-permute-start.16 = (bf16[2,128,128]{2,1,0:T(8,128)(2,1)S(1)}, bf16[2,128,128]{2,1,0:T(8,128)(2,1)S(1)}, u32[]{:S(2)}, u32[]{:S(2)}) collective-permute-start(bf16[2,128,128]{2,1,0:T(8,128)(2,1)S(1)} %get-tuple-element.100), channel_id=1, source_target_pairs={{4,0},{5,1},{6,2},{7,3},{12,8},{13,9},{14,10},{15,11},{20,16},{21,... | collective-permute-start | bytes 196616 | tf_op jit(solution)/shard_map/ppermute | solution.py:277
  47.6 8.9 %collective-permute-start.17 = (bf16[2,128,128]{2,1,0:T(8,128)(2,1)S(1)}, bf16[2,128,128]{2,1,0:T(8,128)(2,1)S(1)}, u32[]{:S(2)}, u32[]{:S(2)}) collective-permute-start(bf16[2,128,128]{2,1,0:T(8,128)(2,1)S(1)} %get-tuple-element.101), channel_id=1, source_target_pairs={{4,1},{5,0},{6,3},{7,2},{12,9},{13,8},{14,11},{15,10},{20,17},{21,... | collective-permute-start | bytes 196616 | tf_op jit(solution)/shard_map/ppermute | solution.py:277
  49.5 12.4 %collective-permute-start.18 = (bf16[2,128,128]{2,1,0:T(8,128)(2,1)S(1)}, bf16[2,128,128]{2,1,0:T(8,128)(2,1)S(1)}, u32[]{:S(2)}, u32[]{:S(2)}) collective-permute-start(bf16[2,128,128]{2,1,0:T(8,128)(2,1)S(1)} %get-tuple-element.102), channel_id=1, source_target_pairs={{4,2},{5,3},{6,0},{7,1},{12,10},{13,11},{14,8},{15,9},{20,18},{21,... | collective-permute-start | bytes 196616 | tf_op jit(solution)/shard_map/ppermute | solution.py:277
  50.8 11.1 %collective-permute-start.19 = (bf16[2,128,128]{2,1,0:T(8,128)(2,1)S(1)}, bf16[2,128,128]{2,1,0:T(8,128)(2,1)S(1)}, u32[]{:S(2)}, u32[]{:S(2)}) collective-permute-start(bf16[2,128,128]{2,1,0:T(8,128)(2,1)S(1)} %get-tuple-element.103), channel_id=1, source_target_pairs={{4,3},{5,2},{6,1},{7,0},{12,11},{13,10},{14,9},{15,8},{20,19},{21,... | collective-permute-start | bytes 196616 | tf_op jit(solution)/shard_map/ppermute | solution.py:277
  52.3 9.6 %collective-permute-start.13 = (bf16[2,128,128]{2,1,0:T(8,128)(2,1)S(1)}, bf16[2,128,128]{2,1,0:T(8,128)(2,1)S(1)}, u32[]{:S(2)}, u32[]{:S(2)}) collective-permute-start(bf16[2,128,128]{2,1,0:T(8,128)(2,1)S(1)} %get-tuple-element.97), channel_id=1, source_target_pairs={{0,1},{1,0},{2,3},{3,2},{4,5},{5,4},{6,7},{7,6},{8,9},{9,8},{10,11... | collective-permute-start | bytes 196616 | tf_op jit(solution)/shard_map/ppermute | solution.py:277
  55.1 6.9 %collective-permute-start.14 = (bf16[2,128,128]{2,1,0:T(8,128)(2,1)S(1)}, bf16[2,128,128]{2,1,0:T(8,128)(2,1)S(1)}, u32[]{:S(2)}, u32[]{:S(2)}) collective-permute-start(bf16[2,128,128]{2,1,0:T(8,128)(2,1)S(1)} %get-tuple-element.98), channel_id=1, source_target_pairs={{0,2},{1,3},{2,0},{3,1},{4,6},{5,7},{6,4},{7,5},{8,10},{9,11},{10,... | collective-permute-start | bytes 196616 | tf_op jit(solution)/shard_map/ppermute | solution.py:277
  56.5 5.4 %collective-permute-start.15 = (bf16[2,128,128]{2,1,0:T(8,128)(2,1)S(1)}, bf16[2,128,128]{2,1,0:T(8,128)(2,1)S(1)}, u32[]{:S(2)}, u32[]{:S(2)}) collective-permute-start(bf16[2,128,128]{2,1,0:T(8,128)(2,1)S(1)} %get-tuple-element.99), channel_id=1, source_target_pairs={{0,3},{1,2},{2,1},{3,0},{4,7},{5,6},{6,5},{7,4},{8,11},{9,10},{10,... | collective-permute-start | bytes 196616 | tf_op jit(solution)/shard_map/ppermute | solution.py:277
